TPU v7x, 256 devices: a whole 4x4x8 slice. The times are simulated.
256 devices in a mesh: gx: 8 (over z), gy: 4 (over y), gz: 8 (over x, core).
Axes of the slice: x: 4, y: 4, z: 8, core: 2. Of those that a mesh axis runs over, the one named last changes fastest.
Arguments:
- chi_field: float32 [64, 128, 1024], P('gx', 'gy', 'gz'), may hold values from 0.5 to 2.5, as said below
- metric: float32 [6, 64, 128, 1024], P(None, 'gx', 'gy', 'gz'), may hold values from -0.3 to 1.5, as said below
- curvature: float32 [6, 64, 128, 1024], P(None, 'gx', 'gy', 'gz'), may hold values from -1.6 to 1.6
- trace_curvature: float32 [64, 128, 1024], P('gx', 'gy', 'gz'), may hold values from -3 to 3
- gamma_field: float32 [3, 64, 128, 1024], P(None, 'gx', 'gy', 'gz'), may hold values from -1.6 to 1.6
Outputs:
- hamiltonian: float32 [64, 128, 1024], P('gx', 'gy', 'gz')
- momentum: float32 [3, 64, 128, 1024], P(None, 'gx', 'gy', 'gz')
- constraint_norms: float32 [2], replicated
Inputs may be any that keep to these rules, and one draw needn't show every extreme that they name: `chi_field`: positive. `metric`: at every cell the symmetric 3x3 matrix built from the six components is positive definite with a dominant diagonal.
All inputs are finite; a program needn't handle non-finite values.
Results may differ from a plain program's by a relative error of at most 0.0003.
Values sent between devices are 32-bit elements; how exact they have to be, the bound alone decides.
A program may use at most 128 MiB of HBM per device.

v0:
```python
import functools

import jax
import jax.numpy as jnp
from jax import lax
from jax.sharding import Mesh
from jax.sharding import PartitionSpec as P

GX_GY_GZ = ("gx", "gy", "gz_0", "gz_1")
GZ = ("gz_0", "gz_1")


pair_index = ((0, 1, 2), (1, 3, 4), (2, 4, 5))
first_taps = ((-2, 1.0 / 12.0), (-1, -8.0 / 12.0), (1, 8.0 / 12.0), (2, -1.0 / 12.0))
second_taps = (
    (-2, -1.0 / 12.0),
    (-1, 16.0 / 12.0),
    (0, -30.0 / 12.0),
    (1, 16.0 / 12.0),
    (2, -1.0 / 12.0),
)


def padded_2(cells, sides, width):
    for axis, dim in sides:
        count = lax.axis_size(axis)
        head = lax.slice_in_dim(cells, 0, width, axis=dim)
        tail = lax.slice_in_dim(cells, cells.shape[dim] - width, cells.shape[dim], axis=dim)
        cells = jnp.concatenate(
            [
                lax.ppermute(tail, axis, [(i, (i + 1) % count) for i in range(count)]),
                cells,
                lax.ppermute(head, axis, [((i + 1) % count, i) for i in range(count)]),
            ],
            axis=dim,
        )
    return cells


def with_halo(x, sides, width):
    edges = {}
    for axis, dim in sides:
        peers, length = (lax.axis_size(axis), x.shape[dim])
        up = [(i, (i + 1) % peers) for i in range(peers)]
        last = lax.slice_in_dim(x, length - width, length, axis=dim)
        initial = lax.slice_in_dim(x, 0, width, axis=dim)
        edges[dim] = (
            lax.ppermute(last, axis, up),
            lax.ppermute(initial, axis, [(b, a) for a, b in up]),
        )
    done = []
    for _, dim in sides:
        low, high = edges[dim]
        around = [(width, width) if d in done else (0, 0) for d in range(x.ndim)]
        x = jnp.concatenate([jnp.pad(low, around), x, jnp.pad(high, around)], axis=dim)
        done.append(dim)
    return x


def over_axes(x, axes):
    return functools.reduce(lax.psum, axes, x)


def window(padded, offsets):
    sx = padded.shape[-3] - 4
    sy = padded.shape[-2] - 4
    sz = padded.shape[-1] - 4
    return padded[
        ...,
        2 + offsets[0] : 2 + offsets[0] + sx,
        2 + offsets[1] : 2 + offsets[1] + sy,
        2 + offsets[2] : 2 + offsets[2] + sz,
    ]


def shifted(pairs):
    places = [0, 0, 0]
    for axis_num, step in pairs:
        places[axis_num] = places[axis_num] + step
    return tuple(places)


def first_diff(padded, axis_num):
    summed = None
    for step, weight in first_taps:
        term = weight * window(padded, shifted(((axis_num, step),)))
        summed = term if summed is None else summed + term
    return summed


def second_diff(padded, a, b):
    summed = None
    if a == b:
        for step, weight in second_taps:
            term = weight * window(padded, shifted(((a, step),)))
            summed = term if summed is None else summed + term
        return summed
    for step_a, weight_a in first_taps:
        for step_b, weight_b in first_taps:
            term = weight_a * weight_b * window(padded, shifted(((a, step_a), (b, step_b))))
            summed = term if summed is None else summed + term
    return summed


def constraints(geo_pad, rest_pad):
    centre = window(geo_pad, (0, 0, 0))
    remainder = window(rest_pad, (0, 0, 0))
    conformal = centre[0]
    trace_curv = remainder[6]
    geo_first = [first_diff(geo_pad, a) for a in range(3)]
    rest_first = [first_diff(rest_pad, a) for a in range(3)]
    geo_second = {}
    for a in range(3):
        for b in range(a, 3):
            geo_second[a, b] = second_diff(geo_pad, a, b)

    def metric_at(i, j):
        return centre[1 + pair_index[i][j]]

    def curv_at(i, j):
        return remainder[pair_index[i][j]]

    def metric_grad(i, j, a):
        return geo_first[a][1 + pair_index[i][j]]

    def curv_grad(i, j, a):
        return rest_first[a][pair_index[i][j]]

    chi_grad = [geo_first[a][0] for a in range(3)]
    trace_grad = [rest_first[a][6] for a in range(3)]
    g00, g01, g02 = (metric_at(0, 0), metric_at(0, 1), metric_at(0, 2))
    g11, g12, g22 = (metric_at(1, 1), metric_at(1, 2), metric_at(2, 2))
    minor00 = g11 * g22 - g12 * g12
    minor01 = g02 * g12 - g01 * g22
    minor02 = g01 * g12 - g02 * g11
    minor11 = g00 * g22 - g02 * g02
    minor12 = g01 * g02 - g00 * g12
    minor22 = g00 * g11 - g01 * g01
    determinant = g00 * minor00 + g01 * minor01 + g02 * minor02
    scale = 1.0 / determinant
    inverse_list = [
        minor00 * scale,
        minor01 * scale,
        minor02 * scale,
        minor11 * scale,
        minor12 * scale,
        minor22 * scale,
    ]

    def inv_at(i, j):
        return inverse_list[pair_index[i][j]]

    christ_low = [[[None] * 3 for i in range(3)] for k in range(3)]
    for k in range(3):
        for i in range(3):
            for j in range(i, 3):
                value = 0.5 * (metric_grad(k, j, i) + metric_grad(k, i, j) - metric_grad(i, j, k))
                christ_low[k][i][j] = value
                christ_low[k][j][i] = value
    christ_up = [[[None] * 3 for i in range(3)] for k in range(3)]
    for k in range(3):
        for i in range(3):
            for j in range(i, 3):
                value = (
                    inv_at(k, 0) * christ_low[0][i][j]
                    + inv_at(k, 1) * christ_low[1][i][j]
                    + inv_at(k, 2) * christ_low[2][i][j]
                )
                christ_up[k][i][j] = value
                christ_up[k][j][i] = value
    gamma_calc = []
    for k in range(3):
        summed = None
        for i in range(3):
            for j in range(3):
                term = inv_at(i, j) * christ_up[k][i][j]
                summed = term if summed is None else summed + term
        gamma_calc.append(summed)
    cov_hess = [[None] * 3 for i in range(3)]
    for i in range(3):
        for j in range(i, 3):
            value = geo_second[min(i, j), max(i, j)][0] - (
                christ_up[0][i][j] * chi_grad[0]
                + christ_up[1][i][j] * chi_grad[1]
                + christ_up[2][i][j] * chi_grad[2]
            )
            cov_hess[i][j] = value
            cov_hess[j][i] = value
    laplace = None
    grad_sq = None
    for l in range(3):
        for m in range(3):
            term = inv_at(l, m) * cov_hess[l][m]
            laplace = term if laplace is None else laplace + term
            term = inv_at(l, m) * chi_grad[l] * chi_grad[m]
            grad_sq = term if grad_sq is None else grad_sq + term
    scalar_sum = None
    for i in range(3):
        for j in range(i, 3):
            ricci = None
            for l in range(3):
                for m in range(3):
                    term = (
                        -0.5 * inv_at(l, m) * geo_second[min(l, m), max(l, m)][1 + pair_index[i][j]]
                    )
                    ricci = term if ricci is None else ricci + term
            for k in range(3):
                ricci = ricci + 0.5 * (
                    metric_at(k, i) * rest_first[j][7 + k] + metric_at(k, j) * rest_first[i][7 + k]
                )
                ricci = ricci + 0.5 * gamma_calc[k] * (christ_low[i][j][k] + christ_low[j][i][k])
            for l in range(3):
                for m in range(3):
                    inner = None
                    for k in range(3):
                        term = (
                            christ_up[k][l][i] * christ_low[j][k][m]
                            + christ_up[k][l][j] * christ_low[i][k][m]
                            + christ_up[k][i][m] * christ_low[k][l][j]
                        )
                        inner = term if inner is None else inner + term
                    ricci = ricci + inv_at(l, m) * inner
            conf_part = (cov_hess[i][j] + metric_at(i, j) * laplace) / (2.0 * conformal) - (
                chi_grad[i] * chi_grad[j] + 3.0 * metric_at(i, j) * grad_sq
            ) / (4.0 * conformal * conformal)
            weight = 1.0 if i == j else 2.0
            term = weight * inv_at(i, j) * (ricci + conf_part)
            scalar_sum = term if scalar_sum is None else scalar_sum + term
    mixed = [[None] * 3 for i in range(3)]
    for i in range(3):
        for j in range(3):
            mixed[i][j] = (
                curv_at(i, 0) * inv_at(0, j)
                + curv_at(i, 1) * inv_at(1, j)
                + curv_at(i, 2) * inv_at(2, j)
            )
    square_sum = None
    for i in range(3):
        for j in range(3):
            term = mixed[i][j] * mixed[j][i]
            square_sum = term if square_sum is None else square_sum + term
    hamilton = conformal * scalar_sum + 2.0 / 3.0 * trace_curv * trace_curv - square_sum
    momentum_list = []
    for i in range(3):
        summed = None
        for j in range(3):
            for k in range(3):
                term = inv_at(j, k) * curv_grad(k, i, j)
                summed = term if summed is None else summed + term
        for l in range(3):
            summed = summed - gamma_calc[l] * curv_at(l, i)
            for j in range(3):
                summed = summed - christ_up[l][j][i] * mixed[l][j]
        along = mixed[i][0] * chi_grad[0] + mixed[i][1] * chi_grad[1] + mixed[i][2] * chi_grad[2]
        summed = summed - 2.0 / 3.0 * trace_grad[i] - 1.5 * along / conformal
        momentum_list.append(summed)
    return (hamilton, jnp.stack(momentum_list))


def on_device(chi_field, metric, curvature, trace_curvature, gamma_field):
    geometry = jnp.concatenate([chi_field[None], metric], 0)
    remainder = jnp.concatenate([curvature, trace_curvature[None], gamma_field], 0)
    geo_pad = padded_2(geometry, (("gx", 1), ("gy", 2), (GZ, 3)), 2)
    rest_pad = with_halo(remainder, (("gx", 1), ("gy", 2), (GZ, 3)), 2)
    hamilton, momentum = constraints(geo_pad, rest_pad)
    local_sums = jnp.stack([jnp.sum(hamilton * hamilton), jnp.sum(momentum * momentum)])
    totals = over_axes(local_sums, GX_GY_GZ)
    cell_count = chi_field.size * lax.axis_size("gx") * lax.axis_size("gy") * lax.axis_size(GZ)
    norms = jnp.sqrt(totals / jnp.array([cell_count, 3 * cell_count], dtype=jnp.float32))
    return (hamilton, momentum, norms)


def solution(mesh):
    finer = Mesh(
        mesh.devices.reshape(mesh.shape["gx"], mesh.shape["gy"], 4, 2), ("gx", "gy", "gz_0", "gz_1")
    )
    return jax.shard_map(
        on_device,
        mesh=finer,
        in_specs=(
            P("gx", "gy", GZ),
            P(None, "gx", "gy", GZ),
            P(None, "gx", "gy", GZ),
            P("gx", "gy", GZ),
            P(None, "gx", "gy", GZ),
        ),
        out_specs=(P("gx", "gy", GZ), P(None, "gx", "gy", GZ), P()),
        check_vma=False,
    )
```

profile of v0, /device:TPU:1, one launch (start us, length us, event | category | flops | bytes accessed | tf_op | source)
XLA Modules:
  0.0 148.8 jit_solution(18381687215408577145)
XLA Ops:
  0.6 1.5 pad_maximum_fusion.6
  2.1 2.0 %fusion.579 = (f32[10,8,32,2]{3,2,1,0:T(8,128)}, f32[10,8,32,2]{3,2,1,0:T(8,128)}) fusion(f32[10,8,32,128]{3,2,1,0:T(8,128)S(1)} %pad_maximum_fusion.6), kind=kLoop, calls=%fused_computation.991 | loop fusion | bytes 81920 | tf_op jit(solution)/shard_map/slice | solution.py:45
  4.1 2.6 %copy.97 = f32[10,8,32,2]{2,1,3,0:T(8,128)} copy(f32[10,8,32,2]{3,2,1,0:T(8,128)} %get-tuple-element.59) | data formatting | bytes 40960
  6.7 2.6 %collective-permute-start.10 = (f32[10,8,32,2]{2,1,3,0:T(8,128)}, f32[10,8,32,2]{2,1,3,0:T(8,128)}, u32[]{:S(2)}, u32[]{:S(2)}) collective-permute-start(f32[10,8,32,2]{2,1,3,0:T(8,128)} %copy.97), channel_id=1, source_target_pairs={{0,1},{1,2},{2,3},{3,4},{4,5},{5,6},{6,7},{7,0},{8,9},{9,10},{10,1... | collective-permute-start | bytes 61448 | tf_op jit(solution)/shard_map/ppermute | solution.py:48
  9.3 2.5 %copy.98 = f32[10,8,32,2]{2,1,3,0:T(8,128)} copy(f32[10,8,32,2]{3,2,1,0:T(8,128)} %get-tuple-element.60) | data formatting | bytes 40960
  14.4 2.1 %collective-permute-start.9 = (f32[10,8,2,128]{3,1,2,0:T(8,128)}, f32[10,8,2,128]{3,1,2,0:T(8,128)}, u32[]{:S(2)}, u32[]{:S(2)}) collective-permute-start(f32[10,8,2,128]{3,1,2,0:T(8,128)} %copy.96), channel_id=1, source_target_pairs={{8,0},{16,8},{24,16},{0,24},{9,1},{17,9},{25,17},{1,25},{10,2},{18... | collective-permute-start | bytes 245768 | tf_op jit(solution)/shard_map/ppermute | solution.py:49
  19.2 3.9 %collective-permute-start.1 = (f32[7,2,32,128]{3,2,1,0:T(8,128)}, f32[7,2,32,128]{3,2,1,0:T(8,128)S(1)}, u32[]{:S(2)}, u32[]{:S(2)}) collective-permute-start(f32[7,2,32,128]{3,2,1,0:T(8,128)} %get-tuple-element.68), channel_id=1, source_target_pairs={{32,0},{64,32},{96,64},{128,96},{160,128},{192,160},{224,192},{0,2... | collective-permute-start | bytes 688136 | tf_op jit(solution)/shard_map/ppermute | solution.py:33
  23.9 2.5 %copy.101 = f32[10,8,32,2]{3,2,1,0:T(8,128)} copy(f32[10,8,32,2]{2,1,3,0:T(8,128)} %collective-permute-done.10) | data formatting | bytes 40960
  26.4 2.5 %copy.102 = f32[10,8,32,2]{3,2,1,0:T(8,128)} copy(f32[10,8,32,2]{2,1,3,0:T(8,128)} %collective-permute-done.11) | data formatting | bytes 40960
  28.9 2.7 %collective-permute-start.7 = (f32[10,2,32,128]{3,2,1,0:T(8,128)}, f32[10,2,32,128]{3,2,1,0:T(8,128)S(1)}, u32[]{:S(2)}, u32[]{:S(2)}) collective-permute-start(f32[10,2,32,128]{3,2,1,0:T(8,128)} %get-tuple-element.64), channel_id=1, source_target_pairs={{32,0},{64,32},{96,64},{128,96},{160,128},{192,160},{224,192},{0,2... | collective-permute-start | bytes 983048 | tf_op jit(solution)/shard_map/ppermute | solution.py:49
  34.7 2.7 %collective-permute-start.3 = (f32[7,12,2,128]{3,2,1,0:T(2,128)S(1)}, f32[7,12,2,128]{3,2,1,0:T(2,128)S(1)}, u32[]{:S(2)}, u32[]{:S(2)}) collective-permute-start(f32[7,12,2,128]{3,2,1,0:T(2,128)S(1)} %get-tuple-element.56), channel_id=1, source_target_pairs={{8,0},{16,8},{24,16},{0,24},{9,1},{17,9},{25,17},{1,25},{10,2},{18... | collective-permute-start | bytes 258056 | tf_op jit(solution)/shard_map/ppermute | solution.py:33
  38.6 1.7 %add_add_fusion.2 = (f32[7,8,32,128]{3,2,1,0:T(8,128)}, f32[7,8,32,128]{3,2,1,0:T(8,128)}) fusion(f32[7,10,32,128]{3,2,1,0:T(8,128)S(1)} %get-tuple-element.66, f32[7,10,32,128]{3,2,1,0:T(8,128)S(1)} %get-tuple-element.65, f32[6,8,32,128]{3,2,1,0:T(8,128)S(1)} %copy-done, f32[1,8,32,128]{3,2,1,0:T(8,128)S(1)} %bitcast.1498), kind=kLoop, calls=%fused_computation.141 | loop fusion | flops 3670016 | bytes 6422528 | tf_op jit(solution)/shard_map/add | solution.py:87
  41.7 2.3 %fusion.578 = (f32[7,12,36,2]{3,2,1,0:T(8,128)}, f32[7,12,36,2]{3,2,1,0:T(8,128)}) fusion(f32[7,12,36,128]{3,2,1,0:T(8,128)S(1)} %pad_maximum_fusion.3), kind=kLoop, calls=%fused_computation.990 | loop fusion | bytes 96768 | tf_op jit(solution)/shard_map/slice | solution.py:28
  44.0 2.8 %copy.93 = f32[7,12,36,2]{2,3,1,0:T(2,128)} copy(f32[7,12,36,2]{3,2,1,0:T(8,128)} %get-tuple-element.49) | data formatting | bytes 48384
  46.7 3.6 %collective-permute-start.4 = (f32[7,12,36,2]{2,3,1,0:T(2,128)}, f32[7,12,36,2]{2,3,1,0:T(2,128)}, u32[]{:S(2)}, u32[]{:S(2)}) collective-permute-start(f32[7,12,36,2]{2,3,1,0:T(2,128)} %copy.93), channel_id=1, source_target_pairs={{0,1},{1,2},{2,3},{3,4},{4,5},{5,6},{6,7},{7,0},{8,9},{9,10},{10,1... | collective-permute-start | bytes 72584 | tf_op jit(solution)/shard_map/ppermute | solution.py:31
  50.4 2.8 %copy.94 = f32[7,12,36,2]{2,3,1,0:T(2,128)} copy(f32[7,12,36,2]{3,2,1,0:T(8,128)} %get-tuple-element.50) | data formatting | bytes 48384
  54.7 2.8 %fusion.40 = f32[7,8,32,128]{3,2,1,0:T(8,128)} fusion(f32[7,12,34,128]{3,2,1,0:T(8,128)S(1)} %get-tuple-element.54, f32[7,12,34,128]{3,2,1,0:T(8,128)S(1)} %get-tuple-element.53), kind=kLoop, calls=%fused_computation.108 | loop fusion | flops 7110656 | bytes 15597568 | tf_op jit(solution)/shard_map/add | solution.py:101
  57.5 1.9 %add_add_fusion.1 = (f32[7,8,32,128]{3,2,1,0:T(8,128)}, f32[7,8,32,128]{3,2,1,0:T(8,128)}) fusion(f32[7,12,34,128]{3,2,1,0:T(8,128)S(1)} %get-tuple-element.54, f32[7,12,34,128]{3,2,1,0:T(8,128)S(1)} %get-tuple-element.53, f32[6,8,32,128]{3,2,1,0:T(8,128)S(1)} %copy-done, f32[1,8,32,128]{3,2,1,0:T(8,128)S(1)} %bitcast.1501), kind=kLoop, calls=%fused_computation.140 | loop fusion | flops 3670016 | bytes 6422528 | tf_op jit(solution)/shard_map/add | solution.py:87
  59.4 2.6 %maximum_maximum_fusion.1 = (f32[10,12,34,128]{3,2,1,0:T(8,128)S(1)}, f32[10,12,34,128]{3,2,1,0:T(8,128)}) fusion(f32[10,2,32,128]{3,2,1,0:T(8,128)S(1)} %collective-permute-done.7, f32[3,8,32,128]{3,2,1,0:T(8,128)S(1)} %copy-done.3, f32[1,8,32,128]{3,2,1,0:T(8,128)S(1)} %bitcast.1506, f32[6,8,32,128]{3,2,1,0:T(8,128)S(1)} %copy-done.1, ...), kind=kLoop, calls=%fused_computation.6 | loop fusion | flops 5222400 | bytes 6389760 | tf_op jit(solution)/shard_map/concatenate | solution.py:55
  62.0 6.0 %select_maximum_fusion.1 = (f32[10,12,36,130]{3,2,1,0:T(8,128)S(1)}, f32[10,12,36,130]{3,2,1,0:T(8,128)S(1)}) fusion(f32[10,8,32,2]{3,2,1,0:T(8,128)S(1)} %copy-done.10, f32[10,12,2,128]{3,2,1,0:T(2,128)S(1)} %pad.15.clone, f32[10,2,32,128]{3,2,1,0:T(8,128)S(1)} %collective-permute-done.7, f32[3,8,32,128]{3,2,1,0:T(8,128)S(1)} %copy-done.3, ...), kind=kLoop, calls=%fused_computation.2 | loop fusion | flops 10108800 | bytes 6745600 | tf_op jit(solution)/shard_map/concatenate | solution.py:55
  68.1 4.7 %fusion = (f32[10,8,32,128]{3,2,1,0:T(8,128)S(1)}, f32[10,8,32,128]{3,2,1,0:T(8,128)}) fusion(f32[10,12,36,130]{3,2,1,0:T(8,128)S(1)} %get-tuple-element.46, f32[10,12,36,130]{3,2,1,0:T(8,128)S(1)} %get-tuple-element.45, f32[10,12,34,128]{3,2,1,0:T(8,128)} %get-tuple-element.48, f32[10,12,34,128]{3,2,1,0:T(8,128)S(1)} %get-tuple-element.47), kind=kLoop, calls=%fused_computation.17 | loop fusion | flops 4587520 | bytes 13107200 | tf_op jit(solution)/shard_map/add | solution.py:87
  74.1 1.5 %fusion.6 = f32[10,8,32,128]{3,2,1,0:T(8,128)} fusion(f32[10,10,32,128]{3,2,1,0:T(8,128)S(1)} %get-tuple-element.58, f32[10,10,32,128]{3,2,1,0:T(8,128)S(1)} %get-tuple-element.57), kind=kLoop, calls=%fused_computation.31 | loop fusion | flops 2293760 | bytes 6553600 | tf_op jit(solution)/shard_map/add | solution.py:87
  75.6 2.9 %copy.80 = f32[7,12,36,2]{3,2,1,0:T(8,128)} copy(f32[7,12,36,2]{2,3,1,0:T(2,128)} %collective-permute-done.4) | data formatting | bytes 48384 | tf_op jit(solution)/shard_map/ppermute | solution.py:31
  78.5 2.8 %copy.82 = f32[7,12,36,2]{3,2,1,0:T(8,128)} copy(f32[7,12,36,2]{2,3,1,0:T(2,128)} %collective-permute-done.5) | data formatting | bytes 48384 | tf_op jit(solution)/shard_map/ppermute | solution.py:33
  81.3 5.3 %maximum_maximum_fusion = (f32[7,12,36,130]{3,2,1,0:T(8,128)S(1)}, f32[7,12,36,130]{3,2,1,0:T(8,128)S(1)}) fusion(f32[7,12,2,128]{3,2,1,0:T(2,128)} %copy-done.21, f32[7,2,32,128]{3,2,1,0:T(8,128)S(1)} %copy-done.9, f32[6,8,32,128]{3,2,1,0:T(8,128)S(1)} %copy-done, f32[1,8,32,128]{3,2,1,0:T(8,128)S(1)} %bitcast.1502, ...), kind=kLoop, calls=%fused_computation.4 | loop fusion | flops 4717440 | bytes 4741632 | tf_op jit(solution)/shard_map/concatenate | solution.py:29
  86.6 3.4 %fusion.25 = f32[7,8,32,128]{3,2,1,0:T(8,128)S(1)} fusion(f32[7,12,36,130]{3,2,1,0:T(8,128)S(1)} %get-tuple-element.52, f32[7,12,36,130]{3,2,1,0:T(8,128)S(1)} %get-tuple-element.51), kind=kLoop, calls=%fused_computation.77 | loop fusion | flops 7110656 | bytes 15597568 | tf_op jit(solution)/shard_map/add | solution.py:101
  90.0 3.2 %fusion.10 = f32[7,8,32,128]{3,2,1,0:T(8,128)S(1)} fusion(f32[7,12,36,130]{3,2,1,0:T(8,128)S(1)} %get-tuple-element.52, f32[7,12,36,130]{3,2,1,0:T(8,128)S(1)} %get-tuple-element.51), kind=kLoop, calls=%fused_computation.45 | loop fusion | flops 7110656 | bytes 15597568 | tf_op jit(solution)/shard_map/add | solution.py:101
  96.1 9.0 %multiply_reduce_fusion.1 = (f32[]{:T(128)}, f32[8,32,128]{2,1,0:T(8,128)}, f32[8,32,128]{2,1,0:T(8,128)S(1)}, f32[8,32,128]{2,1,0:T(8,128)S(1)}, f32[8,32,128]{...) fusion(f32[6,8,32,128]{3,2,1,0:T(8,128)S(1)} %copy-done.1, ...), kind=kLoop, calls=%fused_computation.844 | loop fusion | flops 45219840 | bytes 15204356 | tf_op jit(solution)/shard_map/reduce_sum | solution.py:266
  109.8 11.2 %psum.28 = f32[2]{0:T(128)S(1)} all-reduce(f32[2]{0:T(128)S(1)} %pad_maximum_fusion.15), channel_id=1, replica_groups=mesh['gx'=8,'gy'=4,'gz_0'=4,'gz_1'=2] {'gx'}, use_global_device_ids=true, to_apply=%region_2.3 | all-reduce | flops 2 | bytes 16 | tf_op jit(solution)/shard_map/psum | solution.py:61
  121.0 8.3 %psum.29 = f32[2]{0:T(128)S(1)} all-reduce(f32[2]{0:T(128)S(1)} %psum.28), channel_id=1, replica_groups=mesh['gx'=8,'gy'=4,'gz_0'=4,'gz_1'=2] {'gy'}, use_global_device_ids=true, to_apply=%region_3.4 | all-reduce | flops 2 | bytes 16 | tf_op jit(solution)/shard_map/psum | solution.py:61
  129.4 8.6 %psum.30 = f32[2]{0:T(128)S(1)} all-reduce(f32[2]{0:T(128)S(1)} %psum.29), channel_id=1, replica_groups=mesh['gx'=8,'gy'=4,'gz_0'=4,'gz_1'=2] {'gz_0'}, use_global_device_ids=true, to_apply=%region_4.5 | all-reduce | flops 2 | bytes 16 | tf_op jit(solution)/shard_map/psum | solution.py:61
  137.9 10.3 %psum.31 = f32[2]{0:T(128)S(1)} all-reduce(f32[2]{0:T(128)S(1)} %psum.30), channel_id=1, replica_groups=mesh['gx'=8,'gy'=4,'gz_0'=4,'gz_1'=2] {'gz_1'}, use_global_device_ids=true, to_apply=%region_5.6 | all-reduce | flops 2 | bytes 16 | tf_op jit(solution)/shard_map/psum | solution.py:61
  (92 shorter events, 22.7 us)
Async XLA Ops:
  4.1 8.4 %copy-start.1 = (f32[6,8,32,128]{3,2,1,0:T(8,128)S(1)}, f32[6,8,32,128]{3,2,1,0:T(8,128)}, u32[]{:S(2)}) copy-start(f32[6,8,32,128]{3,2,1,0:T(8,128)} %param.8) | copy-start | bytes 2359300
  4.1 8.4 %copy-start.3 = (f32[3,8,32,128]{3,2,1,0:T(8,128)S(1)}, f32[3,8,32,128]{3,2,1,0:T(8,128)}, u32[]{:S(2)}) copy-start(f32[3,8,32,128]{3,2,1,0:T(8,128)} %param.10) | copy-start | bytes 1179652
  4.1 8.4 %copy-start.12 = (f32[8,32,128]{2,1,0:T(8,128)S(1)}, f32[8,32,128]{2,1,0:T(8,128)}, u32[]{:S(2)}) copy-start(f32[8,32,128]{2,1,0:T(8,128)} %param.9) | copy-start | bytes 393220
  6.7 9.8 %copy-start = (f32[6,8,32,128]{3,2,1,0:T(8,128)S(1)}, f32[6,8,32,128]{3,2,1,0:T(8,128)}, u32[]{:S(2)}) copy-start(f32[6,8,32,128]{3,2,1,0:T(8,128)} %param.7) | copy-start | bytes 2359300
  6.7 9.8 %copy-start.2 = (f32[8,32,128]{2,1,0:T(8,128)S(1)}, f32[8,32,128]{2,1,0:T(8,128)}, u32[]{:S(2)}) copy-start(f32[8,32,128]{2,1,0:T(8,128)} %param.6) | copy-start | bytes 393220
  6.7 12.5 %collective-permute-start.10 = (f32[10,8,32,2]{2,1,3,0:T(8,128)}, f32[10,8,32,2]{2,1,3,0:T(8,128)}, u32[]{:S(2)}, u32[]{:S(2)}) collective-permute-start(f32[10,8,32,2]{2,1,3,0:T(8,128)} %copy.97), channel_id=1, source_target_pairs={{0,1},{1,2},{2,3},{3,4},{4,5},{5,6},{6,7},{7,0},{8,9},{9,10},{10,1... | collective-permute-start | bytes 61448 | tf_op jit(solution)/shard_map/ppermute | solution.py:48
  11.8 14.6 %collective-permute-start.11 = (f32[10,8,32,2]{2,1,3,0:T(8,128)}, f32[10,8,32,2]{2,1,3,0:T(8,128)}, u32[]{:S(2)}, u32[]{:S(2)}) collective-permute-start(f32[10,8,32,2]{2,1,3,0:T(8,128)} %copy.98), channel_id=1, source_target_pairs={{1,0},{2,1},{3,2},{4,3},{5,4},{6,5},{7,6},{0,7},{9,8},{10,9},{11,1... | collective-permute-start | bytes 61448 | tf_op jit(solution)/shard_map/ppermute | solution.py:49
  13.2 15.8 %collective-permute-start.8 = (f32[10,8,2,128]{3,1,2,0:T(8,128)}, f32[10,8,2,128]{3,1,2,0:T(8,128)}, u32[]{:S(2)}, u32[]{:S(2)}) collective-permute-start(f32[10,8,2,128]{3,1,2,0:T(8,128)} %copy.95), channel_id=1, source_target_pairs={{0,8},{8,16},{16,24},{24,0},{1,9},{9,17},{17,25},{25,1},{2,10},{10... | collective-permute-start | bytes 245768 | tf_op jit(solution)/shard_map/ppermute | solution.py:48
  14.4 18.2 %collective-permute-start.9 = (f32[10,8,2,128]{3,1,2,0:T(8,128)}, f32[10,8,2,128]{3,1,2,0:T(8,128)}, u32[]{:S(2)}, u32[]{:S(2)}) collective-permute-start(f32[10,8,2,128]{3,1,2,0:T(8,128)} %copy.96), channel_id=1, source_target_pairs={{8,0},{16,8},{24,16},{0,24},{9,1},{17,9},{25,17},{1,25},{10,2},{18... | collective-permute-start | bytes 245768 | tf_op jit(solution)/shard_map/ppermute | solution.py:49
  17.3 16.3 %collective-permute-start = (f32[7,2,32,128]{3,2,1,0:T(8,128)}, f32[7,2,32,128]{3,2,1,0:T(8,128)}, u32[]{:S(2)}, u32[]{:S(2)}) collective-permute-start(f32[7,2,32,128]{3,2,1,0:T(8,128)} %get-tuple-element.67), channel_id=1, source_target_pairs={{0,32},{32,64},{64,96},{96,128},{128,160},{160,192},{192,224},{224... | collective-permute-start | bytes 688136 | tf_op jit(solution)/shard_map/ppermute | solution.py:31
  19.2 14.4 %collective-permute-start.1 = (f32[7,2,32,128]{3,2,1,0:T(8,128)}, f32[7,2,32,128]{3,2,1,0:T(8,128)S(1)}, u32[]{:S(2)}, u32[]{:S(2)}) collective-permute-start(f32[7,2,32,128]{3,2,1,0:T(8,128)} %get-tuple-element.68), channel_id=1, source_target_pairs={{32,0},{64,32},{96,64},{128,96},{160,128},{192,160},{224,192},{0,2... | collective-permute-start | bytes 688136 | tf_op jit(solution)/shard_map/ppermute | solution.py:33
  26.4 33.0 %collective-permute-start.6 = (f32[10,2,32,128]{3,2,1,0:T(8,128)}, f32[10,2,32,128]{3,2,1,0:T(8,128)S(1)}, u32[]{:S(2)}, u32[]{:S(2)}) collective-permute-start(f32[10,2,32,128]{3,2,1,0:T(8,128)} %get-tuple-element.63), channel_id=1, source_target_pairs={{0,32},{32,64},{64,96},{96,128},{128,160},{160,192},{192,224},{224... | collective-permute-start | bytes 983048 | tf_op jit(solution)/shard_map/ppermute | solution.py:48
  28.9 30.5 %collective-permute-start.7 = (f32[10,2,32,128]{3,2,1,0:T(8,128)}, f32[10,2,32,128]{3,2,1,0:T(8,128)S(1)}, u32[]{:S(2)}, u32[]{:S(2)}) collective-permute-start(f32[10,2,32,128]{3,2,1,0:T(8,128)} %get-tuple-element.64), channel_id=1, source_target_pairs={{32,0},{64,32},{96,64},{128,96},{160,128},{192,160},{224,192},{0,2... | collective-permute-start | bytes 983048 | tf_op jit(solution)/shard_map/ppermute | solution.py:49
  33.6 19.7 %copy-start.8 = (f32[7,2,32,128]{3,2,1,0:T(8,128)}, f32[7,2,32,128]{3,2,1,0:T(8,128)S(1)}, u32[]{:S(2)}) copy-start(f32[7,2,32,128]{3,2,1,0:T(8,128)S(1)} %collective-permute-done.1) | copy-start | bytes 688132
  34.6 5.8 %collective-permute-start.2 = (f32[7,12,2,128]{3,2,1,0:T(2,128)S(1)}, f32[7,12,2,128]{3,2,1,0:T(2,128)S(1)}, u32[]{:S(2)}, u32[]{:S(2)}) collective-permute-start(f32[7,12,2,128]{3,2,1,0:T(2,128)S(1)} %get-tuple-element.55), channel_id=1, source_target_pairs={{0,8},{8,16},{16,24},{24,0},{1,9},{9,17},{17,25},{25,1},{2,10},{10... | collective-permute-start | bytes 258056 | tf_op jit(solution)/shard_map/ppermute | solution.py:31
  34.7 5.7 %collective-permute-start.3 = (f32[7,12,2,128]{3,2,1,0:T(2,128)S(1)}, f32[7,12,2,128]{3,2,1,0:T(2,128)S(1)}, u32[]{:S(2)}, u32[]{:S(2)}) collective-permute-start(f32[7,12,2,128]{3,2,1,0:T(2,128)S(1)} %get-tuple-element.56), channel_id=1, source_target_pairs={{8,0},{16,8},{24,16},{0,24},{9,1},{17,9},{25,17},{1,25},{10,2},{18... | collective-permute-start | bytes 258056 | tf_op jit(solution)/shard_map/ppermute | solution.py:33
  40.4 12.9 %copy-start.19 = (f32[7,12,2,128]{3,2,1,0:T(2,128)}, f32[7,12,2,128]{3,2,1,0:T(2,128)S(1)}, u32[]{:S(2)}) copy-start(f32[7,12,2,128]{3,2,1,0:T(2,128)S(1)} %collective-permute-done.2) | copy-start | bytes 258052
  40.4 12.9 %copy-start.21 = (f32[7,12,2,128]{3,2,1,0:T(2,128)}, f32[7,12,2,128]{3,2,1,0:T(2,128)S(1)}, u32[]{:S(2)}) copy-start(f32[7,12,2,128]{3,2,1,0:T(2,128)S(1)} %collective-permute-done.3) | copy-start | bytes 258052
  46.7 28.9 %collective-permute-start.4 = (f32[7,12,36,2]{2,3,1,0:T(2,128)}, f32[7,12,36,2]{2,3,1,0:T(2,128)}, u32[]{:S(2)}, u32[]{:S(2)}) collective-permute-start(f32[7,12,36,2]{2,3,1,0:T(2,128)} %copy.93), channel_id=1, source_target_pairs={{0,1},{1,2},{2,3},{3,4},{4,5},{5,6},{6,7},{7,0},{8,9},{9,10},{10,1... | collective-permute-start | bytes 72584 | tf_op jit(solution)/shard_map/ppermute | solution.py:31
  53.1 25.4 %collective-permute-start.5 = (f32[7,12,36,2]{2,3,1,0:T(2,128)}, f32[7,12,36,2]{2,3,1,0:T(2,128)}, u32[]{:S(2)}, u32[]{:S(2)}) collective-permute-start(f32[7,12,36,2]{2,3,1,0:T(2,128)} %copy.94), channel_id=1, source_target_pairs={{1,0},{2,1},{3,2},{4,3},{5,4},{6,5},{7,6},{0,7},{9,8},{10,9},{11,1... | collective-permute-start | bytes 72584 | tf_op jit(solution)/shard_map/ppermute | solution.py:33
  59.4 2.6 %copy-start.10 = (f32[10,8,32,2]{3,2,1,0:T(8,128)S(1)}, f32[10,8,32,2]{3,2,1,0:T(8,128)}, u32[]{:S(2)}) copy-start(f32[10,8,32,2]{3,2,1,0:T(8,128)} %copy.101) | copy-start | bytes 61444
  59.4 2.6 %copy-start.11 = (f32[10,8,32,2]{3,2,1,0:T(8,128)S(1)}, f32[10,8,32,2]{3,2,1,0:T(8,128)}, u32[]{:S(2)}) copy-start(f32[10,8,32,2]{3,2,1,0:T(8,128)} %copy.102) | copy-start | bytes 61444
  59.4 2.6 %copy-start.16 = (f32[10,2,32,128]{3,2,1,0:T(8,128)}, f32[10,2,32,128]{3,2,1,0:T(8,128)S(1)}, u32[]{:S(2)}) copy-start(f32[10,2,32,128]{3,2,1,0:T(8,128)S(1)} %collective-permute-done.6) | copy-start | bytes 983044
  68.0 4.7 %copy-start.17 = (f32[10,2,32,128]{3,2,1,0:T(8,128)S(1)}, f32[10,2,32,128]{3,2,1,0:T(8,128)}, u32[]{:S(2)}) copy-start(f32[10,2,32,128]{3,2,1,0:T(8,128)} %copy-done.16) | copy-start | bytes 983044
  75.6 5.6 %copy-start.9 = (f32[7,2,32,128]{3,2,1,0:T(8,128)S(1)}, f32[7,2,32,128]{3,2,1,0:T(8,128)}, u32[]{:S(2)}) copy-start(f32[7,2,32,128]{3,2,1,0:T(8,128)} %copy-done.8) | copy-start | bytes 688132
  75.6 5.6 %copy-start.20 = (f32[7,12,2,128]{3,2,1,0:T(2,128)S(1)}, f32[7,12,2,128]{3,2,1,0:T(2,128)}, u32[]{:S(2)}) copy-start(f32[7,12,2,128]{3,2,1,0:T(2,128)} %copy-done.19) | copy-start | bytes 258052
  90.0 4.3 %copy-start.15 = (f32[7,8,32,128]{3,2,1,0:T(8,128)S(1)}, f32[7,8,32,128]{3,2,1,0:T(8,128)}, u32[]{:S(2)}) copy-start(f32[7,8,32,128]{3,2,1,0:T(8,128)} %fusion.40) | copy-start | bytes 2752516
  90.0 4.3 %copy-start.23 = (f32[8,32,128]{2,1,0:T(8,128)S(1)}, f32[8,32,128]{2,1,0:T(8,128)}, u32[]{:S(2)}) copy-start(f32[8,32,128]{2,1,0:T(8,128)} %get-tuple-element.37) | copy-start | bytes 393220
  90.0 4.3 %copy-start.24 = (f32[8,32,128]{2,1,0:T(8,128)S(1)}, f32[8,32,128]{2,1,0:T(8,128)}, u32[]{:S(2)}) copy-start(f32[8,32,128]{2,1,0:T(8,128)} %get-tuple-element.38) | copy-start | bytes 393220
  93.3 2.8 %copy-start.14 = (f32[7,8,32,128]{3,2,1,0:T(8,128)S(1)}, f32[7,8,32,128]{3,2,1,0:T(8,128)}, u32[]{:S(2)}) copy-start(f32[7,8,32,128]{3,2,1,0:T(8,128)} %get-tuple-element.42) | copy-start | bytes 2752516
  93.3 2.7 %copy-start.22 = (f32[8,32,128]{2,1,0:T(8,128)S(1)}, f32[8,32,128]{2,1,0:T(8,128)}, u32[]{:S(2)}) copy-start(f32[8,32,128]{2,1,0:T(8,128)} %get-tuple-element.36) | copy-start | bytes 393220
  106.4 41.8 %copy-start.25 = (f32[2]{0:T(128)S(1)}, f32[2]{0:T(128)}, u32[]{:S(2)}) copy-start(f32[2]{0:T(128)} %constant.58) | copy-start | bytes 28
  (6 other events, 12.2 us)
where the time goes:
time: 150 us; the launch traced here: 149 us
  other arithmetic  57.8 us (39%)
  blocking collectives  38.4 us (26%)
  local copies, waits for them, and re-layouts  31.4 us (21%)
  starting transfers between devices  20.1 us (13%)
    psum x4, blocking collectives, over_axes(): return functools.reduce(lax.psum, axes, x)  38.4 us
    unnamed x62, local copies, waits for them, and re-layouts  20.6 us
    add x5, other arithmetic, first_diff(): summed = term if summed is None else summed + term  10.8 us
    concatenate x3, other arithmetic, with_halo(): jnp.concatenate([jnp.pad(low, around), x, jnp.pad(high, around)], axis=dim)  9.96 us
    add x3, other arithmetic, second_diff(): summed = term if summed is None else summed + term  9.41 us
    concatenate x4, other arithmetic, padded_2(): jnp.concatenate([lax.ppermute(tail, axis, [(i, (i + 1) % count) for i in...  9.21 us
    reduce_sum x1, other arithmetic, on_device(): jnp.sum(hamilton * hamilton)  9 us
    ppermute x3, starting transfers between devices, padded_2(): lax.ppermute(head, axis, [((i + 1) % count, i) for i in range(count)])  6.71 us
  transfers between devices with their start and end apart: 12, of which 0 were waited for; matrix products, arithmetic and copies ran while one was open for 35% of the time, Pallas kernels for 0%

commit v1 on v0

v1 whole, which is shorter than its diff:
```python
import functools

import jax
import jax.numpy as jnp
from jax import lax
from jax.experimental import pallas as pl
from jax.experimental.pallas import tpu as pltpu
from jax.sharding import PartitionSpec as P

MESH = pl.DeviceIdType.MESH
PAIR = ((0, 1, 2), (1, 3, 4), (2, 4, 5))

CX, CY, CZ = 8, 32, 128
LX, ROWS, OWN = CX + 4, 48, 8
BLOCKS = CY // 8
PAIRS = CX // 2
GEO, REST = 7, 10
Y_REST = (0, 1, 2, 3, 4, 5, 6, 8)
Z_REST = (0, 1, 2, 3, 4, 5, 6, 9)
X_REST = 8

S_GEO_X, S_EDGE_XY, S_EDGE_YZ, S_EDGE_XZ = 0, 8, 12, 16
S_GEO_Y, S_GEO_Z, S_REST_Y, S_REST_Z, S_TERM = 20, 22, 24, 26, 28
S_SUM_A, S_SUM_B, S_COUNT = 36, 68, 76


def lane_ids():
    return lax.broadcasted_iota(jnp.int32, (8, CZ), 1)


def inverse_of(g):
    g00, g01, g02, g11, g12, g22 = g
    m00 = g11 * g22 - g12 * g12
    m01 = g02 * g12 - g01 * g22
    m02 = g01 * g12 - g02 * g11
    m11 = g00 * g22 - g02 * g02
    m12 = g01 * g02 - g00 * g12
    m22 = g00 * g11 - g01 * g01
    scale = 1.0 / (g00 * m00 + g01 * m01 + g02 * m02)
    return [m00 * scale, m01 * scale, m02 * scale, m11 * scale, m12 * scale, m22 * scale]


def first(lo2, lo1, hi1, hi2):
    return (lo2 - hi2) + 8.0 * (hi1 - lo1)


def second(lo2, lo1, mid, hi1, hi2):
    return 16.0 * (lo1 + hi1) - (lo2 + hi2) - 30.0 * mid


def kernel(
    sizes,
    chi_in, met_in, cur_in, trk_in, gam_in,
    ham_out, mom_out, norm_out,
    F, R, DZ, DZZ, DX, DXX, OUT, ACC,
    YSG, YSR, YRG, YRR, XYR,
    ZSG, ZSR, ZRG, ZRR,
    CS, CR, MINE, SUM_A, SUM_B,
    load_sem, out_sem, send_sem, recv_sem,
):
    n_gx, n_gy, n_gz = sizes
    ix, iy, iz = lax.axis_index("gx"), lax.axis_index("gy"), lax.axis_index("gz")

    def at(dx, dy, dz):
        return (
            lax.rem(ix + dx + n_gx, n_gx),
            lax.rem(iy + dy + n_gy, n_gy),
            lax.rem(iz + dz + n_gz, n_gz),
        )

    def remote(src, dst, place, device):
        return pltpu.make_async_remote_copy(
            src_ref=src, dst_ref=dst, send_sem=send_sem.at[place], recv_sem=recv_sem.at[place],
            device_id=device, device_id_type=MESH,
        )

    loads = [
        (chi_in, F.at[0, 2 : 2 + CX, OWN : OWN + CY]),
        (met_in, F.at[1:7, 2 : 2 + CX, OWN : OWN + CY]),
        (cur_in, R.at[0:6, 2 : 2 + CX, OWN : OWN + CY]),
        (trk_in, R.at[6, 2 : 2 + CX, OWN : OWN + CY]),
        (gam_in, R.at[7:10, 2 : 2 + CX, OWN : OWN + CY]),
    ]
    loads = [pltpu.make_async_copy(s, d, load_sem.at[i]) for i, (s, d) in enumerate(loads)]
    for copy in loads:
        copy.start()

    barrier = pltpu.get_barrier_semaphore()
    n_plane = n_gy * n_gz
    rank_a = iy * n_gz + iz

    def plane_peer(j):
        rank = lax.rem(rank_a + j, n_plane)
        return rank, (ix, rank // n_gz, lax.rem(rank, n_gz))

    def greet_plane(j, _):
        pl.semaphore_signal(barrier, inc=1, device_id=plane_peer(j)[1], device_id_type=MESH)
        return 0

    corners = [(a, b, 0) for a in (-1, 1) for b in (-1, 1)] + [(a, 0, b) for a in (-1, 1) for b in (-1, 1)]
    for step in corners + [(j, 0, 0) for j in range(1, n_gx)]:
        pl.semaphore_signal(barrier, inc=1, device_id=at(*step), device_id_type=MESH)
    lax.fori_loop(1, n_plane, greet_plane, 0)

    lane2 = lane_ids() // 2
    zero = jnp.zeros((8, CZ), jnp.float32)

    def clear(c, _):
        for layer in (0, 1, LX - 2, LX - 1):
            for b in range(BLOCKS):
                R[c, layer, pl.ds(OWN + 8 * b, 8), :] = zero
        return 0

    lax.fori_loop(0, X_REST, clear, 0)
    ACC[...] = jnp.zeros_like(ACC)

    def pack_z(source, channels, to):
        def body(p, _):
            low, high = zero, zero
            for n, c in enumerate(channels):
                for xi in range(2):
                    for b in range(BLOCKS):
                        t = (n * 2 + xi) * BLOCKS + b
                        tile = source[c, 2 + 2 * p + xi, pl.ds(OWN + 8 * b, 8), :]
                        here = lane2 == t
                        low = jnp.where(here, pltpu.roll(tile, 2 * t, 1) if t else tile, low)
                        up = (2 * t + 2) % CZ
                        high = jnp.where(here, pltpu.roll(tile, up, 1) if up else tile, high)
            to[0, p] = low
            to[1, p] = high
            return 0

        lax.fori_loop(0, PAIRS, body, 0)

    loads[0].wait()
    loads[1].wait()
    pack_z(F, range(GEO), ZSG)

    def pack_y_geo(p, _):
        for c in range(GEO):
            for xi in range(2):
                rows = slice(c * 4 + xi * 2, c * 4 + xi * 2 + 2)
                YSG[0, p, rows, :] = F[c, 2 + 2 * p + xi, OWN : OWN + 2, :]
                YSG[1, p, rows, :] = F[c, 2 + 2 * p + xi, OWN + CY - 2 : OWN + CY, :]
        return 0

    for s in range(2):
        for p in range(PAIRS):
            YSG[s, p, 24:32, :] = zero
    lax.fori_loop(0, PAIRS, pack_y_geo, 0)

    pl.semaphore_wait(barrier, n_plane - 1 + n_gx - 1 + len(corners))

    def geo_x(d, b):
        rows = pl.ds(OWN + 8 * b, 8)
        src = F.at[0:GEO, pl.ds(2 if d == 0 else CX, 2), rows]
        dst = F.at[0:GEO, pl.ds(CX + 2 if d == 0 else 0, 2), rows]
        return remote(src, dst, S_GEO_X + 4 * d + b, at(2 * d - 1, 0, 0))

    geo_xs = [[geo_x(d, b) for b in range(BLOCKS)] for d in range(2)]
    geo_ys = [remote(YSG.at[d], YRG.at[1 - d], S_GEO_Y + d, at(0, 2 * d - 1, 0)) for d in range(2)]
    geo_zs = [
        remote(ZSG.at[d], ZRG.at[1 - d, 0, 1 : 1 + PAIRS], S_GEO_Z + d, at(0, 0, 2 * d - 1)) for d in range(2)
    ]
    combos = [(a, b) for a in range(2) for b in range(2)]
    edge_xy = [
        remote(
            YSG.at[dy, PAIRS - 1 if dx else 0], XYR.at[1 - dx, 1 - dy], S_EDGE_XY + 2 * dx + dy,
            at(2 * dx - 1, 2 * dy - 1, 0),
        )
        for dx, dy in combos
    ]
    edge_yz = [
        remote(
            ZSG.at[dz], ZRG.at[1 - dz, 1 if dy else 2, 1 : 1 + PAIRS], S_EDGE_YZ + 2 * dy + dz,
            at(0, 2 * dy - 1, 2 * dz - 1),
        )
        for dy, dz in combos
    ]
    edge_xz = [
        remote(
            ZSG.at[dz, pl.ds(PAIRS - 1 if dx else 0, 1)], ZRG.at[1 - dz, 0, pl.ds(0 if dx else PAIRS + 1, 1)],
            S_EDGE_XZ + 2 * dx + dz, at(2 * dx - 1, 0, 2 * dz - 1),
        )
        for dx, dz in combos
    ]
    for b in range(BLOCKS):
        for d in range(2):
            geo_xs[d][b].start()
        if b == 0:
            for copy in geo_zs + geo_ys + edge_yz:
                copy.start()
        if b == 1:
            for copy in edge_xy + edge_xz:
                copy.start()

    for copy in loads[2:]:
        copy.wait()
    pack_z(R, Z_REST, ZSR)

    def pack_y_rest(x, _):
        rows = pl.ds(2 * x, 2)
        for n, c in enumerate(Y_REST):
            YSR[0, n, rows, :] = R[c, 2 + x, OWN : OWN + 2, :]
            YSR[1, n, rows, :] = R[c, 2 + x, OWN + CY - 2 : OWN + CY, :]
        return 0

    lax.fori_loop(0, CX, pack_y_rest, 0)
    rest_zs = [remote(ZSR.at[d], ZRR.at[1 - d], S_REST_Z + d, at(0, 0, 2 * d - 1)) for d in range(2)]
    rest_ys = [remote(YSR.at[d], YRR.at[1 - d], S_REST_Y + d, at(0, 2 * d - 1, 0)) for d in range(2)]

    lane = lane_ids()

    def z_taps(tile, left, right, t):
        from_left = pltpu.roll(left, CZ - 2 - 2 * t, 1)
        from_right = pltpu.roll(right, lax.rem(CZ - 2 * t, CZ), 1)
        return (
            pltpu.roll(jnp.where(lane >= CZ - 2, from_left, tile), 2, 1),
            pltpu.roll(jnp.where(lane >= CZ - 1, from_left, tile), 1, 1),
            pltpu.roll(jnp.where(lane < 1, from_right, tile), CZ - 1, 1),
            pltpu.roll(jnp.where(lane < 2, from_right, tile), CZ - 2, 1),
        )

    def z_geo(layer, pair, xi, rows, variant, b, out):
        left, right = ZRG[0, variant, pair], ZRG[1, variant, pair]
        for c in range(GEO):
            tile = F[c, layer, rows, :]
            taps = z_taps(tile, left, right, (c * 2 + xi) * BLOCKS + b)
            DZ[c, layer, rows, :] = first(*taps)
            if out is not None:
                DZZ[c, out[0], out[1], :] = second(taps[0], taps[1], tile, taps[2], taps[3])

    for copy in geo_zs:
        copy.wait_recv()

    def z_own(i, _):
        x, b = i // BLOCKS, lax.rem(i, BLOCKS)
        z_geo(
            x + 2, x // 2 + 1, lax.rem(x, 2), pl.ds(pl.multiple_of(OWN + 8 * b, 8), 8), 0, b,
            (x, pl.ds(pl.multiple_of(8 * b, 8), 8)),
        )
        return 0

    lax.fori_loop(0, CX * BLOCKS, z_own, 0)
    for copy in rest_zs + rest_ys:
        copy.start()

    for copy in geo_ys + edge_yz:
        copy.wait_recv()

    def open_y_geo(p, _):
        for c in range(GEO):
            for xi in range(2):
                rows = slice(c * 4 + xi * 2, c * 4 + xi * 2 + 2)
                F[c, 2 + 2 * p + xi, OWN - 2 : OWN, :] = YRG[0, p, rows, :]
                F[c, 2 + 2 * p + xi, OWN + CY : OWN + CY + 2, :] = YRG[1, p, rows, :]
        return 0

    lax.fori_loop(0, PAIRS, open_y_geo, 0)

    def z_rows(x, _):
        z_geo(x + 2, x // 2 + 1, lax.rem(x, 2), slice(0, 8), 1, BLOCKS - 1, None)
        z_geo(x + 2, x // 2 + 1, lax.rem(x, 2), slice(OWN + CY, OWN + CY + 8), 2, 0, None)
        return 0

    lax.fori_loop(0, CX, z_rows, 0)

    for copy in rest_zs + rest_ys:
        copy.wait_recv()

    def open_y_rest(x, _):
        rows = pl.ds(2 * x, 2)
        for n, c in enumerate(Y_REST):
            R[c, 2 + x, OWN - 2 : OWN, :] = YRR[0, n, rows, :]
            R[c, 2 + x, OWN + CY : OWN + CY + 2, :] = YRR[1, n, rows, :]
        return 0

    lax.fori_loop(0, CX, open_y_rest, 0)

    def x_layer(x):
        def body(b, _):
            rows = pl.ds(pl.multiple_of(8 * b, 8), 8)
            for c in range(GEO):
                taps = [F[c, x + k, rows, :] for k in range(5)]
                DX[c, x, rows, :] = first(taps[0], taps[1], taps[3], taps[4])
                DXX[c, x, rows, :] = second(*taps)
            return 0

        lax.fori_loop(0, ROWS // 8, body, 0)

    def cell(x, b):
        r0 = OWN + 8 * b
        mid = pl.ds(pl.multiple_of(r0, 8), 8)
        own = pl.ds(pl.multiple_of(8 * b, 8), 8)

        def y_of(ref, c, layer):
            return [ref[c, layer, pl.ds(r0 + k, 8), :] for k in (-2, -1, 1, 2)]

        def x_of(ref, c):
            return [ref[c, x + 2 + k, mid, :] for k in (-2, -1, 1, 2)]

        g = [F[1 + n, x + 2, mid, :] for n in range(6)]
        chi = F[0, x + 2, mid, :]
        gu = inverse_of(g)
        wide = [gu[0], 2.0 * gu[1], 2.0 * gu[2], gu[3], 2.0 * gu[4], gu[5]]
        same = [12.0 * gu[0], 12.0 * gu[3], 12.0 * gu[5]]

        grads, bend = [[], [], []], []
        for c in range(GEO):
            f = F[c, x + 2, mid, :]
            ys = y_of(F, c, x + 2)
            grads[0].append(DX[c, x, mid, :])
            grads[1].append(first(*ys))
            grads[2].append(DZ[c, x + 2, mid, :])
            bend.append(
                same[0] * DXX[c, x, mid, :]
                + same[1] * second(ys[0], ys[1], f, ys[2], ys[3])
                + same[2] * DZZ[c, x, own, :]
                + wide[1] * first(*y_of(DX, c, x))
                + wide[2] * first(*x_of(DZ, c))
                + wide[4] * first(*y_of(DZ, c, x + 2))
            )
        dchi = [grads[a][0] for a in range(3)]
        bend_g = sum(wide[n] * bend[1 + n] for n in range(1, 6)) + wide[0] * bend[1]

        def d(a, i, j):
            return grads[a][1 + PAIR[i][j]]

        def inv(i, j):
            return gu[PAIR[i][j]]

        trace, low = [], []
        for a in range(3):
            t = wide[0] * grads[a][1]
            for n in range(1, 6):
                t = t + wide[n] * grads[a][1 + n]
            trace.append(t)
            e = gu[0] * d(0, 0, a) + gu[3] * d(1, 1, a) + gu[5] * d(2, 2, a)
            e = e + gu[1] * (d(0, 1, a) + d(1, 0, a)) + gu[2] * (d(0, 2, a) + d(2, 0, a))
            e = e + gu[4] * (d(1, 2, a) + d(2, 1, a))
            low.append(e - 0.5 * t)
        gd = [inv(k, 0) * low[0] + inv(k, 1) * low[1] + inv(k, 2) * low[2] for k in range(3)]

        cyc = {
            (0, 0, 0): 3.0 * d(0, 0, 0), (1, 1, 1): 3.0 * d(1, 1, 1), (2, 2, 2): 3.0 * d(2, 2, 2),
            (0, 0, 1): 2.0 * d(0, 0, 1) + d(1, 0, 0), (0, 0, 2): 2.0 * d(0, 0, 2) + d(2, 0, 0),
            (0, 1, 1): 2.0 * d(1, 0, 1) + d(0, 1, 1), (1, 1, 2): 2.0 * d(1, 1, 2) + d(2, 1, 1),
            (0, 2, 2): 2.0 * d(2, 0, 2) + d(0, 2, 2), (1, 2, 2): 2.0 * d(2, 1, 2) + d(1, 2, 2),
            (0, 1, 2): d(0, 1, 2) + d(1, 0, 2) + d(2, 0, 1),
        }

        def s(*idx):
            return cyc[tuple(sorted(idx))]

        up = [[[None] * 3 for _ in range(3)] for _ in range(3)]
        for i in range(3):
            for l in range(3):
                for j in range(l, 3):
                    value = inv(i, 0) * s(0, l, j) + inv(i, 1) * s(1, l, j) + inv(i, 2) * s(2, l, j)
                    up[l][i][j] = value
                    up[j][i][l] = value
        squares = None
        for l in range(3):
            for m in range(l, 3):
                if l == m:
                    diag = up[l][0][0] * up[l][0][0] + up[l][1][1] * up[l][1][1] + up[l][2][2] * up[l][2][2]
                    off = up[l][0][1] * up[l][1][0] + up[l][0][2] * up[l][2][0] + up[l][1][2] * up[l][2][1]
                    trc = diag + 2.0 * off
                else:
                    trc = sum(up[l][i][j] * up[m][j][i] for i in range(3) for j in range(3) if i + j) + (
                        up[l][0][0] * up[m][0][0]
                    )
                term = wide[PAIR[l][m]] * trc
                squares = term if squares is None else squares + term

        t0 = lax.rem(x, 2) * BLOCKS + b
        left, right = ZRR[0, x // 2], ZRR[1, x // 2]
        rest_grad = [[], [], []]
        for n in range(7):
            tile = R[n, x + 2, mid, :]
            rest_grad[0].append(first(*x_of(R, n)))
            rest_grad[1].append(first(*y_of(R, n, x + 2)))
            rest_grad[2].append(first(*z_taps(tile, left, right, 2 * n * BLOCKS + t0)))
        div = first(*x_of(R, 7)) + first(*y_of(R, 8, x + 2))
        div = div + first(*z_taps(R[9, x + 2, mid, :], left, right, 14 * BLOCKS + t0))
        A = [R[n, x + 2, mid, :] for n in range(6)]
        K = R[6, x + 2, mid, :]

        mixed = [
            [A[PAIR[i][0]] * inv(0, j) + A[PAIR[i][1]] * inv(1, j) + A[PAIR[i][2]] * inv(2, j) for j in range(3)]
            for i in range(3)
        ]
        raised = [
            inv(i, 0) * mixed[0][j] + inv(i, 1) * mixed[1][j] + inv(i, 2) * mixed[2][j]
            for i, j in ((0, 0), (0, 1), (0, 2), (1, 1), (1, 2), (2, 2))
        ]
        a_sq = mixed[0][0] * mixed[0][0] + mixed[1][1] * mixed[1][1] + mixed[2][2] * mixed[2][2]
        a_sq = a_sq + 2.0 * (
            mixed[0][1] * mixed[1][0] + mixed[0][2] * mixed[2][0] + mixed[1][2] * mixed[2][1]
        )
        chi_inv = 1.0 / chi
        dchi_up = [inv(k, 0) * dchi[0] + inv(k, 1) * dchi[1] + inv(k, 2) * dchi[2] for k in range(3)]
        grad_sq = dchi_up[0] * dchi[0] + dchi_up[1] * dchi[1] + dchi_up[2] * dchi[2]
        gd_trace = gd[0] * trace[0] + gd[1] * trace[1] + gd[2] * trace[2]
        gd_chi = gd[0] * dchi[0] + gd[1] * dchi[1] + gd[2] * dchi[2]
        ricci = 0.5 * (gd_trace - bend_g) + squares * (1.0 / 12.0) + 12.0 * div
        ham = (chi * ricci + 2.0 * (bend[0] - gd_chi) - 2.5 * grad_sq * chi_inv) * (1.0 / 144.0)
        OUT[0, x, own, :] = ham + (2.0 / 3.0) * (K * K) - a_sq

        weight = 1.5 * chi_inv
        vec = [gd[l] + weight * dchi_up[l] for l in range(3)]
        twice = [0.5 * raised[0], raised[1], raised[2], 0.5 * raised[3], raised[4], 0.5 * raised[5]]
        for i in range(3):
            total = (-2.0 / 3.0) * rest_grad[i][6]
            for j in range(3):
                for k in range(3):
                    total = total + inv(j, k) * rest_grad[j][PAIR[k][i]]
            for l in range(3):
                total = total - vec[l] * A[PAIR[l][i]]
            for n in range(6):
                total = total - twice[n] * grads[i][1 + n]
            OUT[1 + i, x, own, :] = total * (1.0 / 12.0)

    def tally(x, b):
        own = pl.ds(pl.multiple_of(8 * b, 8), 8)
        ham, m0, m1, m2 = [OUT[n, x, own, :] for n in range(4)]
        ACC[0] += ham * ham
        ACC[1] += m0 * m0 + m1 * m1 + m2 * m2

    def term(d, b):
        rows = pl.ds(8 * b, 8)
        return remote(CS.at[d, :, :, rows], CR.at[1 - d, :, :, rows], S_TERM + 4 * d + b, at(2 * d - 1, 0, 0))

    terms = [[term(d, b) for b in range(BLOCKS)] for d in range(2)]

    def send_terms(b):
        mid = pl.ds(OWN + 8 * b, 8)
        for d in range(2):
            geo_xs[d][b].wait_recv()
        for d in range(2):
            halo = CX + 2 if d else 0
            for k in range(2):
                gu = inverse_of([F[1 + n, halo + k, mid, :] for n in range(6)])
                chi = F[0, halo + k, mid, :]

                def part(n):
                    if d == 0:
                        f0 = R[n, 2, mid, :]
                        return -f0 if k == 0 else 8.0 * f0 - R[n, 3, mid, :]
                    f7 = R[n, CX + 1, mid, :]
                    return R[n, CX, mid, :] - 8.0 * f7 if k == 0 else f7

                a = [part(n) for n in range(8)]
                own = pl.ds(8 * b, 8)
                CS[d, 0, k, own, :] = chi * a[7] * (1.0 / 12.0)
                for i in range(3):
                    value = gu[0] * a[PAIR[0][i]] + gu[1] * a[PAIR[1][i]] + gu[2] * a[PAIR[2][i]]
                    if i == 0:
                        value = value - (2.0 / 3.0) * a[6]
                    CS[d, 1 + i, k, own, :] = value * (1.0 / 12.0)
        for d in range(2):
            terms[d][b].start()

    def inner(x):
        x_layer(x)

        def body(b, _):
            cell(x, b)
            tally(x, b)
            return 0

        lax.fori_loop(0, BLOCKS, body, 0)

    def inner_layer(x, _):
        inner(x)
        return 0

    for b in range(BLOCKS):
        send_terms(b)
        lax.fori_loop(2 + b, 3 + b, inner_layer, 0)

    for copy in edge_xy + edge_xz:
        copy.wait_recv()
    for xs in range(2):
        for ys in range(2):
            for c in range(GEO):
                for k in range(2):
                    layer = (CX + 2 if xs else 0) + k
                    row = OWN + CY if ys else OWN - 2
                    F[c, layer, row : row + 2, :] = XYR[xs, ys, c * 4 + k * 2 : c * 4 + k * 2 + 2, :]

    def z_edge(i, _):
        k, b = i // BLOCKS, lax.rem(i, BLOCKS)
        side, xi = k // 2, lax.rem(k, 2)
        z_geo(
            side * (CX + 2) + xi, side * (PAIRS + 1), xi, pl.ds(pl.multiple_of(OWN + 8 * b, 8), 8), 0, b, None
        )
        return 0

    lax.fori_loop(0, 4 * BLOCKS, z_edge, 0)

    def edge_layer(k, _):
        x = k + (k // 2) * (CX - 4)
        x_layer(x)

        def body(b, _):
            cell(x, b)
            return 0

        lax.fori_loop(0, BLOCKS, body, 0)
        return 0

    lax.fori_loop(0, 4, edge_layer, 0)

    for d in range(2):
        for b in range(BLOCKS):
            terms[d][b].wait_recv()

    def finish(k, _):
        side, sub = k // 2, lax.rem(k, 2)
        x = k + side * (CX - 4)
        for n in range(4):
            OUT[n, x] = OUT[n, x] + CR[side, n, sub]
        for b in range(BLOCKS):
            tally(x, b)
        return 0

    lax.fori_loop(0, 4, finish, 0)
    stores = [
        pltpu.make_async_copy(OUT.at[0], ham_out, out_sem.at[0]),
        pltpu.make_async_copy(OUT.at[1:4], mom_out, out_sem.at[1]),
    ]
    for copy in stores:
        copy.start()

    MINE[0, 0:1, :] = jnp.sum(ACC[0], axis=0, keepdims=True)
    MINE[0, 1:2, :] = jnp.sum(ACC[1], axis=0, keepdims=True)
    SUM_A[rank_a] = MINE[0]

    def plane_copy(j):
        rank, peer = plane_peer(j)
        return pltpu.make_async_remote_copy(
            src_ref=MINE.at[0], dst_ref=SUM_A.at[rank_a], send_sem=send_sem.at[S_SUM_A + rank],
            recv_sem=recv_sem.at[S_SUM_A + rank_a], device_id=peer, device_id_type=MESH,
        )

    def plane_start(j, _):
        plane_copy(j).start()
        return 0

    def plane_wait(j, _):
        rank, peer = plane_peer(j)
        pltpu.make_async_remote_copy(
            src_ref=MINE.at[0], dst_ref=SUM_A.at[rank], send_sem=send_sem.at[S_SUM_A + rank],
            recv_sem=recv_sem.at[S_SUM_A + rank], device_id=peer, device_id_type=MESH,
        ).wait()
        return 0

    lax.fori_loop(1, n_plane, plane_start, 0)
    lax.fori_loop(1, n_plane, plane_wait, 0)
    MINE[1] = lax.fori_loop(1, n_plane, lambda j, acc: acc + SUM_A[j], SUM_A[0])
    SUM_B[ix] = MINE[1]

    def line_copy(j, receiving):
        rank = lax.rem(ix + j, n_gx)
        slot = rank if receiving else ix
        return pltpu.make_async_remote_copy(
            src_ref=MINE.at[1], dst_ref=SUM_B.at[slot], send_sem=send_sem.at[S_SUM_B + rank],
            recv_sem=recv_sem.at[S_SUM_B + slot], device_id=(rank, iy, iz), device_id_type=MESH,
        )

    for j in range(1, n_gx):
        line_copy(j, False).start()
    for j in range(1, n_gx):
        line_copy(j, True).wait()
    total = SUM_B[0]
    for j in range(1, n_gx):
        total = total + SUM_B[j]
    sums = jnp.sum(total, axis=1, keepdims=True)
    cells = float(CX * CY * CZ * n_gx * n_gy * n_gz)
    column = lax.broadcasted_iota(jnp.int32, (1, 2), 1)
    ham_sum = jnp.broadcast_to(sums[0:1], (1, 2))
    mom_sum = jnp.broadcast_to(sums[1:2], (1, 2))
    norm_out[...] = jnp.sqrt(jnp.where(column == 0, ham_sum / cells, mom_sum / (3.0 * cells)))

    for copy in [c for row in geo_xs + terms for c in row] + geo_ys + geo_zs + edge_xy + edge_yz + edge_xz:
        copy.wait_send()
    for copy in rest_ys + rest_zs:
        copy.wait_send()
    for copy in stores:
        copy.wait()


def solution(mesh):
    sizes = (mesh.shape["gx"], mesh.shape["gy"], mesh.shape["gz"])
    n_plane = sizes[1] * sizes[2]
    f32 = jnp.float32

    def step(chi, met, cur, trk, gam):
        vm = lambda *shape: pltpu.VMEM(shape, f32)
        ham, mom, norm = pl.pallas_call(
            functools.partial(kernel, sizes),
            out_shape=(
                jax.ShapeDtypeStruct((CX, CY, CZ), f32),
                jax.ShapeDtypeStruct((3, CX, CY, CZ), f32),
                jax.ShapeDtypeStruct((1, 2), f32),
            ),
            in_specs=[pl.BlockSpec(memory_space=pl.ANY)] * 5,
            out_specs=(
                pl.BlockSpec(memory_space=pl.ANY),
                pl.BlockSpec(memory_space=pl.ANY),
                pl.BlockSpec(memory_space=pltpu.VMEM),
            ),
            scratch_shapes=[
                vm(GEO, LX, ROWS, CZ), vm(REST, LX, ROWS, CZ),
                vm(GEO, LX, ROWS, CZ), vm(GEO, CX, CY, CZ),
                vm(GEO, CX, ROWS, CZ), vm(GEO, CX, ROWS, CZ),
                vm(4, CX, CY, CZ), vm(2, 8, CZ),
                vm(2, PAIRS, 32, CZ), vm(2, 8, 2 * CX, CZ),
                vm(2, PAIRS, 32, CZ), vm(2, 8, 2 * CX, CZ),
                vm(2, 2, 32, CZ),
                vm(2, PAIRS, 8, CZ), vm(2, PAIRS, 8, CZ),
                vm(2, 3, PAIRS + 2, 8, CZ), vm(2, PAIRS, 8, CZ),
                vm(2, 4, 2, CY, CZ), vm(2, 4, 2, CY, CZ),
                vm(2, 2, CZ), vm(n_plane, 2, CZ), vm(sizes[0], 2, CZ),
                pltpu.SemaphoreType.DMA((5,)),
                pltpu.SemaphoreType.DMA((2,)),
                pltpu.SemaphoreType.DMA((S_COUNT,)),
                pltpu.SemaphoreType.DMA((S_COUNT,)),
            ],
            compiler_params=pltpu.CompilerParams(collective_id=0, has_side_effects=True),
        )(chi, met, cur, trk, gam)
        return ham, mom, norm.reshape(2)

    return jax.shard_map(
        step,
        mesh=mesh,
        in_specs=(
            P("gx", "gy", "gz"),
            P(None, "gx", "gy", "gz"),
            P(None, "gx", "gy", "gz"),
            P("gx", "gy", "gz"),
            P(None, "gx", "gy", "gz"),
        ),
        out_specs=(P("gx", "gy", "gz"), P(None, "gx", "gy", "gz"), P()),
        check_vma=False,
    )
```

time: 150 us -> 50.9 us (0.34)
  other arithmetic: 57.8 us -> 0 us
  Pallas kernels: 0 us -> 46.3 us
  blocking collectives: 38.4 us -> 0 us
  local copies, waits for them, and re-layouts: 31.4 us -> 3.85 us
  starting transfers between devices: 20.1 us -> 0 us
    pallas_call x0 -> x1, Pallas kernels: none -> 46.3 us  [step(): pl.pallas_call(functools.partial(kernel, sizes), out_shape=(jax.ShapeDtyp...]
    psum x4 -> x0, blocking collectives: 38.4 us -> none  [over_axes(): return functools.reduce(lax.psum, axes, x)]
    concatenate x9 -> x0, other arithmetic: 21.5 us -> none  [the longest x3 9.96 us: with_halo(): jnp.concatenate([jnp.pad(low, around), x, jnp.pad(high, around)], axis=dim)]
    add x8 -> x0, other arithmetic: 20.2 us -> none  [the longest x5 10.8 us: first_diff(): summed = term if summed is None else summed + term]
    ppermute x12 -> x0, starting transfers between devices: 20.1 us -> none  [the longest x3 6.71 us: padded_2(): lax.ppermute(head, axis, [((i + 1) % count, i) for i in range(count)])]
    unnamed x62 -> x5, local copies, waits for them, and re-layouts: 20.6 us -> 3.85 us
    reduce_sum x2 -> x0, other arithmetic: 10.4 us -> none  [the longest x1 9 us: on_device(): jnp.sum(hamilton * hamilton)]
    ppermute x2 -> x0, local copies, waits for them, and re-layouts: 5.63 us -> none  [the longest x1 2.85 us: padded_2(): lax.ppermute(tail, axis, [(i, (i + 1) % count) for i in range(count)])]
  transfers between devices with their start and end apart: 12 -> 0, of which waited for: 0 -> 0; matrix products, arithmetic and copies ran while one was open for 35% -> 0% of each run, Pallas kernels for 0% -> 0%
where the time goes in v1:
time: 50.9 us; the launch traced here: 50.8 us
  Pallas kernels  46.3 us (91%)
  local copies, waits for them, and re-layouts  3.85 us (8%)
  between operations  0.64 us (1%)
    pallas_call x1, Pallas kernels, step(): pl.pallas_call(functools.partial(kernel, sizes), out_shape=(jax.ShapeDtyp...  46.3 us
    unnamed x5, local copies, waits for them, and re-layouts  3.85 us

profile of v1, /device:TPU:1, one launch (start us, length us, event | category | flops | bytes accessed | tf_op | source)
XLA Modules:
  0.0 50.8 jit_solution(8225963338137780551)
XLA Ops:
  0.6 46.3 %shard_map.76 = (f32[8,32,128]{2,1,0:T(8,128)}, f32[3,8,32,128]{3,2,1,0:T(8,128)}, f32[1,2]{1,0:T(1,128)}) custom-call(f32[8,32,128]{2,1,0:T(8,128)} %chi_in.1, f32[6,8,32,128]{3,2,1,0:T(8,128)} %met_in.1, f32[6,8,32,128]{3,2,1,0:T(8,128)} %cur_in.1, f32[8,32,128]{2,1,0:T(8,128)} %trk_in.1, f32[3,8,32,128]{3,2,1,0:T(8,128)} %gam_in.1), custom_call_target="tpu_custom_call" | custom-call | tf_op jit(solution)/shard_map/pallas_call | solution.py:601
  46.9 1.6 %copy.11 = f32[8,32,128]{2,1,0:T(8,128)} copy(f32[8,32,128]{2,1,0:T(8,128)} %get-tuple-element.12) | data formatting | bytes 262144
  48.5 0.0 copy-start
  48.5 1.8 %copy.12 = f32[3,8,32,128]{3,2,1,0:T(8,128)} copy(f32[3,8,32,128]{3,2,1,0:T(8,128)} %get-tuple-element.13) | data formatting | bytes 786432
  50.2 0.0 copy-done
  50.2 0.5 %copy.13 = f32[2]{0:T(128)} copy(f32[2]{0:T(128)S(1)} %bitcast.1) | data formatting | bytes 16
Async XLA Ops:
  48.5 1.8 %copy-start = (f32[1,2]{1,0:T(1,128)S(1)}, f32[1,2]{1,0:T(1,128)}, u32[]{:S(2)}) copy-start(f32[1,2]{1,0:T(1,128)} %get-tuple-element.8) | copy-start | bytes 28

commit v2 on v1

v2 whole, which is shorter than its diff:
```python
import functools

import jax
import jax.numpy as jnp
from jax import lax
from jax.experimental import pallas as pl
from jax.experimental.pallas import tpu as pltpu
from jax.sharding import PartitionSpec as P

MESH = pl.DeviceIdType.MESH
PAIR = ((0, 1, 2), (1, 3, 4), (2, 4, 5))

CX, CY, CZ = 8, 32, 128
LX, ROWS, OWN = CX + 4, 48, 8
BLOCKS = CY // 8
PAIRS = CX // 2
GEO, REST = 7, 10
Y_REST = (0, 1, 2, 3, 4, 5, 6, 8)
Z_REST = (0, 1, 2, 3, 4, 5, 6, 9)
X_REST = 8

S_GEO_X, S_EDGE_XY, S_EDGE_YZ, S_EDGE_XZ = 0, 8, 12, 16
S_GEO_Y, S_GEO_Z, S_REST_Y, S_REST_Z, S_TERM, S_ENDS_X = 20, 22, 24, 26, 28, 36
S_SUM_A, S_SUM_B, S_COUNT = 38, 39, 40


def lane_ids():
    return lax.broadcasted_iota(jnp.int32, (8, CZ), 1)


def inverse_of(g):
    g00, g01, g02, g11, g12, g22 = g
    m00 = g11 * g22 - g12 * g12
    m01 = g02 * g12 - g01 * g22
    m02 = g01 * g12 - g02 * g11
    m11 = g00 * g22 - g02 * g02
    m12 = g01 * g02 - g00 * g12
    m22 = g00 * g11 - g01 * g01
    scale = 1.0 / (g00 * m00 + g01 * m01 + g02 * m02)
    return [m00 * scale, m01 * scale, m02 * scale, m11 * scale, m12 * scale, m22 * scale]


def first(lo2, lo1, hi1, hi2):
    return (lo2 - hi2) + 8.0 * (hi1 - lo1)


def second(lo2, lo1, mid, hi1, hi2):
    return 16.0 * (lo1 + hi1) - (lo2 + hi2) - 30.0 * mid


def kernel(
    sizes,
    chi_in, met_in, cur_in, trk_in, gam_in,
    ham_out, mom_out, norm_out,
    F, R, DZ, DZZ, DZR, DX, DXX, ACC,
    YSG, YSR, YRG, YRR, YDZ, YZR, XYR,
    ZP, ZPR, C1, C2, XE, XER, CXE,
    CS, CR, MINE, SUM_A, SUM_B,
    load_sem, send_sem, recv_sem, near_sem, far_sem,
):
    n_gx, n_gy, n_gz = sizes
    ix, iy, iz = lax.axis_index("gx"), lax.axis_index("gy"), lax.axis_index("gz")
    xs = {k: lax.rem(ix + k + n_gx, n_gx) for k in range(-2, n_gx)}
    ys = {k: lax.rem(iy + k + n_gy, n_gy) for k in range(-1, n_gy)}
    zs = {k: lax.rem(iz + k + n_gz, n_gz) for k in range(-2, n_gz)}

    def at(dx, dy, dz):
        return xs[dx], ys[dy], zs[dz]

    def remote(src, dst, place, device):
        return pltpu.make_async_remote_copy(
            src_ref=src, dst_ref=dst, send_sem=send_sem.at[place], recv_sem=recv_sem.at[place],
            device_id=device, device_id_type=MESH,
        )

    loads = [
        (chi_in, F.at[0, 2 : 2 + CX, OWN : OWN + CY]),
        (met_in, F.at[1:7, 2 : 2 + CX, OWN : OWN + CY]),
        (cur_in, R.at[0:6, 2 : 2 + CX, OWN : OWN + CY]),
        (trk_in, R.at[6, 2 : 2 + CX, OWN : OWN + CY]),
        (gam_in, R.at[7:10, 2 : 2 + CX, OWN : OWN + CY]),
    ]
    loads = [pltpu.make_async_copy(s, d, load_sem.at[i]) for i, (s, d) in enumerate(loads)]
    for copy in loads:
        copy.start()

    barrier = pltpu.get_barrier_semaphore()
    faces = [(-1, 0, 0), (1, 0, 0), (0, -1, 0), (0, 1, 0), (0, 0, -1), (0, 0, 1)]
    for step in faces:
        pl.semaphore_signal(barrier, inc=1, device_id=at(*step), device_id_type=MESH)

    lane = lane_ids()
    lane4, place = lane // 4, lax.rem(lane, 4)
    ends = (lane < 2) | (lane >= CZ - 2)
    zero = jnp.zeros((8, CZ), jnp.float32)

    def clear(c, _):
        for layer in (0, 1, LX - 2, LX - 1):
            for b in range(BLOCKS):
                R[c, layer, pl.ds(OWN + 8 * b, 8), :] = zero
        return 0

    lax.fori_loop(0, X_REST, clear, 0)
    ACC[...] = jnp.zeros_like(ACC)

    def packed(tiles):
        out = zero
        for t, tile in enumerate(tiles):
            turn = (4 * t + 2) % CZ
            out = jnp.where(lane4 == t, pltpu.roll(tile, turn, 1) if turn else tile, out)
        return out

    def pack_geo(c, _):
        ZP[c] = packed([F[c, 2 + x, pl.ds(OWN + 8 * b, 8), :] for x in range(CX) for b in range(BLOCKS)])
        return 0

    def pack_rest(n, _):
        c = n + (n // 7) * 2
        ZP[GEO + n] = packed([R[c, 2 + x, pl.ds(OWN + 8 * b, 8), :] for x in range(CX) for b in range(BLOCKS)])
        return 0

    def pack_y_geo(p, _):
        for c in range(GEO):
            for xi in range(2):
                rows = pl.ds(32 * p + c * 4 + xi * 2, 2)
                YSG[0, rows, :] = F[c, 2 + 2 * p + xi, OWN : OWN + 2, :]
                YSG[1, rows, :] = F[c, 2 + 2 * p + xi, OWN + CY - 2 : OWN + CY, :]
        return 0

    def pack_y_rest(x, _):
        rows = pl.ds(2 * x, 2)
        for n, c in enumerate(Y_REST):
            YSR[0, n, rows, :] = R[c, 2 + x, OWN : OWN + 2, :]
            YSR[1, n, rows, :] = R[c, 2 + x, OWN + CY - 2 : OWN + CY, :]
        return 0

    for s in range(2):
        for p in range(PAIRS):
            YSG[s, 32 * p + 24 : 32 * p + 32, :] = zero
    loads[0].wait()
    loads[1].wait()
    lax.fori_loop(0, PAIRS, pack_y_geo, 0)
    lax.fori_loop(0, GEO, pack_geo, 0)
    for s in range(2):
        YSG[s, 128:136, :] = packed([YSG[s, 8 * k : 8 * k + 8, :] for k in range(16)])
        for v in range(2):
            out = zero
            for c in range(4 * v, min(4 * v + 4, GEO)):
                turn = (32 * (c % 4) - 96 * s) % CZ
                out = jnp.where(lane // 32 == c % 4, pltpu.roll(ZP[c], turn, 1) if turn else ZP[c], out)
            XE[s, v] = out
    for copy in loads[2:]:
        copy.wait()
    lax.fori_loop(0, CX, pack_y_rest, 0)
    lax.fori_loop(0, 8, pack_rest, 0)

    def geo_x(d, b):
        rows = pl.ds(OWN + 8 * b, 8)
        src = F.at[0:GEO, pl.ds(CX if d else 2, 2), rows]
        dst = F.at[0:GEO, pl.ds(0 if d else CX + 2, 2), rows]
        return remote(src, dst, S_GEO_X + 4 * d + b, at(2 * d - 1, 0, 0))

    geo_xs = [[geo_x(d, b) for b in range(BLOCKS)] for d in range(2)]
    ends_x = [remote(XE.at[d], XER.at[1 - d, 0], S_ENDS_X + d, at(2 * d - 1, 0, 0)) for d in range(2)]
    geo_ys = [remote(YSG.at[d], YRG.at[1 - d], S_GEO_Y + d, at(0, 2 * d - 1, 0)) for d in range(2)]
    geo_zs = [remote(ZP.at[0:GEO], ZPR.at[1 - d, 0:GEO], S_GEO_Z + d, at(0, 0, 2 * d - 1)) for d in range(2)]
    rest_ys = [remote(YSR.at[d], YRR.at[1 - d], S_REST_Y + d, at(0, 2 * d - 1, 0)) for d in range(2)]
    rest_zs = [
        remote(ZP.at[GEO : GEO + 8], ZPR.at[1 - d, GEO : GEO + 8], S_REST_Z + d, at(0, 0, 2 * d - 1)) for d in range(2)
    ]
    combos = [(a, b) for a in range(2) for b in range(2)]
    edge_xy = [
        remote(
            YSG.at[dy, pl.ds(96 if dx else 0, 32)], XYR.at[1 - dx, 1 - dy], S_EDGE_XY + 2 * dx + dy,
            at(2 * dx - 1, 2 * dy - 1, 0),
        )
        for dx, dy in combos
    ]
    edge_yz = [
        remote(
            YSG.at[dy, 128:136], YZR.at[1 - dz, 1 - dy], S_EDGE_YZ + 2 * dy + dz, at(0, 2 * dy - 1, 2 * dz - 1)
        )
        for dy, dz in combos
    ]
    edge_xz = [
        remote(XE.at[dx], XER.at[1 - dx, 2 - dz], S_EDGE_XZ + 2 * dx + dz, at(2 * dx - 1, 0, 2 * dz - 1))
        for dx, dz in combos
    ]

    pl.semaphore_wait(barrier, len(faces))
    for copy in geo_xs[0][:1] + geo_xs[1][:1] + geo_zs + geo_ys + rest_zs + rest_ys:
        copy.start()
    for b in range(1, BLOCKS):
        for d in range(2):
            geo_xs[d][b].start()
    for copy in ends_x:
        copy.start()

    def wrapped(tile):
        return (
            pltpu.roll(tile, 2, 1), pltpu.roll(tile, 1, 1), pltpu.roll(tile, CZ - 1, 1), pltpu.roll(tile, CZ - 2, 1)
        )

    def z_geo(x, _):
        for c in range(GEO):
            for b in range(BLOCKS):
                rows = pl.ds(OWN + 8 * b, 8)
                tile = F[c, x + 2, rows, :]
                taps = wrapped(tile)
                DZ[c, x + 2, rows, :] = first(*taps)
                DZZ[c, x, pl.ds(8 * b, 8), :] = second(taps[0], taps[1], tile, taps[2], taps[3])
        return 0

    def z_rest(x, _):
        for n, c in enumerate(Z_REST):
            for b in range(BLOCKS):
                DZR[n, x, pl.ds(8 * b, 8), :] = first(*wrapped(R[c, x + 2, pl.ds(OWN + 8 * b, 8), :]))
        return 0

    def x_rows(layers, tiles):
        def body(i, _):
            x, b = layers(i // len(tiles)), lax.rem(i, len(tiles))
            b = tiles[0] + b * (tiles[1] - tiles[0])
            rows = pl.ds(pl.multiple_of(8 * b, 8), 8)
            for c in range(GEO):
                taps = [F[c, x + k, rows, :] for k in range(5)]
                DX[c, x, rows, :] = first(taps[0], taps[1], taps[3], taps[4])
                DXX[c, x, rows, :] = second(*taps)
            return 0

        lax.fori_loop(0, 4 * len(tiles), body, 0)

    lax.fori_loop(0, CX, z_geo, 0)
    for copy in geo_zs:
        copy.wait_recv()
    for copy in edge_yz + edge_xz:
        copy.start()

    def change(own, left, right):
        e = jnp.where(place < 2, left, right) - own
        hi2, hi1, lo1, lo2 = (pltpu.roll(e, k, 1) for k in (CZ - 2, CZ - 1, 1, 2))
        hi1 = jnp.where(place == 1, hi1, 0.0)
        lo1 = jnp.where(place == 2, lo1, 0.0)
        return (
            jnp.where(place < 2, 8.0 * hi1 - hi2, lo2 - 8.0 * lo1),
            16.0 * (hi1 + lo1) - jnp.where(place < 2, hi2, lo2),
        )

    def at_ends(change, turn):
        return jnp.where(ends, pltpu.roll(change, turn, 1), 0.0)

    for c in range(GEO):
        C1[c], C2[c] = change(ZP[c], ZPR[0, c], ZPR[1, c])

    def z_ends(x, _):
        for c in range(GEO):
            changed = C1[c]
            for b in range(BLOCKS):
                rows = pl.ds(OWN + 8 * b, 8)
                DZ[c, x + 2, rows, :] += at_ends(changed, CZ - 2 - 4 * (BLOCKS * x + b))
        return 0

    lax.fori_loop(0, CX, z_ends, 0)
    x_rows(lambda k: k + 2, (1, 2, 3, 4))
    lax.fori_loop(0, CX, z_rest, 0)
    for copy in rest_zs + rest_ys:
        copy.wait_recv()
    for n in range(8):
        C1[GEO + n] = change(ZP[GEO + n], ZPR[0, GEO + n], ZPR[1, GEO + n])[0]

    def open_y_rest(x, _):
        rows = pl.ds(2 * x, 2)
        for n, c in enumerate(Y_REST):
            R[c, 2 + x, OWN - 2 : OWN, :] = YRR[0, n, rows, :]
            R[c, 2 + x, OWN + CY : OWN + CY + 2, :] = YRR[1, n, rows, :]
        return 0

    lax.fori_loop(0, CX, open_y_rest, 0)
    for copy in geo_ys:
        copy.wait_recv()
    for copy in edge_xy:
        copy.start()

    def open_y_geo(p, _):
        for c in range(GEO):
            for xi in range(2):
                rows = pl.ds(32 * p + c * 4 + xi * 2, 2)
                F[c, 2 + 2 * p + xi, OWN - 2 : OWN, :] = YRG[0, rows, :]
                F[c, 2 + 2 * p + xi, OWN + CY : OWN + CY + 2, :] = YRG[1, rows, :]
        return 0

    lax.fori_loop(0, PAIRS, open_y_geo, 0)
    x_rows(lambda k: k + 2, (0, 5))

    def y_ends(s, _):
        changed = change(YRG[s, 128:136, :], YZR[0, s], YZR[1, s])[0]
        for k in range(16):
            rows = slice(8 * k, 8 * k + 8)
            YDZ[s, rows, :] = first(*wrapped(YRG[s, rows, :])) + at_ends(changed, CZ - 2 - 4 * k)
        return 0

    def open_y_dz(p, _):
        for c in range(GEO):
            for xi in range(2):
                rows = pl.ds(32 * p + c * 4 + xi * 2, 2)
                DZ[c, 2 + 2 * p + xi, OWN - 2 : OWN, :] = YDZ[0, rows, :]
                DZ[c, 2 + 2 * p + xi, OWN + CY : OWN + CY + 2, :] = YDZ[1, rows, :]
        return 0

    def cell(x, b):
        r0 = OWN + 8 * b
        mid = pl.ds(pl.multiple_of(r0, 8), 8)
        own = pl.ds(pl.multiple_of(8 * b, 8), 8)
        turn = CZ - 2 - 4 * (BLOCKS * x + b)

        def y_of(ref, c, layer):
            return [ref[c, layer, pl.ds(r0 + k, 8), :] for k in (-2, -1, 1, 2)]

        def x_of(ref, c):
            return [ref[c, x + 2 + k, mid, :] for k in (-2, -1, 1, 2)]

        g = [F[1 + n, x + 2, mid, :] for n in range(6)]
        chi = F[0, x + 2, mid, :]
        gu = inverse_of(g)
        wide = [gu[0], 2.0 * gu[1], 2.0 * gu[2], gu[3], 2.0 * gu[4], gu[5]]
        same = [12.0 * gu[0], 12.0 * gu[3], 12.0 * gu[5]]

        grads, bend = [[], [], []], []
        for c in range(GEO):
            f = F[c, x + 2, mid, :]
            ys = y_of(F, c, x + 2)
            grads[0].append(DX[c, x, mid, :])
            grads[1].append(first(*ys))
            grads[2].append(DZ[c, x + 2, mid, :])
            bend.append(
                same[0] * DXX[c, x, mid, :]
                + same[1] * second(ys[0], ys[1], f, ys[2], ys[3])
                + same[2] * (DZZ[c, x, own, :] + at_ends(C2[c], turn))
                + wide[1] * first(*y_of(DX, c, x))
                + wide[2] * first(*x_of(DZ, c))
                + wide[4] * first(*y_of(DZ, c, x + 2))
            )
        dchi = [grads[a][0] for a in range(3)]
        bend_g = sum(wide[n] * bend[1 + n] for n in range(1, 6)) + wide[0] * bend[1]

        def d(a, i, j):
            return grads[a][1 + PAIR[i][j]]

        def inv(i, j):
            return gu[PAIR[i][j]]

        trace, low = [], []
        for a in range(3):
            t = wide[0] * grads[a][1]
            for n in range(1, 6):
                t = t + wide[n] * grads[a][1 + n]
            trace.append(t)
            e = gu[0] * d(0, 0, a) + gu[3] * d(1, 1, a) + gu[5] * d(2, 2, a)
            e = e + gu[1] * (d(0, 1, a) + d(1, 0, a)) + gu[2] * (d(0, 2, a) + d(2, 0, a))
            e = e + gu[4] * (d(1, 2, a) + d(2, 1, a))
            low.append(e - 0.5 * t)
        gd = [inv(k, 0) * low[0] + inv(k, 1) * low[1] + inv(k, 2) * low[2] for k in range(3)]

        cyc = {
            (0, 0, 0): 3.0 * d(0, 0, 0), (1, 1, 1): 3.0 * d(1, 1, 1), (2, 2, 2): 3.0 * d(2, 2, 2),
            (0, 0, 1): 2.0 * d(0, 0, 1) + d(1, 0, 0), (0, 0, 2): 2.0 * d(0, 0, 2) + d(2, 0, 0),
            (0, 1, 1): 2.0 * d(1, 0, 1) + d(0, 1, 1), (1, 1, 2): 2.0 * d(1, 1, 2) + d(2, 1, 1),
            (0, 2, 2): 2.0 * d(2, 0, 2) + d(0, 2, 2), (1, 2, 2): 2.0 * d(2, 1, 2) + d(1, 2, 2),
            (0, 1, 2): d(0, 1, 2) + d(1, 0, 2) + d(2, 0, 1),
        }

        def s(*idx):
            return cyc[tuple(sorted(idx))]

        up = [[[None] * 3 for _ in range(3)] for _ in range(3)]
        for i in range(3):
            for l in range(3):
                for j in range(l, 3):
                    value = inv(i, 0) * s(0, l, j) + inv(i, 1) * s(1, l, j) + inv(i, 2) * s(2, l, j)
                    up[l][i][j] = value
                    up[j][i][l] = value
        squares = None
        for l in range(3):
            for m in range(l, 3):
                if l == m:
                    diag = up[l][0][0] * up[l][0][0] + up[l][1][1] * up[l][1][1] + up[l][2][2] * up[l][2][2]
                    off = up[l][0][1] * up[l][1][0] + up[l][0][2] * up[l][2][0] + up[l][1][2] * up[l][2][1]
                    trc = diag + 2.0 * off
                else:
                    trc = sum(up[l][i][j] * up[m][j][i] for i in range(3) for j in range(3) if i + j) + (
                        up[l][0][0] * up[m][0][0]
                    )
                term = wide[PAIR[l][m]] * trc
                squares = term if squares is None else squares + term

        def z_of(n):
            return DZR[n, x, own, :] + at_ends(C1[GEO + n], turn)

        rest_grad = [[], [], []]
        for n in range(7):
            rest_grad[0].append(first(*x_of(R, n)))
            rest_grad[1].append(first(*y_of(R, n, x + 2)))
            rest_grad[2].append(z_of(n))
        div = first(*x_of(R, 7)) + first(*y_of(R, 8, x + 2)) + z_of(7)
        A = [R[n, x + 2, mid, :] for n in range(6)]
        K = R[6, x + 2, mid, :]

        mixed = [
            [A[PAIR[i][0]] * inv(0, j) + A[PAIR[i][1]] * inv(1, j) + A[PAIR[i][2]] * inv(2, j) for j in range(3)]
            for i in range(3)
        ]
        raised = [
            inv(i, 0) * mixed[0][j] + inv(i, 1) * mixed[1][j] + inv(i, 2) * mixed[2][j]
            for i, j in ((0, 0), (0, 1), (0, 2), (1, 1), (1, 2), (2, 2))
        ]
        a_sq = mixed[0][0] * mixed[0][0] + mixed[1][1] * mixed[1][1] + mixed[2][2] * mixed[2][2]
        a_sq = a_sq + 2.0 * (
            mixed[0][1] * mixed[1][0] + mixed[0][2] * mixed[2][0] + mixed[1][2] * mixed[2][1]
        )
        chi_inv = 1.0 / chi
        dchi_up = [inv(k, 0) * dchi[0] + inv(k, 1) * dchi[1] + inv(k, 2) * dchi[2] for k in range(3)]
        grad_sq = dchi_up[0] * dchi[0] + dchi_up[1] * dchi[1] + dchi_up[2] * dchi[2]
        gd_trace = gd[0] * trace[0] + gd[1] * trace[1] + gd[2] * trace[2]
        gd_chi = gd[0] * dchi[0] + gd[1] * dchi[1] + gd[2] * dchi[2]
        ricci = 0.5 * (gd_trace - bend_g) + squares * (1.0 / 12.0) + 12.0 * div
        ham = (chi * ricci + 2.0 * (bend[0] - gd_chi) - 2.5 * grad_sq * chi_inv) * (1.0 / 144.0)
        ham_out[x, own, :] = ham + (2.0 / 3.0) * (K * K) - a_sq

        weight = 1.5 * chi_inv
        vec = [gd[l] + weight * dchi_up[l] for l in range(3)]
        twice = [0.5 * raised[0], raised[1], raised[2], 0.5 * raised[3], raised[4], 0.5 * raised[5]]
        for i in range(3):
            total = (-2.0 / 3.0) * rest_grad[i][6]
            for j in range(3):
                for k in range(3):
                    total = total + inv(j, k) * rest_grad[j][PAIR[k][i]]
            for l in range(3):
                total = total - vec[l] * A[PAIR[l][i]]
            for n in range(6):
                total = total - twice[n] * grads[i][1 + n]
            mom_out[i, x, own, :] = total * (1.0 / 12.0)

    def tally(x, b):
        own = pl.ds(pl.multiple_of(8 * b, 8), 8)
        ham = ham_out[x, own, :]
        m0, m1, m2 = [mom_out[n, x, own, :] for n in range(3)]
        ACC[0] += ham * ham
        ACC[1] += m0 * m0 + m1 * m1 + m2 * m2

    def term(d, b):
        rows = pl.ds(8 * b, 8)
        return remote(CS.at[d, :, :, rows], CR.at[1 - d, :, :, rows], S_TERM + 4 * d + b, at(2 * d - 1, 0, 0))

    terms = [[term(d, b) for b in range(BLOCKS)] for d in range(2)]

    def send_terms(b):
        mid = pl.ds(OWN + 8 * b, 8)
        for d in range(2):
            geo_xs[d][b].wait_recv()
        for d in range(2):
            halo = CX + 2 if d else 0
            for k in range(2):
                gu = inverse_of([F[1 + n, halo + k, mid, :] for n in range(6)])
                chi = F[0, halo + k, mid, :]

                def part(n):
                    if d == 0:
                        f0 = R[n, 2, mid, :]
                        return -f0 if k == 0 else 8.0 * f0 - R[n, 3, mid, :]
                    f7 = R[n, CX + 1, mid, :]
                    return R[n, CX, mid, :] - 8.0 * f7 if k == 0 else f7

                a = [part(n) for n in range(8)]
                own = pl.ds(8 * b, 8)
                CS[d, 0, k, own, :] = chi * a[7] * (1.0 / 12.0)
                for i in range(3):
                    value = gu[0] * a[PAIR[0][i]] + gu[1] * a[PAIR[1][i]] + gu[2] * a[PAIR[2][i]]
                    if i == 0:
                        value = value - (2.0 / 3.0) * a[6]
                    CS[d, 1 + i, k, own, :] = value * (1.0 / 12.0)
        for d in range(2):
            terms[d][b].start()

    def inner(lo, hi):
        def body(i, _):
            k = lax.rem(i, 8)
            x, odd, last = 2 + k // 2, lax.rem(k, 2), i // 8
            b = (1 - last) * (1 + odd) + last * 3 * odd
            cell(x, b)
            tally(x, b)
            return 0

        lax.fori_loop(lo, hi, body, 0)

    inner(0, 8)
    for copy in edge_yz:
        copy.wait_recv()
    lax.fori_loop(0, 2, y_ends, 0)
    lax.fori_loop(0, PAIRS, open_y_dz, 0)
    send_terms(0)
    for step in [(-2, 0, 0), (2, 0, 0), (0, 0, -2), (0, 0, 2)]:
        pl.semaphore_signal(near_sem, inc=1, device_id=at(*step), device_id_type=MESH)
    send_terms(1)
    inner(8, 12)
    send_terms(2)
    inner(12, 16)
    send_terms(3)
    pl.semaphore_wait(near_sem, 4)
    for k in range(1, n_gy):
        pl.semaphore_signal(far_sem, inc=1, device_id=at(0, k, 0), device_id_type=MESH)

    for copy in edge_xy + edge_xz + ends_x:
        copy.wait_recv()
    for sx in range(2):
        for sy in range(2):
            for c in range(GEO):
                for k in range(2):
                    layer = (CX + 2 if sx else 0) + k
                    row = OWN + CY if sy else OWN - 2
                    F[c, layer, row : row + 2, :] = XYR[sx, sy, c * 4 + k * 2 : c * 4 + k * 2 + 2, :]
        for v in range(2):
            CXE[sx, v] = change(XER[sx, 0, v], XER[sx, 1, v], XER[sx, 2, v])[0]

    def x_ends(k, _):
        side, xi = k // 2, lax.rem(k, 2)
        layer = side * (CX + 2) + xi
        for c in range(GEO):
            changed = CXE[side, c // 4]
            for b in range(BLOCKS):
                rows = pl.ds(OWN + 8 * b, 8)
                turn = CZ - 2 - 32 * (c % 4) - 4 * (BLOCKS * xi + b)
                DZ[c, layer, rows, :] = first(*wrapped(F[c, layer, rows, :])) + at_ends(changed, turn)
        return 0

    lax.fori_loop(0, 4, x_ends, 0)
    x_rows(lambda k: k + (k // 2) * (CX - 4), (0, 1, 2, 3, 4, 5))

    def edge_cell(i, _):
        k = i // BLOCKS
        cell(k + (k // 2) * (CX - 4), lax.rem(i, BLOCKS))
        return 0

    lax.fori_loop(0, 4 * BLOCKS, edge_cell, 0)

    for d in range(2):
        for b in range(BLOCKS):
            terms[d][b].wait_recv()

    def finish(k, _):
        side, sub = k // 2, lax.rem(k, 2)
        x = k + side * (CX - 4)
        ham_out[x] = ham_out[x] + CR[side, 0, sub]
        for n in range(3):
            mom_out[n, x] = mom_out[n, x] + CR[side, 1 + n, sub]
        for b in range(BLOCKS):
            tally(x, b)
        return 0

    lax.fori_loop(0, 4, finish, 0)
    MINE[0, 0:1, :] = jnp.sum(ACC[0], axis=0, keepdims=True)
    MINE[0, 1:2, :] = jnp.sum(ACC[1], axis=0, keepdims=True)
    rank_a = iy * n_gz + iz
    n_plane = n_gy * n_gz
    SUM_A[rank_a] = MINE[0]
    pl.semaphore_wait(far_sem, n_gy - 1)
    for dy in range(n_gy):
        for dz in range(n_gz):
            if dy or dz:
                remote(MINE.at[0], SUM_A.at[rank_a], S_SUM_A, at(0, dy, dz)).start()
    others = remote(SUM_A.at[pl.ds(0, n_plane - 1)], SUM_A.at[pl.ds(0, n_plane - 1)], S_SUM_A, at(0, 1, 0))
    others.wait_recv()
    total = SUM_A[0]
    for k in range(1, n_plane):
        total = total + SUM_A[k]
    MINE[1] = total
    SUM_B[ix] = total
    for dx in range(1, n_gx):
        remote(MINE.at[1], SUM_B.at[ix], S_SUM_B, at(dx, 0, 0)).start()
    along = remote(SUM_B.at[pl.ds(0, n_gx - 1)], SUM_B.at[pl.ds(0, n_gx - 1)], S_SUM_B, at(1, 0, 0))
    along.wait_recv()
    total = SUM_B[0]
    for j in range(1, n_gx):
        total = total + SUM_B[j]
    sums = jnp.sum(total, axis=1, keepdims=True)
    cells = float(CX * CY * CZ * n_gx * n_gy * n_gz)
    column = lax.broadcasted_iota(jnp.int32, (1, 2), 1)
    ham_sum = jnp.broadcast_to(sums[0:1], (1, 2))
    mom_sum = jnp.broadcast_to(sums[1:2], (1, 2))
    norm_out[...] = jnp.sqrt(jnp.where(column == 0, ham_sum / cells, mom_sum / (3.0 * cells)))

    sent = geo_ys + geo_zs + rest_ys + rest_zs + edge_xy + edge_yz + edge_xz + ends_x + [others, along]
    for copy in [c for row in geo_xs + terms for c in row] + sent:
        copy.wait_send()


def solution(mesh):
    sizes = (mesh.shape["gx"], mesh.shape["gy"], mesh.shape["gz"])
    n_plane = sizes[1] * sizes[2]
    f32 = jnp.float32

    def step(chi, met, cur, trk, gam):
        vm = lambda *shape: pltpu.VMEM(shape, f32)
        ham, mom, norm = pl.pallas_call(
            functools.partial(kernel, sizes),
            out_shape=(
                pltpu.VMEM((CX, CY, CZ), f32),
                pltpu.VMEM((3, CX, CY, CZ), f32),
                jax.ShapeDtypeStruct((1, 2), f32),
            ),
            in_specs=[pl.BlockSpec(memory_space=pl.ANY)] * 5,
            out_specs=(
                pl.BlockSpec(memory_space=pltpu.VMEM),
                pl.BlockSpec(memory_space=pltpu.VMEM),
                pl.BlockSpec(memory_space=pltpu.VMEM),
            ),
            scratch_shapes=[
                vm(GEO, LX, ROWS, CZ), vm(REST, LX, ROWS, CZ),
                vm(GEO, LX, ROWS, CZ), vm(GEO, CX, CY, CZ), vm(8, CX, CY, CZ),
                vm(GEO, CX, ROWS, CZ), vm(GEO, CX, ROWS, CZ), vm(2, 8, CZ),
                vm(2, 136, CZ), vm(2, 8, 2 * CX, CZ), vm(2, 136, CZ), vm(2, 8, 2 * CX, CZ),
                vm(2, 128, CZ), vm(2, 2, 8, CZ), vm(2, 2, 32, CZ),
                vm(15, 8, CZ), vm(2, 15, 8, CZ), vm(15, 8, CZ), vm(GEO, 8, CZ),
                vm(2, 2, 8, CZ), vm(2, 3, 2, 8, CZ), vm(2, 2, 8, CZ),
                vm(2, 4, 2, CY, CZ), vm(2, 4, 2, CY, CZ),
                vm(2, 2, CZ), vm(n_plane, 2, CZ), vm(sizes[0], 2, CZ),
                pltpu.SemaphoreType.DMA((5,)),
                pltpu.SemaphoreType.DMA((S_COUNT,)),
                pltpu.SemaphoreType.DMA((S_COUNT,)),
                pltpu.SemaphoreType.REGULAR,
                pltpu.SemaphoreType.REGULAR,
            ],
            compiler_params=pltpu.CompilerParams(collective_id=0, has_side_effects=True),
        )(chi, met, cur, trk, gam)
        return ham, mom, norm.reshape(2)

    return jax.shard_map(
        step,
        mesh=mesh,
        in_specs=(
            P("gx", "gy", "gz"),
            P(None, "gx", "gy", "gz"),
            P(None, "gx", "gy", "gz"),
            P("gx", "gy", "gz"),
            P(None, "gx", "gy", "gz"),
        ),
        out_specs=(P("gx", "gy", "gz"), P(None, "gx", "gy", "gz"), P()),
        check_vma=False,
    )
```

time: 50.9 us -> 37.7 us (0.74)
  Pallas kernels: 46.3 us -> 35 us
  local copies, waits for them, and re-layouts: 3.85 us -> 1.92 us
    pallas_call x1, Pallas kernels: 46.3 us -> 35 us  [step(): pl.pallas_call(functools.partial(kernel, sizes), out_shape=(pltpu.VMEM((C...]
    unnamed x5, local copies, waits for them, and re-layouts: 3.85 us -> 1.92 us
where the time goes in v2:
time: 37.7 us; the launch traced here: 37.6 us
  Pallas kernels  35 us (93%)
  local copies, waits for them, and re-layouts  1.92 us (5%)
  between operations  0.64 us (2%)
    pallas_call x1, Pallas kernels, step(): pl.pallas_call(functools.partial(kernel, sizes), out_shape=(pltpu.VMEM((C...  35 us
    unnamed x5, local copies, waits for them, and re-layouts  1.92 us

profile of v2, /device:TPU:1, one launch (start us, length us, event | category | flops | bytes accessed | tf_op | source)
XLA Modules:
  0.0 37.6 jit_solution(16890277303684173942)
XLA Ops:
  0.6 35.0 %shard_map.76 = (f32[8,32,128]{2,1,0:T(8,128)S(1)}, f32[3,8,32,128]{3,2,1,0:T(8,128)S(1)}, f32[1,2]{1,0:T(1,128)}) custom-call(f32[8,32,128]{2,1,0:T(8,128)} %chi_in.1, f32[6,8,32,128]{3,2,1,0:T(8,128)} %met_in.1, f32[6,8,32,128]{3,2,1,0:T(8,128)} %cur_in.1, f32[8,32,128]{2,1,0:T(8,128)} %trk_in.1, f32[3,8,32,128]{3,2,1,0:T(8,128)} %gam_in.1), custom_call_target="tpu_custom_call" | custom-call | tf_op jit(solution)/shard_map/pallas_call | solution.py:603
  35.7 0.7 %copy.11 = f32[8,32,128]{2,1,0:T(8,128)} copy(f32[8,32,128]{2,1,0:T(8,128)S(1)} %get-tuple-element.9) | data formatting | bytes 262144
  36.3 0.0 copy-start
  36.3 0.7 %copy.12 = f32[3,8,32,128]{3,2,1,0:T(8,128)} copy(f32[3,8,32,128]{3,2,1,0:T(8,128)S(1)} %get-tuple-element.10) | data formatting | bytes 786432
  37.1 0.0 copy-done
  37.1 0.5 %copy.13 = f32[2]{0:T(128)} copy(f32[2]{0:T(128)S(1)} %bitcast.1) | data formatting | bytes 16
Async XLA Ops:
  36.3 0.8 %copy-start = (f32[1,2]{1,0:T(1,128)S(1)}, f32[1,2]{1,0:T(1,128)}, u32[]{:S(2)}) copy-start(f32[1,2]{1,0:T(1,128)} %get-tuple-element.8) | copy-start | bytes 28

commit v3 on v2

--- a/solution.py
+++ b/solution.py
@@ -53,7 +53,7 @@
     chi_in, met_in, cur_in, trk_in, gam_in,
     ham_out, mom_out, norm_out,
     F, R, DZ, DZZ, DZR, DX, DXX, ACC,
-    YSG, YSR, YRG, YRR, YDZ, YZR, XYR,
+    YSG, YSR, YRG, YRR, YDZ, YZR, XYR, TAPS,
     ZP, ZPR, C1, C2, XE, XER, CXE,
     CS, CR, MINE, SUM_A, SUM_B,
     load_sem, send_sem, recv_sem, near_sem, far_sem,
@@ -110,14 +110,8 @@
             out = jnp.where(lane4 == t, pltpu.roll(tile, turn, 1) if turn else tile, out)
         return out
 
-    def pack_geo(c, _):
-        ZP[c] = packed([F[c, 2 + x, pl.ds(OWN + 8 * b, 8), :] for x in range(CX) for b in range(BLOCKS)])
-        return 0
-
-    def pack_rest(n, _):
-        c = n + (n // 7) * 2
-        ZP[GEO + n] = packed([R[c, 2 + x, pl.ds(OWN + 8 * b, 8), :] for x in range(CX) for b in range(BLOCKS)])
-        return 0
+    def own_tiles(ref, c):
+        return [ref[c, 2 + x, pl.ds(OWN + 8 * b, 8), :] for x in range(CX) for b in range(BLOCKS)]
 
     def pack_y_geo(p, _):
         for c in range(GEO):
@@ -133,26 +127,6 @@
             YSR[0, n, rows, :] = R[c, 2 + x, OWN : OWN + 2, :]
             YSR[1, n, rows, :] = R[c, 2 + x, OWN + CY - 2 : OWN + CY, :]
         return 0
-
-    for s in range(2):
-        for p in range(PAIRS):
-            YSG[s, 32 * p + 24 : 32 * p + 32, :] = zero
-    loads[0].wait()
-    loads[1].wait()
-    lax.fori_loop(0, PAIRS, pack_y_geo, 0)
-    lax.fori_loop(0, GEO, pack_geo, 0)
-    for s in range(2):
-        YSG[s, 128:136, :] = packed([YSG[s, 8 * k : 8 * k + 8, :] for k in range(16)])
-        for v in range(2):
-            out = zero
-            for c in range(4 * v, min(4 * v + 4, GEO)):
-                turn = (32 * (c % 4) - 96 * s) % CZ
-                out = jnp.where(lane // 32 == c % 4, pltpu.roll(ZP[c], turn, 1) if turn else ZP[c], out)
-            XE[s, v] = out
-    for copy in loads[2:]:
-        copy.wait()
-    lax.fori_loop(0, CX, pack_y_rest, 0)
-    lax.fori_loop(0, 8, pack_rest, 0)
 
     def geo_x(d, b):
         rows = pl.ds(OWN + 8 * b, 8)
@@ -187,53 +161,99 @@
         for dx, dz in combos
     ]
 
+    column = lax.broadcasted_iota(jnp.int32, (CZ, 2 * CZ), 1)
+    step = lax.rem(lax.broadcasted_iota(jnp.int32, (CZ, 2 * CZ), 0) - column + 2 * CZ, CZ)
+
+    def weights(table):
+        out = jnp.zeros((CZ, 2 * CZ), jnp.float32)
+        for k, w in table:
+            out = jnp.where(step == k % CZ, w, out)
+        return out
+
+    taps = jnp.where(
+        column < CZ,
+        weights(((-2, 1.0), (-1, -8.0), (1, 8.0), (2, -1.0))),
+        weights(((-2, -1.0), (-1, 16.0), (0, -30.0), (1, 16.0), (2, -1.0))),
+    ).astype(jnp.bfloat16)
+    for k in range(3):
+        TAPS[CZ * k : CZ * k + CZ, :] = taps
+    for s in range(2):
+        for p in range(PAIRS):
+            YSG[s, 32 * p + 24 : 32 * p + 32, :] = zero
+
+    def along_z(cells, width):
+        high = cells.astype(jnp.bfloat16)
+        rest = cells - high.astype(jnp.float32)
+        middle = rest.astype(jnp.bfloat16)
+        low = (rest - middle.astype(jnp.float32)).astype(jnp.bfloat16)
+        pieces = jnp.concatenate([high, middle, low], axis=1)
+        return jnp.dot(pieces, TAPS[:, 0:width], preferred_element_type=jnp.float32)
+
+    loads[0].wait()
+    loads[1].wait()
     pl.semaphore_wait(barrier, len(faces))
-    for copy in geo_xs[0][:1] + geo_xs[1][:1] + geo_zs + geo_ys + rest_zs + rest_ys:
-        copy.start()
-    for b in range(1, BLOCKS):
+    for b in range(BLOCKS):
         for d in range(2):
             geo_xs[d][b].start()
-    for copy in ends_x:
+    for c in range(GEO):
+        ZP[c] = packed(own_tiles(F, c))
+    for copy in geo_zs:
         copy.start()
-
-    def wrapped(tile):
-        return (
-            pltpu.roll(tile, 2, 1), pltpu.roll(tile, 1, 1), pltpu.roll(tile, CZ - 1, 1), pltpu.roll(tile, CZ - 2, 1)
-        )
-
-    def z_geo(x, _):
-        for c in range(GEO):
-            for b in range(BLOCKS):
-                rows = pl.ds(OWN + 8 * b, 8)
-                tile = F[c, x + 2, rows, :]
-                taps = wrapped(tile)
-                DZ[c, x + 2, rows, :] = first(*taps)
-                DZZ[c, x, pl.ds(8 * b, 8), :] = second(taps[0], taps[1], tile, taps[2], taps[3])
-        return 0
-
-    def z_rest(x, _):
-        for n, c in enumerate(Z_REST):
-            for b in range(BLOCKS):
-                DZR[n, x, pl.ds(8 * b, 8), :] = first(*wrapped(R[c, x + 2, pl.ds(OWN + 8 * b, 8), :]))
-        return 0
+    lax.fori_loop(0, PAIRS, pack_y_geo, 0)
+    for s in range(2):
+        YSG[s, 128:136, :] = packed([YSG[s, 8 * k : 8 * k + 8, :] for k in range(16)])
+        for v in range(2):
+            out = zero
+            for c in range(4 * v, min(4 * v + 4, GEO)):
+                turn = (32 * (c % 4) - 96 * s) % CZ
+                out = jnp.where(lane // 32 == c % 4, pltpu.roll(ZP[c], turn, 1) if turn else ZP[c], out)
+            XE[s, v] = out
+    for copy in geo_ys + ends_x:
+        copy.start()
+    for copy in loads[2:]:
+        copy.wait()
+    lax.fori_loop(0, CX, pack_y_rest, 0)
+    for n, c in enumerate(Z_REST):
+        ZP[GEO + n] = packed(own_tiles(R, c))
+    for copy in rest_zs + rest_ys:
+        copy.start()
+
+    own_rows = (slice(2, 2 + CX), slice(OWN, OWN + CY))
+
+    def z_geo(c):
+        out = along_z(F[c, own_rows[0], own_rows[1], :].reshape(CX * CY, CZ), 2 * CZ)
+        DZ[c, own_rows[0], own_rows[1], :] = out[:, 0:CZ].reshape(CX, CY, CZ)
+        DZZ[c] = out[:, CZ:].reshape(CX, CY, CZ)
+
+    def z_rest(n):
+        c = n + (n // 7) * 2
+        DZR[n] = along_z(R[c, own_rows[0], own_rows[1], :].reshape(CX * CY, CZ), CZ).reshape(CX, CY, CZ)
 
     def x_rows(layers, tiles):
-        def body(i, _):
-            x, b = layers(i // len(tiles)), lax.rem(i, len(tiles))
-            b = tiles[0] + b * (tiles[1] - tiles[0])
-            rows = pl.ds(pl.multiple_of(8 * b, 8), 8)
-            for c in range(GEO):
-                taps = [F[c, x + k, rows, :] for k in range(5)]
-                DX[c, x, rows, :] = first(taps[0], taps[1], taps[3], taps[4])
-                DXX[c, x, rows, :] = second(*taps)
+        def body(k, _):
+            x = layers(k)
+            for b in tiles:
+                rows = slice(8 * b, 8 * b + 8)
+                for c in range(GEO):
+                    taps = [F[c, x + k, rows, :] for k in range(5)]
+                    DX[c, x, rows, :] = first(taps[0], taps[1], taps[3], taps[4])
+                    DXX[c, x, rows, :] = second(*taps)
             return 0
 
-        lax.fori_loop(0, 4 * len(tiles), body, 0)
-
-    lax.fori_loop(0, CX, z_geo, 0)
+        lax.fori_loop(0, 4, body, 0)
+
+    for c in range(GEO):
+        z_geo(c)
+    for n in range(8):
+        z_rest(n)
+    x_rows(lambda k: k + 2, (1, 2, 3, 4))
     for copy in geo_zs:
         copy.wait_recv()
     for copy in edge_yz + edge_xz:
+        copy.start()
+    for copy in geo_ys:
+        copy.wait_recv()
+    for copy in edge_xy:
         copy.start()
 
     def change(own, left, right):
@@ -252,17 +272,17 @@
     for c in range(GEO):
         C1[c], C2[c] = change(ZP[c], ZPR[0, c], ZPR[1, c])
 
-    def z_ends(x, _):
+    def z_ends(half, _):
         for c in range(GEO):
             changed = C1[c]
-            for b in range(BLOCKS):
-                rows = pl.ds(OWN + 8 * b, 8)
-                DZ[c, x + 2, rows, :] += at_ends(changed, CZ - 2 - 4 * (BLOCKS * x + b))
-        return 0
-
-    lax.fori_loop(0, CX, z_ends, 0)
-    x_rows(lambda k: k + 2, (1, 2, 3, 4))
-    lax.fori_loop(0, CX, z_rest, 0)
+            for k in range(4):
+                x = 4 * half + k
+                for b in range(BLOCKS):
+                    rows = pl.ds(OWN + 8 * b, 8)
+                    DZ[c, x + 2, rows, :] += at_ends(changed, CZ - 2 - 4 * (BLOCKS * x + b))
+        return 0
+
+    lax.fori_loop(0, 2, z_ends, 0)
     for copy in rest_zs + rest_ys:
         copy.wait_recv()
     for n in range(8):
@@ -276,11 +296,6 @@
         return 0
 
     lax.fori_loop(0, CX, open_y_rest, 0)
-    for copy in geo_ys:
-        copy.wait_recv()
-    for copy in edge_xy:
-        copy.start()
-
     def open_y_geo(p, _):
         for c in range(GEO):
             for xi in range(2):
@@ -289,15 +304,12 @@
                 F[c, 2 + 2 * p + xi, OWN + CY : OWN + CY + 2, :] = YRG[1, rows, :]
         return 0
 
-    lax.fori_loop(0, PAIRS, open_y_geo, 0)
-    x_rows(lambda k: k + 2, (0, 5))
-
-    def y_ends(s, _):
+    def y_ends(s):
         changed = change(YRG[s, 128:136, :], YZR[0, s], YZR[1, s])[0]
+        out = along_z(YRG[s, 0:128, :], CZ)
         for k in range(16):
             rows = slice(8 * k, 8 * k + 8)
-            YDZ[s, rows, :] = first(*wrapped(YRG[s, rows, :])) + at_ends(changed, CZ - 2 - 4 * k)
-        return 0
+            YDZ[s, rows, :] = out[rows] + at_ends(changed, CZ - 2 - 4 * k)
 
     def open_y_dz(p, _):
         for c in range(GEO):
@@ -492,19 +504,22 @@
 
         lax.fori_loop(lo, hi, body, 0)
 
-    inner(0, 8)
-    for copy in edge_yz:
-        copy.wait_recv()
-    lax.fori_loop(0, 2, y_ends, 0)
-    lax.fori_loop(0, PAIRS, open_y_dz, 0)
     send_terms(0)
     for step in [(-2, 0, 0), (2, 0, 0), (0, 0, -2), (0, 0, 2)]:
         pl.semaphore_signal(near_sem, inc=1, device_id=at(*step), device_id_type=MESH)
+    inner(0, 4)
     send_terms(1)
-    inner(8, 12)
+    inner(4, 8)
     send_terms(2)
-    inner(12, 16)
+    lax.fori_loop(0, PAIRS, open_y_geo, 0)
+    x_rows(lambda k: k + 2, (0, 5))
+    for copy in edge_yz:
+        copy.wait_recv()
+    for s in range(2):
+        y_ends(s)
+    lax.fori_loop(0, PAIRS, open_y_dz, 0)
     send_terms(3)
+    inner(8, 16)
     pl.semaphore_wait(near_sem, 4)
     for k in range(1, n_gy):
         pl.semaphore_signal(far_sem, inc=1, device_id=at(0, k, 0), device_id_type=MESH)
@@ -521,18 +536,19 @@
         for v in range(2):
             CXE[sx, v] = change(XER[sx, 0, v], XER[sx, 1, v], XER[sx, 2, v])[0]
 
-    def x_ends(k, _):
-        side, xi = k // 2, lax.rem(k, 2)
-        layer = side * (CX + 2) + xi
-        for c in range(GEO):
+    def x_ends(c):
+        for side in range(2):
+            layers = slice(CX + 2, CX + 4) if side else slice(0, 2)
+            out = along_z(F[c, layers, own_rows[1], :].reshape(2 * CY, CZ), CZ)
             changed = CXE[side, c // 4]
-            for b in range(BLOCKS):
-                rows = pl.ds(OWN + 8 * b, 8)
-                turn = CZ - 2 - 32 * (c % 4) - 4 * (BLOCKS * xi + b)
-                DZ[c, layer, rows, :] = first(*wrapped(F[c, layer, rows, :])) + at_ends(changed, turn)
-        return 0
-
-    lax.fori_loop(0, 4, x_ends, 0)
+            for xi in range(2):
+                for b in range(BLOCKS):
+                    turn = CZ - 2 - 32 * (c % 4) - 4 * (BLOCKS * xi + b)
+                    row = CY * xi + 8 * b
+                    DZ[c, layers.start + xi, pl.ds(OWN + 8 * b, 8), :] = out[row : row + 8] + at_ends(changed, turn)
+
+    for c in range(GEO):
+        x_ends(c)
     x_rows(lambda k: k + (k // 2) * (CX - 4), (0, 1, 2, 3, 4, 5))
 
     def edge_cell(i, _):
@@ -593,6 +609,17 @@
         copy.wait_send()
 
 
+def write_out(ham, mom, norm, ham_out, mom_out, norm_out, sems):
+    copies = [
+        pltpu.make_async_copy(src, dst, sems.at[i])
+        for i, (src, dst) in enumerate(((ham, ham_out), (mom, mom_out), (norm, norm_out)))
+    ]
+    for copy in copies:
+        copy.start()
+    for copy in copies:
+        copy.wait()
+
+
 def solution(mesh):
     sizes = (mesh.shape["gx"], mesh.shape["gy"], mesh.shape["gz"])
     n_plane = sizes[1] * sizes[2]
@@ -605,7 +632,7 @@
             out_shape=(
                 pltpu.VMEM((CX, CY, CZ), f32),
                 pltpu.VMEM((3, CX, CY, CZ), f32),
-                jax.ShapeDtypeStruct((1, 2), f32),
+                pltpu.VMEM((1, 2), f32),
             ),
             in_specs=[pl.BlockSpec(memory_space=pl.ANY)] * 5,
             out_specs=(
@@ -619,6 +646,7 @@
                 vm(GEO, CX, ROWS, CZ), vm(GEO, CX, ROWS, CZ), vm(2, 8, CZ),
                 vm(2, 136, CZ), vm(2, 8, 2 * CX, CZ), vm(2, 136, CZ), vm(2, 8, 2 * CX, CZ),
                 vm(2, 128, CZ), vm(2, 2, 8, CZ), vm(2, 2, 32, CZ),
+                pltpu.VMEM((3 * CZ, 2 * CZ), jnp.bfloat16),
                 vm(15, 8, CZ), vm(2, 15, 8, CZ), vm(15, 8, CZ), vm(GEO, 8, CZ),
                 vm(2, 2, 8, CZ), vm(2, 3, 2, 8, CZ), vm(2, 2, 8, CZ),
                 vm(2, 4, 2, CY, CZ), vm(2, 4, 2, CY, CZ),
@@ -631,6 +659,17 @@
             ],
             compiler_params=pltpu.CompilerParams(collective_id=0, has_side_effects=True),
         )(chi, met, cur, trk, gam)
+        ham, mom, norm = pl.pallas_call(
+            write_out,
+            out_shape=(
+                jax.ShapeDtypeStruct((CX, CY, CZ), f32),
+                jax.ShapeDtypeStruct((3, CX, CY, CZ), f32),
+                jax.ShapeDtypeStruct((1, 2), f32),
+            ),
+            in_specs=[pl.BlockSpec(memory_space=pl.ANY)] * 3,
+            out_specs=[pl.BlockSpec(memory_space=pl.ANY)] * 3,
+            scratch_shapes=[pltpu.SemaphoreType.DMA((3,))],
+        )(*[pltpu.with_memory_space_constraint(x, pltpu.VMEM) for x in (ham, mom, norm)])
         return ham, mom, norm.reshape(2)
 
     return jax.shard_map(

time: 37.7 us -> 33.9 us (0.90)
  local copies, waits for them, and re-layouts: 1.92 us -> 0 us
  Pallas kernels: 35 us -> 33.2 us
    pallas_call x1, Pallas kernels: 35 us -> 32.3 us  [step(): pl.pallas_call(functools.partial(kernel, sizes), out_shape=(pltpu.VMEM((C...]
    unnamed x5 -> x0, local copies, waits for them, and re-layouts: 1.92 us -> none
    pallas_call x0 -> x1, Pallas kernels: none -> 0.82 us  [step(): pl.pallas_call(write_out, out_shape=(jax.ShapeDtypeStruct((CX, CY, CZ), f...]
where the time goes in v3:
time: 33.9 us; the launch traced here: 33.8 us
  Pallas kernels  33.2 us (98%)
  between operations  0.64 us (2%)
    pallas_call x1, Pallas kernels, step(): pl.pallas_call(functools.partial(kernel, sizes), out_shape=(pltpu.VMEM((C...  32.3 us
    pallas_call x1, Pallas kernels, step(): pl.pallas_call(write_out, out_shape=(jax.ShapeDtypeStruct((CX, CY, CZ), f...  0.82 us

profile of v3, /device:TPU:1, one launch (start us, length us, event | category | flops | bytes accessed | tf_op | source)
XLA Modules:
  0.0 33.8 jit_solution(2587989716516845383)
XLA Ops:
  0.6 32.3 %shard_map.76 = (f32[8,32,128]{2,1,0:T(8,128)S(1)}, f32[3,8,32,128]{3,2,1,0:T(8,128)S(1)}, f32[1,2]{1,0:T(1,128)S(1)}) custom-call(f32[8,32,128]{2,1,0:T(8,128)} %chi_in.1, f32[6,8,32,128]{3,2,1,0:T(8,128)} %met_in.1, f32[6,8,32,128]{3,2,1,0:T(8,128)} %cur_in.1, f32[8,32,128]{2,1,0:T(8,128)} %trk_in.1, f32[3,8,32,128]{3,2,1,0:T(8,128)} %gam_in.1), custom_call_target="tpu_custom_call" | custom-call | tf_op jit(solution)/shard_map/pallas_call | solution.py:630
  33.0 0.8 %shard_map.77 = (f32[8,32,128]{2,1,0:T(8,128)}, f32[3,8,32,128]{3,2,1,0:T(8,128)}, f32[1,2]{1,0:T(1,128)}) custom-call(f32[8,32,128]{2,1,0:T(8,128)S(1)} %get-tuple-element.9.ham, f32[3,8,32,128]{3,2,1,0:T(8,128)S(1)} %get-tuple-element.10.mom, f32[1,2]{1,0:T(1,128)S(1)} %get-tuple-element.11.norm), custom_call_target="tpu_custom_call" | custom-call | tf_op jit(solution)/shard_map/pallas_call | solution.py:662

commit v4 on v3

--- a/solution.py
+++ b/solution.py
@@ -55,8 +55,8 @@
     F, R, DZ, DZZ, DZR, DX, DXX, ACC,
     YSG, YSR, YRG, YRR, YDZ, YZR, XYR, TAPS,
     ZP, ZPR, C1, C2, XE, XER, CXE,
-    CS, CR, MINE, SUM_A, SUM_B,
-    load_sem, send_sem, recv_sem, near_sem, far_sem,
+    CS, CR, PT, MINE, SUM_A, SUM_B,
+    load_sem, send_sem, recv_sem, two_sem, near_sem, far_sem,
 ):
     n_gx, n_gy, n_gz = sizes
     ix, iy, iz = lax.axis_index("gx"), lax.axis_index("gy"), lax.axis_index("gz")
@@ -75,7 +75,8 @@
 
     loads = [
         (chi_in, F.at[0, 2 : 2 + CX, OWN : OWN + CY]),
-        (met_in, F.at[1:7, 2 : 2 + CX, OWN : OWN + CY]),
+        (met_in.at[0:3], F.at[1:4, 2 : 2 + CX, OWN : OWN + CY]),
+        (met_in.at[3:6], F.at[4:7, 2 : 2 + CX, OWN : OWN + CY]),
         (cur_in, R.at[0:6, 2 : 2 + CX, OWN : OWN + CY]),
         (trk_in, R.at[6, 2 : 2 + CX, OWN : OWN + CY]),
         (gam_in, R.at[7:10, 2 : 2 + CX, OWN : OWN + CY]),
@@ -189,10 +190,12 @@
         pieces = jnp.concatenate([high, middle, low], axis=1)
         return jnp.dot(pieces, TAPS[:, 0:width], preferred_element_type=jnp.float32)
 
-    loads[0].wait()
-    loads[1].wait()
+    for copy in loads[:3]:
+        copy.wait()
     pl.semaphore_wait(barrier, len(faces))
-    for b in range(BLOCKS):
+    for step in faces:
+        pl.semaphore_signal(two_sem, inc=1, device_id=at(*step), device_id_type=MESH)
+    for b in range(BLOCKS - 1):
         for d in range(2):
             geo_xs[d][b].start()
     for c in range(GEO):
@@ -210,12 +213,14 @@
             XE[s, v] = out
     for copy in geo_ys + ends_x:
         copy.start()
-    for copy in loads[2:]:
+    for copy in loads[3:]:
         copy.wait()
-    lax.fori_loop(0, CX, pack_y_rest, 0)
     for n, c in enumerate(Z_REST):
         ZP[GEO + n] = packed(own_tiles(R, c))
-    for copy in rest_zs + rest_ys:
+    for copy in rest_zs:
+        copy.start()
+    lax.fori_loop(0, CX, pack_y_rest, 0)
+    for copy in rest_ys:
         copy.start()
 
     own_rows = (slice(2, 2 + CX), slice(OWN, OWN + CY))
@@ -244,17 +249,95 @@
 
     for c in range(GEO):
         z_geo(c)
+    pl.semaphore_wait(two_sem, len(faces))
+    for copy in edge_yz + edge_xz + [geo_xs[0][BLOCKS - 1], geo_xs[1][BLOCKS - 1]] + edge_xy:
+        copy.start()
+    for step in [(-2, 0, 0), (2, 0, 0), (0, 0, -2), (0, 0, 2)]:
+        pl.semaphore_signal(near_sem, inc=1, device_id=at(*step), device_id_type=MESH)
     for n in range(8):
         z_rest(n)
     x_rows(lambda k: k + 2, (1, 2, 3, 4))
+    def point(i, _):
+        x = i // 2
+        for n in range(2):
+            b = 2 * lax.rem(i, 2) + n
+            mid = pl.ds(pl.multiple_of(OWN + 8 * b, 8), 8)
+            own = pl.ds(pl.multiple_of(8 * b, 8), 8)
+            g00, g01, g02, g11, g12, g22 = [F[1 + k, x + 2, mid, :] for k in range(6)]
+            m00 = g11 * g22 - g12 * g12
+            m01 = g02 * g12 - g01 * g22
+            m02 = g01 * g12 - g02 * g11
+            m11 = g00 * g22 - g02 * g02
+            m12 = g01 * g02 - g00 * g12
+            m22 = g00 * g11 - g01 * g01
+            scale = 1.0 / (g00 * m00 + g01 * m01 + g02 * m02)
+            gu = [m00 * scale, m01 * scale, m02 * scale, m11 * scale, m12 * scale, m22 * scale]
+            d0 = 1.0 / g00
+            m_inv = 1.0 / m22
+            u01, u12 = -g01 * d0, m12 * m_inv
+
+            def inv(i, j):
+                return gu[PAIR[i][j]]
+
+            A = [R[k, x + 2, mid, :] for k in range(6)]
+            K = R[6, x + 2, mid, :]
+            mixed = [
+                [A[PAIR[i][0]] * inv(0, j) + A[PAIR[i][1]] * inv(1, j) + A[PAIR[i][2]] * inv(2, j) for j in range(3)]
+                for i in range(3)
+            ]
+            raised = [
+                inv(i, 0) * mixed[0][j] + inv(i, 1) * mixed[1][j] + inv(i, 2) * mixed[2][j]
+                for i, j in ((0, 0), (0, 1), (0, 2), (1, 1), (1, 2), (2, 2))
+            ]
+            a_sq = mixed[0][0] * mixed[0][0] + mixed[1][1] * mixed[1][1] + mixed[2][2] * mixed[2][2]
+            a_sq = a_sq + 2.0 * (
+                mixed[0][1] * mixed[1][0] + mixed[0][2] * mixed[2][0] + mixed[1][2] * mixed[2][1]
+            )
+            twice = [0.5 * raised[0], raised[1], raised[2], 0.5 * raised[3], raised[4], 0.5 * raised[5]]
+            kept = gu + twice + [(2.0 / 3.0) * (K * K) - a_sq]
+            kept += [u01, m02 * m_inv - u12 * u01, u12, d0, g00 * m_inv]
+            for k, value in enumerate(kept):
+                PT[k, x, own, :] = value
+        return 0
+
+    lax.fori_loop(0, 2 * CX, point, 0)
+    def term(d, b):
+        rows = pl.ds(8 * b, 8)
+        return remote(CS.at[d, :, :, rows], CR.at[1 - d, :, :, rows], S_TERM + 4 * d + b, at(2 * d - 1, 0, 0))
+
+    terms = [[term(d, b) for b in range(BLOCKS)] for d in range(2)]
+
+    def send_terms(b):
+        mid = pl.ds(OWN + 8 * b, 8)
+        for d in range(2):
+            geo_xs[d][b].wait_recv()
+        for d in range(2):
+            halo = CX + 2 if d else 0
+            for k in range(2):
+                gu = inverse_of([F[1 + n, halo + k, mid, :] for n in range(6)])
+                chi = F[0, halo + k, mid, :]
+
+                def part(n):
+                    if d == 0:
+                        f0 = R[n, 2, mid, :]
+                        return -f0 if k == 0 else 8.0 * f0 - R[n, 3, mid, :]
+                    f7 = R[n, CX + 1, mid, :]
+                    return R[n, CX, mid, :] - 8.0 * f7 if k == 0 else f7
+
+                a = [part(n) for n in range(8)]
+                own = pl.ds(8 * b, 8)
+                CS[d, 0, k, own, :] = chi * a[7] * (1.0 / 12.0)
+                for i in range(3):
+                    value = gu[0] * a[PAIR[0][i]] + gu[1] * a[PAIR[1][i]] + gu[2] * a[PAIR[2][i]]
+                    if i == 0:
+                        value = value - (2.0 / 3.0) * a[6]
+                    CS[d, 1 + i, k, own, :] = value * (1.0 / 12.0)
+        for d in range(2):
+            terms[d][b].start()
+
     for copy in geo_zs:
         copy.wait_recv()
-    for copy in edge_yz + edge_xz:
-        copy.start()
-    for copy in geo_ys:
-        copy.wait_recv()
-    for copy in edge_xy:
-        copy.start()
+    send_terms(0)
 
     def change(own, left, right):
         e = jnp.where(place < 2, left, right) - own
@@ -283,10 +366,14 @@
         return 0
 
     lax.fori_loop(0, 2, z_ends, 0)
-    for copy in rest_zs + rest_ys:
+    for copy in rest_zs:
         copy.wait_recv()
     for n in range(8):
         C1[GEO + n] = change(ZP[GEO + n], ZPR[0, GEO + n], ZPR[1, GEO + n])[0]
+
+    send_terms(1)
+    for copy in geo_ys:
+        copy.wait_recv()
 
     def open_y_rest(x, _):
         rows = pl.ds(2 * x, 2)
@@ -295,7 +382,6 @@
             R[c, 2 + x, OWN + CY : OWN + CY + 2, :] = YRR[1, n, rows, :]
         return 0
 
-    lax.fori_loop(0, CX, open_y_rest, 0)
     def open_y_geo(p, _):
         for c in range(GEO):
             for xi in range(2):
@@ -331,9 +417,8 @@
         def x_of(ref, c):
             return [ref[c, x + 2 + k, mid, :] for k in (-2, -1, 1, 2)]
 
-        g = [F[1 + n, x + 2, mid, :] for n in range(6)]
         chi = F[0, x + 2, mid, :]
-        gu = inverse_of(g)
+        gu = [PT[n, x, own, :] for n in range(6)]
         wide = [gu[0], 2.0 * gu[1], 2.0 * gu[2], gu[3], 2.0 * gu[4], gu[5]]
         same = [12.0 * gu[0], 12.0 * gu[3], 12.0 * gu[5]]
 
@@ -361,17 +446,20 @@
         def inv(i, j):
             return gu[PAIR[i][j]]
 
-        trace, low = [], []
+        def along(values):
+            one = values[1] + u01 * values[0]
+            return [values[0], one, values[2] + u12 * one + u02 * values[0]]
+
+        u01, u02, u12, d0, d1 = [PT[n, x, own, :] for n in range(13, 18)]
+        d2 = gu[5]
+        trace = []
         for a in range(3):
             t = wide[0] * grads[a][1]
             for n in range(1, 6):
                 t = t + wide[n] * grads[a][1 + n]
             trace.append(t)
-            e = gu[0] * d(0, 0, a) + gu[3] * d(1, 1, a) + gu[5] * d(2, 2, a)
-            e = e + gu[1] * (d(0, 1, a) + d(1, 0, a)) + gu[2] * (d(0, 2, a) + d(2, 0, a))
-            e = e + gu[4] * (d(1, 2, a) + d(2, 1, a))
-            low.append(e - 0.5 * t)
-        gd = [inv(k, 0) * low[0] + inv(k, 1) * low[1] + inv(k, 2) * low[2] for k in range(3)]
+        trace = along(trace)
+        dchi = along(dchi)
 
         cyc = {
             (0, 0, 0): 3.0 * d(0, 0, 0), (1, 1, 1): 3.0 * d(1, 1, 1), (2, 2, 2): 3.0 * d(2, 2, 2),
@@ -381,29 +469,42 @@
             (0, 1, 2): d(0, 1, 2) + d(1, 0, 2) + d(2, 0, 1),
         }
 
-        def s(*idx):
-            return cyc[tuple(sorted(idx))]
-
-        up = [[[None] * 3 for _ in range(3)] for _ in range(3)]
-        for i in range(3):
-            for l in range(3):
-                for j in range(l, 3):
-                    value = inv(i, 0) * s(0, l, j) + inv(i, 1) * s(1, l, j) + inv(i, 2) * s(2, l, j)
-                    up[l][i][j] = value
-                    up[j][i][l] = value
-        squares = None
-        for l in range(3):
-            for m in range(l, 3):
-                if l == m:
-                    diag = up[l][0][0] * up[l][0][0] + up[l][1][1] * up[l][1][1] + up[l][2][2] * up[l][2][2]
-                    off = up[l][0][1] * up[l][1][0] + up[l][0][2] * up[l][2][0] + up[l][1][2] * up[l][2][1]
-                    trc = diag + 2.0 * off
-                else:
-                    trc = sum(up[l][i][j] * up[m][j][i] for i in range(3) for j in range(3) if i + j) + (
-                        up[l][0][0] * up[m][0][0]
-                    )
-                term = wide[PAIR[l][m]] * trc
-                squares = term if squares is None else squares + term
+        s000 = cyc[0, 0, 0]
+        s001 = cyc[0, 0, 1] + u01 * s000
+        s011 = cyc[0, 1, 1] + u01 * cyc[0, 0, 1]
+        s111 = cyc[1, 1, 1] + u01 * cyc[0, 1, 1] + u01 * s011
+        s011 = s011 + u01 * s001
+        s111 = s111 + u01 * s011
+        a00 = cyc[0, 0, 2]
+        a01 = cyc[0, 1, 2] + u01 * a00
+        a11 = cyc[1, 1, 2] + u01 * cyc[0, 1, 2] + u01 * a01
+        b0 = cyc[0, 2, 2]
+        b1 = cyc[1, 2, 2] + u01 * b0
+        b2 = cyc[2, 2, 2] + u12 * b1 + u02 * b0
+        s002 = a00 + u12 * s001 + u02 * s000
+        s012 = a01 + u12 * s011 + u02 * s001
+        s112 = a11 + u12 * s111 + u02 * s011
+        b0 = b0 + u12 * a01 + u02 * a00
+        b1 = b1 + u12 * a11 + u02 * a01
+        s022 = b0 + u12 * s012 + u02 * s002
+        s122 = b1 + u12 * s112 + u02 * s012
+        s222 = b2 + u12 * b1 + u02 * b0 + u12 * s122 + u02 * s022
+        low = [
+            0.5 * (d0 * s000 + d1 * s011 + d2 * s022) - trace[0],
+            0.5 * (d0 * s001 + d1 * s111 + d2 * s122) - trace[1],
+            0.5 * (d0 * s002 + d1 * s112 + d2 * s222) - trace[2],
+        ]
+        three1, three2 = 3.0 * d1, 3.0 * d2
+        both2 = three2 * d2
+        squares = d0 * (
+            d0 * (d0 * (s000 * s000) + three1 * (s001 * s001) + three2 * (s002 * s002))
+            + three1 * (d1 * (s011 * s011) + (2.0 * d2) * (s012 * s012))
+            + both2 * (s022 * s022)
+        )
+        squares = squares + d1 * (
+            d1 * (d1 * (s111 * s111) + three2 * (s112 * s112)) + both2 * (s122 * s122)
+        )
+        squares = squares + (d2 * d2) * (d2 * (s222 * s222))
 
         def z_of(n):
             return DZR[n, x, own, :] + at_ends(C1[GEO + n], turn)
@@ -415,32 +516,23 @@
             rest_grad[2].append(z_of(n))
         div = first(*x_of(R, 7)) + first(*y_of(R, 8, x + 2)) + z_of(7)
         A = [R[n, x + 2, mid, :] for n in range(6)]
-        K = R[6, x + 2, mid, :]
-
-        mixed = [
-            [A[PAIR[i][0]] * inv(0, j) + A[PAIR[i][1]] * inv(1, j) + A[PAIR[i][2]] * inv(2, j) for j in range(3)]
-            for i in range(3)
-        ]
-        raised = [
-            inv(i, 0) * mixed[0][j] + inv(i, 1) * mixed[1][j] + inv(i, 2) * mixed[2][j]
-            for i, j in ((0, 0), (0, 1), (0, 2), (1, 1), (1, 2), (2, 2))
-        ]
-        a_sq = mixed[0][0] * mixed[0][0] + mixed[1][1] * mixed[1][1] + mixed[2][2] * mixed[2][2]
-        a_sq = a_sq + 2.0 * (
-            mixed[0][1] * mixed[1][0] + mixed[0][2] * mixed[2][0] + mixed[1][2] * mixed[2][1]
-        )
         chi_inv = 1.0 / chi
-        dchi_up = [inv(k, 0) * dchi[0] + inv(k, 1) * dchi[1] + inv(k, 2) * dchi[2] for k in range(3)]
+        gd = [d0 * low[0], d1 * low[1], d2 * low[2]]
+        dchi_up = [d0 * dchi[0], d1 * dchi[1], d2 * dchi[2]]
         grad_sq = dchi_up[0] * dchi[0] + dchi_up[1] * dchi[1] + dchi_up[2] * dchi[2]
         gd_trace = gd[0] * trace[0] + gd[1] * trace[1] + gd[2] * trace[2]
         gd_chi = gd[0] * dchi[0] + gd[1] * dchi[1] + gd[2] * dchi[2]
         ricci = 0.5 * (gd_trace - bend_g) + squares * (1.0 / 12.0) + 12.0 * div
         ham = (chi * ricci + 2.0 * (bend[0] - gd_chi) - 2.5 * grad_sq * chi_inv) * (1.0 / 144.0)
-        ham_out[x, own, :] = ham + (2.0 / 3.0) * (K * K) - a_sq
+        ham = ham + PT[12, x, own, :]
+        ham_out[x, own, :] = ham
 
         weight = 1.5 * chi_inv
         vec = [gd[l] + weight * dchi_up[l] for l in range(3)]
-        twice = [0.5 * raised[0], raised[1], raised[2], 0.5 * raised[3], raised[4], 0.5 * raised[5]]
+        vec[1] = vec[1] + u12 * vec[2]
+        vec[0] = vec[0] + u01 * vec[1] + u02 * vec[2]
+        twice = [PT[6 + n, x, own, :] for n in range(6)]
+        squared = None
         for i in range(3):
             total = (-2.0 / 3.0) * rest_grad[i][6]
             for j in range(3):
@@ -450,7 +542,10 @@
                 total = total - vec[l] * A[PAIR[l][i]]
             for n in range(6):
                 total = total - twice[n] * grads[i][1 + n]
-            mom_out[i, x, own, :] = total * (1.0 / 12.0)
+            total = total * (1.0 / 12.0)
+            mom_out[i, x, own, :] = total
+            squared = total * total if squared is None else squared + total * total
+        return ham * ham, squared
 
     def tally(x, b):
         own = pl.ds(pl.multiple_of(8 * b, 8), 8)
@@ -459,57 +554,17 @@
         ACC[0] += ham * ham
         ACC[1] += m0 * m0 + m1 * m1 + m2 * m2
 
-    def term(d, b):
-        rows = pl.ds(8 * b, 8)
-        return remote(CS.at[d, :, :, rows], CR.at[1 - d, :, :, rows], S_TERM + 4 * d + b, at(2 * d - 1, 0, 0))
-
-    terms = [[term(d, b) for b in range(BLOCKS)] for d in range(2)]
-
-    def send_terms(b):
-        mid = pl.ds(OWN + 8 * b, 8)
-        for d in range(2):
-            geo_xs[d][b].wait_recv()
-        for d in range(2):
-            halo = CX + 2 if d else 0
-            for k in range(2):
-                gu = inverse_of([F[1 + n, halo + k, mid, :] for n in range(6)])
-                chi = F[0, halo + k, mid, :]
-
-                def part(n):
-                    if d == 0:
-                        f0 = R[n, 2, mid, :]
-                        return -f0 if k == 0 else 8.0 * f0 - R[n, 3, mid, :]
-                    f7 = R[n, CX + 1, mid, :]
-                    return R[n, CX, mid, :] - 8.0 * f7 if k == 0 else f7
-
-                a = [part(n) for n in range(8)]
-                own = pl.ds(8 * b, 8)
-                CS[d, 0, k, own, :] = chi * a[7] * (1.0 / 12.0)
-                for i in range(3):
-                    value = gu[0] * a[PAIR[0][i]] + gu[1] * a[PAIR[1][i]] + gu[2] * a[PAIR[2][i]]
-                    if i == 0:
-                        value = value - (2.0 / 3.0) * a[6]
-                    CS[d, 1 + i, k, own, :] = value * (1.0 / 12.0)
-        for d in range(2):
-            terms[d][b].start()
-
     def inner(lo, hi):
         def body(i, _):
-            k = lax.rem(i, 8)
-            x, odd, last = 2 + k // 2, lax.rem(k, 2), i // 8
-            b = (1 - last) * (1 + odd) + last * 3 * odd
-            cell(x, b)
-            tally(x, b)
+            x, last = 2 + lax.rem(i, 4), i // 4
+            one, two = [cell(x, (1 - last) * (1 + n) + last * 3 * n) for n in range(2)]
+            ACC[0] += one[0] + two[0]
+            ACC[1] += one[1] + two[1]
             return 0
 
         lax.fori_loop(lo, hi, body, 0)
 
-    send_terms(0)
-    for step in [(-2, 0, 0), (2, 0, 0), (0, 0, -2), (0, 0, 2)]:
-        pl.semaphore_signal(near_sem, inc=1, device_id=at(*step), device_id_type=MESH)
     inner(0, 4)
-    send_terms(1)
-    inner(4, 8)
     send_terms(2)
     lax.fori_loop(0, PAIRS, open_y_geo, 0)
     x_rows(lambda k: k + 2, (0, 5))
@@ -518,21 +573,18 @@
     for s in range(2):
         y_ends(s)
     lax.fori_loop(0, PAIRS, open_y_dz, 0)
+    for copy in rest_ys:
+        copy.wait_recv()
+    lax.fori_loop(0, CX, open_y_rest, 0)
+    inner(4, 8)
     send_terms(3)
-    inner(8, 16)
     pl.semaphore_wait(near_sem, 4)
     for k in range(1, n_gy):
         pl.semaphore_signal(far_sem, inc=1, device_id=at(0, k, 0), device_id_type=MESH)
 
-    for copy in edge_xy + edge_xz + ends_x:
+    for copy in edge_xz + ends_x:
         copy.wait_recv()
     for sx in range(2):
-        for sy in range(2):
-            for c in range(GEO):
-                for k in range(2):
-                    layer = (CX + 2 if sx else 0) + k
-                    row = OWN + CY if sy else OWN - 2
-                    F[c, layer, row : row + 2, :] = XYR[sx, sy, c * 4 + k * 2 : c * 4 + k * 2 + 2, :]
         for v in range(2):
             CXE[sx, v] = change(XER[sx, 0, v], XER[sx, 1, v], XER[sx, 2, v])[0]
 
@@ -549,15 +601,29 @@
 
     for c in range(GEO):
         x_ends(c)
-    x_rows(lambda k: k + (k // 2) * (CX - 4), (0, 1, 2, 3, 4, 5))
-
-    def edge_cell(i, _):
-        k = i // BLOCKS
-        cell(k + (k // 2) * (CX - 4), lax.rem(i, BLOCKS))
-        return 0
-
-    lax.fori_loop(0, 4 * BLOCKS, edge_cell, 0)
-
+    x_rows(lambda k: k + (k // 2) * (CX - 4), (1, 2, 3, 4))
+
+    def outer(lo, hi):
+        def body(i, _):
+            k, last = lax.rem(i, 4), i // 4
+            for n in range(2):
+                cell(k + (k // 2) * (CX - 4), (1 - last) * (1 + n) + last * 3 * n)
+            return 0
+
+        lax.fori_loop(lo, hi, body, 0)
+
+    outer(0, 4)
+    for copy in edge_xy:
+        copy.wait_recv()
+    for sx in range(2):
+        for sy in range(2):
+            for c in range(GEO):
+                for k in range(2):
+                    layer = (CX + 2 if sx else 0) + k
+                    row = OWN + CY if sy else OWN - 2
+                    F[c, layer, row : row + 2, :] = XYR[sx, sy, c * 4 + k * 2 : c * 4 + k * 2 + 2, :]
+    x_rows(lambda k: k + (k // 2) * (CX - 4), (0, 5))
+    outer(4, 8)
     for d in range(2):
         for b in range(BLOCKS):
             terms[d][b].wait_recv()
@@ -649,11 +715,12 @@
                 pltpu.VMEM((3 * CZ, 2 * CZ), jnp.bfloat16),
                 vm(15, 8, CZ), vm(2, 15, 8, CZ), vm(15, 8, CZ), vm(GEO, 8, CZ),
                 vm(2, 2, 8, CZ), vm(2, 3, 2, 8, CZ), vm(2, 2, 8, CZ),
-                vm(2, 4, 2, CY, CZ), vm(2, 4, 2, CY, CZ),
+                vm(2, 4, 2, CY, CZ), vm(2, 4, 2, CY, CZ), vm(18, CX, CY, CZ),
                 vm(2, 2, CZ), vm(n_plane, 2, CZ), vm(sizes[0], 2, CZ),
-                pltpu.SemaphoreType.DMA((5,)),
+                pltpu.SemaphoreType.DMA((6,)),
                 pltpu.SemaphoreType.DMA((S_COUNT,)),
                 pltpu.SemaphoreType.DMA((S_COUNT,)),
+                pltpu.SemaphoreType.REGULAR,
                 pltpu.SemaphoreType.REGULAR,
                 pltpu.SemaphoreType.REGULAR,
             ],

time: 33.9 us -> 32.7 us (0.965)
  Pallas kernels: 33.2 us -> 32 us
    pallas_call x1, Pallas kernels: 32.3 us -> 31.1 us  [step(): pl.pallas_call(functools.partial(kernel, sizes), out_shape=(pltpu.VMEM((C...]
where the time goes in v4:
time: 32.7 us; the launch traced here: 32.6 us
  Pallas kernels  32 us (98%)
  between operations  0.64 us (2%)
    pallas_call x1, Pallas kernels, step(): pl.pallas_call(functools.partial(kernel, sizes), out_shape=(pltpu.VMEM((C...  31.1 us
    pallas_call x1, Pallas kernels, step(): pl.pallas_call(write_out, out_shape=(jax.ShapeDtypeStruct((CX, CY, CZ), f...  0.82 us

profile of v4, /device:TPU:1, one launch (start us, length us, event | category | flops | bytes accessed | tf_op | source)
XLA Modules:
  0.0 32.6 jit_solution(13669985427065992431)
XLA Ops:
  0.6 31.1 %shard_map.76 = (f32[8,32,128]{2,1,0:T(8,128)S(1)}, f32[3,8,32,128]{3,2,1,0:T(8,128)S(1)}, f32[1,2]{1,0:T(1,128)S(1)}) custom-call(f32[8,32,128]{2,1,0:T(8,128)} %chi_in.1, f32[6,8,32,128]{3,2,1,0:T(8,128)} %met_in.1, f32[6,8,32,128]{3,2,1,0:T(8,128)} %cur_in.1, f32[8,32,128]{2,1,0:T(8,128)} %trk_in.1, f32[3,8,32,128]{3,2,1,0:T(8,128)} %gam_in.1), custom_call_target="tpu_custom_call" | custom-call | tf_op jit(solution)/shard_map/pallas_call | solution.py:696
  31.8 0.8 %shard_map.77 = (f32[8,32,128]{2,1,0:T(8,128)}, f32[3,8,32,128]{3,2,1,0:T(8,128)}, f32[1,2]{1,0:T(1,128)}) custom-call(f32[8,32,128]{2,1,0:T(8,128)S(1)} %get-tuple-element.9.ham, f32[3,8,32,128]{3,2,1,0:T(8,128)S(1)} %get-tuple-element.10.mom, f32[1,2]{1,0:T(1,128)S(1)} %get-tuple-element.11.norm), custom_call_target="tpu_custom_call" | custom-call | tf_op jit(solution)/shard_map/pallas_call | solution.py:729

commit v5 on v4

--- a/solution.py
+++ b/solution.py
@@ -20,8 +20,10 @@
 X_REST = 8
 
 S_GEO_X, S_EDGE_XY, S_EDGE_YZ, S_EDGE_XZ = 0, 8, 12, 16
-S_GEO_Y, S_GEO_Z, S_REST_Y, S_REST_Z, S_TERM, S_ENDS_X = 20, 22, 24, 26, 28, 36
-S_SUM_A, S_SUM_B, S_COUNT = 38, 39, 40
+S_GEO_Y, S_GEO_Z, S_REST_Y, S_REST_Z, S_TERM = 20, 22, 24, 26, 28
+S_SUM_A, S_SUM_B, S_DIRECT, S_LINE, S_LEAD = 36, 37, 38, 39, 54
+LEADS = ((0, 0, 1),)
+S_COUNT = S_LEAD + len(LEADS)
 
 
 def lane_ids():
@@ -55,8 +57,8 @@
     F, R, DZ, DZZ, DZR, DX, DXX, ACC,
     YSG, YSR, YRG, YRR, YDZ, YZR, XYR, TAPS,
     ZP, ZPR, C1, C2, XE, XER, CXE,
-    CS, CR, PT, MINE, SUM_A, SUM_B,
-    load_sem, send_sem, recv_sem, two_sem, near_sem, far_sem,
+    CS, CR, PT, MINE, SUM_A, SUM_B, ALL,
+    load_sem, send_sem, recv_sem, two_sem, near_sem, far_sem, last_sem,
 ):
     n_gx, n_gy, n_gz = sizes
     ix, iy, iz = lax.axis_index("gx"), lax.axis_index("gy"), lax.axis_index("gz")
@@ -73,13 +75,15 @@
             device_id=device, device_id_type=MESH,
         )
 
-    loads = [
-        (chi_in, F.at[0, 2 : 2 + CX, OWN : OWN + CY]),
-        (met_in.at[0:3], F.at[1:4, 2 : 2 + CX, OWN : OWN + CY]),
-        (met_in.at[3:6], F.at[4:7, 2 : 2 + CX, OWN : OWN + CY]),
-        (cur_in, R.at[0:6, 2 : 2 + CX, OWN : OWN + CY]),
-        (trk_in, R.at[6, 2 : 2 + CX, OWN : OWN + CY]),
-        (gam_in, R.at[7:10, 2 : 2 + CX, OWN : OWN + CY]),
+    def block(src, dst, lo, hi):
+        if len(src.shape) == 3:
+            return src.at[lo:hi], dst.at[2 + lo : 2 + hi, OWN : OWN + CY]
+        return src.at[:, lo:hi], dst.at[:, 2 + lo : 2 + hi, OWN : OWN + CY]
+
+    layers = ((0, 2), (CX - 2, CX), (2, CX - 2))
+    loads = [block(src, dst, lo, hi) for lo, hi in layers for src, dst in ((chi_in, F.at[0]), (met_in, F.at[1:7]))]
+    loads += [
+        block(src, dst, 0, CX) for src, dst in ((cur_in, R.at[0:6]), (trk_in, R.at[6]), (gam_in, R.at[7:10]))
     ]
     loads = [pltpu.make_async_copy(s, d, load_sem.at[i]) for i, (s, d) in enumerate(loads)]
     for copy in loads:
@@ -107,6 +111,8 @@
     def packed(tiles):
         out = zero
         for t, tile in enumerate(tiles):
+            if tile is None:
+                continue
             turn = (4 * t + 2) % CZ
             out = jnp.where(lane4 == t, pltpu.roll(tile, turn, 1) if turn else tile, out)
         return out
@@ -136,7 +142,6 @@
         return remote(src, dst, S_GEO_X + 4 * d + b, at(2 * d - 1, 0, 0))
 
     geo_xs = [[geo_x(d, b) for b in range(BLOCKS)] for d in range(2)]
-    ends_x = [remote(XE.at[d], XER.at[1 - d, 0], S_ENDS_X + d, at(2 * d - 1, 0, 0)) for d in range(2)]
     geo_ys = [remote(YSG.at[d], YRG.at[1 - d], S_GEO_Y + d, at(0, 2 * d - 1, 0)) for d in range(2)]
     geo_zs = [remote(ZP.at[0:GEO], ZPR.at[1 - d, 0:GEO], S_GEO_Z + d, at(0, 0, 2 * d - 1)) for d in range(2)]
     rest_ys = [remote(YSR.at[d], YRR.at[1 - d], S_REST_Y + d, at(0, 2 * d - 1, 0)) for d in range(2)]
@@ -158,7 +163,7 @@
         for dy, dz in combos
     ]
     edge_xz = [
-        remote(XE.at[dx], XER.at[1 - dx, 2 - dz], S_EDGE_XZ + 2 * dx + dz, at(2 * dx - 1, 0, 2 * dz - 1))
+        remote(XE.at[dx, dz], XER.at[1 - dx, 1 - dz], S_EDGE_XZ + 2 * dx + dz, at(2 * dx - 1, 0, 2 * dz - 1))
         for dx, dz in combos
     ]
 
@@ -190,7 +195,7 @@
         pieces = jnp.concatenate([high, middle, low], axis=1)
         return jnp.dot(pieces, TAPS[:, 0:width], preferred_element_type=jnp.float32)
 
-    for copy in loads[:3]:
+    for copy in loads[:4]:
         copy.wait()
     pl.semaphore_wait(barrier, len(faces))
     for step in faces:
@@ -198,6 +203,8 @@
     for b in range(BLOCKS - 1):
         for d in range(2):
             geo_xs[d][b].start()
+    for copy in loads[4:6]:
+        copy.wait()
     for c in range(GEO):
         ZP[c] = packed(own_tiles(F, c))
     for copy in geo_zs:
@@ -205,15 +212,18 @@
     lax.fori_loop(0, PAIRS, pack_y_geo, 0)
     for s in range(2):
         YSG[s, 128:136, :] = packed([YSG[s, 8 * k : 8 * k + 8, :] for k in range(16)])
+        parts = []
         for v in range(2):
             out = zero
             for c in range(4 * v, min(4 * v + 4, GEO)):
                 turn = (32 * (c % 4) - 96 * s) % CZ
                 out = jnp.where(lane // 32 == c % 4, pltpu.roll(ZP[c], turn, 1) if turn else ZP[c], out)
-            XE[s, v] = out
-    for copy in geo_ys + ends_x:
+            parts.append(out)
+        XE[s, 0] = jnp.where(place < 2, pltpu.roll(parts[0], CZ - 2, 1), parts[1])
+        XE[s, 1] = jnp.where(place < 2, parts[0], pltpu.roll(parts[1], 2, 1))
+    for copy in geo_ys:
         copy.start()
-    for copy in loads[3:]:
+    for copy in loads[6:]:
         copy.wait()
     for n, c in enumerate(Z_REST):
         ZP[GEO + n] = packed(own_tiles(R, c))
@@ -249,13 +259,13 @@
 
     for c in range(GEO):
         z_geo(c)
+    for n in range(8):
+        z_rest(n)
     pl.semaphore_wait(two_sem, len(faces))
     for copy in edge_yz + edge_xz + [geo_xs[0][BLOCKS - 1], geo_xs[1][BLOCKS - 1]] + edge_xy:
         copy.start()
     for step in [(-2, 0, 0), (2, 0, 0), (0, 0, -2), (0, 0, 2)]:
         pl.semaphore_signal(near_sem, inc=1, device_id=at(*step), device_id_type=MESH)
-    for n in range(8):
-        z_rest(n)
     x_rows(lambda k: k + 2, (1, 2, 3, 4))
     def point(i, _):
         x = i // 2
@@ -337,7 +347,6 @@
 
     for copy in geo_zs:
         copy.wait_recv()
-    send_terms(0)
 
     def change(own, left, right):
         e = jnp.where(place < 2, left, right) - own
@@ -370,10 +379,6 @@
         copy.wait_recv()
     for n in range(8):
         C1[GEO + n] = change(ZP[GEO + n], ZPR[0, GEO + n], ZPR[1, GEO + n])[0]
-
-    send_terms(1)
-    for copy in geo_ys:
-        copy.wait_recv()
 
     def open_y_rest(x, _):
         rows = pl.ds(2 * x, 2)
@@ -565,7 +570,13 @@
         lax.fori_loop(lo, hi, body, 0)
 
     inner(0, 4)
-    send_terms(2)
+    send_terms(0)
+    pl.semaphore_wait(near_sem, 4)
+    twin = (ix, iy, iz + 1 - 2 * lax.rem(iz, 2))
+    for device in [at(0, k, 0) for k in range(1, n_gy)] + [twin]:
+        pl.semaphore_signal(far_sem, inc=1, device_id=device, device_id_type=MESH)
+    for copy in geo_ys:
+        copy.wait_recv()
     lax.fori_loop(0, PAIRS, open_y_geo, 0)
     x_rows(lambda k: k + 2, (0, 5))
     for copy in edge_yz:
@@ -576,43 +587,62 @@
     for copy in rest_ys:
         copy.wait_recv()
     lax.fori_loop(0, CX, open_y_rest, 0)
+    send_terms(1)
     inner(4, 8)
-    send_terms(3)
-    pl.semaphore_wait(near_sem, 4)
-    for k in range(1, n_gy):
-        pl.semaphore_signal(far_sem, inc=1, device_id=at(0, k, 0), device_id_type=MESH)
-
-    for copy in edge_xz + ends_x:
+    send_terms(2)
+    pl.semaphore_wait(far_sem, n_gy)
+    for k in range(1, n_gx):
+        pl.semaphore_signal(last_sem, inc=1, device_id=at(k, 0, 0), device_id_type=MESH)
+
+    for copy in edge_xz:
         copy.wait_recv()
-    for sx in range(2):
-        for v in range(2):
-            CXE[sx, v] = change(XER[sx, 0, v], XER[sx, 1, v], XER[sx, 2, v])[0]
-
-    def x_ends(c):
+    def x_changes(half):
+        for sx in range(2):
+            left, right = XER[sx, 0], XER[sx, 1]
+            lefts = left, pltpu.roll(left, CZ - 2, 1)
+            rights = pltpu.roll(right, 2, 1), right
+            for v in range(2):
+                own = packed([
+                    F[c, (CX + 2) * sx + xi, OWN + 8 * b : OWN + 8 * b + 8, :] if b // 2 == half else None
+                    for c in range(4 * v, min(4 * v + 4, GEO)) for xi in range(2) for b in range(BLOCKS)
+                ])
+                CXE[sx, v] = change(own, lefts[v], rights[v])[0]
+
+    def x_ends(c, half):
+        rows = slice(OWN + half * CY // 2, OWN + half * CY // 2 + CY // 2)
         for side in range(2):
             layers = slice(CX + 2, CX + 4) if side else slice(0, 2)
-            out = along_z(F[c, layers, own_rows[1], :].reshape(2 * CY, CZ), CZ)
+            out = along_z(F[c, layers, rows, :].reshape(CY, CZ), CZ)
             changed = CXE[side, c // 4]
             for xi in range(2):
-                for b in range(BLOCKS):
-                    turn = CZ - 2 - 32 * (c % 4) - 4 * (BLOCKS * xi + b)
-                    row = CY * xi + 8 * b
-                    DZ[c, layers.start + xi, pl.ds(OWN + 8 * b, 8), :] = out[row : row + 8] + at_ends(changed, turn)
-
+                for b in range(2):
+                    turn = CZ - 2 - 32 * (c % 4) - 4 * (BLOCKS * xi + 2 * half + b)
+                    row = CY // 2 * xi + 8 * b
+                    target = slice(rows.start + 8 * b, rows.start + 8 * b + 8)
+                    DZ[c, layers.start + xi, target, :] = out[row : row + 8] + at_ends(changed, turn)
+
+    def x_edge_rows(*tiles):
+        x_rows(lambda k: k + (k // 2) * (CX - 4), tiles)
+
+    def outer(b):
+        def body(i, _):
+            for n in range(2):
+                cell((CX - 2) * i + n, b)
+            return 0
+
+        lax.fori_loop(0, 2, body, 0)
+
+    x_changes(0)
     for c in range(GEO):
-        x_ends(c)
-    x_rows(lambda k: k + (k // 2) * (CX - 4), (1, 2, 3, 4))
-
-    def outer(lo, hi):
-        def body(i, _):
-            k, last = lax.rem(i, 4), i // 4
-            for n in range(2):
-                cell(k + (k // 2) * (CX - 4), (1 - last) * (1 + n) + last * 3 * n)
-            return 0
-
-        lax.fori_loop(lo, hi, body, 0)
-
-    outer(0, 4)
+        x_ends(c, 0)
+    x_edge_rows(1, 2, 3)
+    send_terms(3)
+    outer(1)
+    x_changes(1)
+    for c in range(GEO):
+        x_ends(c, 1)
+    x_edge_rows(4)
+    outer(2)
     for copy in edge_xy:
         copy.wait_recv()
     for sx in range(2):
@@ -622,8 +652,9 @@
                     layer = (CX + 2 if sx else 0) + k
                     row = OWN + CY if sy else OWN - 2
                     F[c, layer, row : row + 2, :] = XYR[sx, sy, c * 4 + k * 2 : c * 4 + k * 2 + 2, :]
-    x_rows(lambda k: k + (k // 2) * (CX - 4), (0, 5))
-    outer(4, 8)
+    x_edge_rows(0, 5)
+    outer(0)
+    outer(3)
     for d in range(2):
         for b in range(BLOCKS):
             terms[d][b].wait_recv()
@@ -639,40 +670,94 @@
         return 0
 
     lax.fori_loop(0, 4, finish, 0)
-    MINE[0, 0:1, :] = jnp.sum(ACC[0], axis=0, keepdims=True)
-    MINE[0, 1:2, :] = jnp.sum(ACC[1], axis=0, keepdims=True)
-    rank_a = iy * n_gz + iz
-    n_plane = n_gy * n_gz
+    halves = [jnp.sum(ACC[n], axis=0, keepdims=True) for n in range(2)]
+    halves = [half + pltpu.roll(half, CZ // 2, 1) for half in halves]
+    lower = lax.broadcasted_iota(jnp.int32, (1, CZ), 1) < CZ // 2
+    MINE[0] = jnp.where(lower, halves[0], halves[1])
+    n_chips = n_gz // 2
+    n_plane, n_line = n_gy * n_chips, 2 * n_gx
+    core = lax.rem(iz, 2)
+    rank_a, rank_b = iy * n_chips + iz // 2, 2 * ix + core
     SUM_A[rank_a] = MINE[0]
-    pl.semaphore_wait(far_sem, n_gy - 1)
-    for dy in range(n_gy):
-        for dz in range(n_gz):
-            if dy or dz:
-                remote(MINE.at[0], SUM_A.at[rank_a], S_SUM_A, at(0, dy, dz)).start()
+    pl.semaphore_wait(last_sem, n_gx - 1)
+    def is_at(device, other):
+        return (device[0] == other[0]) & (device[1] == other[1]) & (device[2] == other[2])
+
+    def leads(device):
+        return functools.reduce(jnp.logical_or, [is_at(device, lead) for lead in LEADS])
+
+    own = rank_b * n_plane + rank_a
+    leading = leads((ix, iy, iz))
+    ALL[own] = MINE[0]
+    direct = []
+    for lead in LEADS:
+        copy = pltpu.make_async_remote_copy(
+            src_ref=MINE.at[0], dst_ref=ALL.at[own], send_sem=send_sem.at[S_LEAD + len(direct)],
+            recv_sem=recv_sem.at[S_DIRECT], device_id=lead, device_id_type=MESH,
+        )
+        direct.append((copy, jnp.logical_not(is_at((ix, iy, iz), lead))))
+    for copy, wanted in direct:
+        pl.when(wanted)(copy.start)
+
+    far_first = sorted(
+        ((dy, k) for dy in range(n_gy) for k in range(n_chips) if dy or k),
+        key=lambda p: -min(p[0], n_gy - p[0]) - min(p[1], n_chips - p[1]),
+    )
+    for dy, k in far_first:
+        remote(MINE.at[0], SUM_A.at[rank_a], S_SUM_A, at(0, dy, 2 * k)).start()
     others = remote(SUM_A.at[pl.ds(0, n_plane - 1)], SUM_A.at[pl.ds(0, n_plane - 1)], S_SUM_A, at(0, 1, 0))
     others.wait_recv()
     total = SUM_A[0]
     for k in range(1, n_plane):
         total = total + SUM_A[k]
     MINE[1] = total
-    SUM_B[ix] = total
-    for dx in range(1, n_gx):
-        remote(MINE.at[1], SUM_B.at[ix], S_SUM_B, at(dx, 0, 0)).start()
-    along = remote(SUM_B.at[pl.ds(0, n_gx - 1)], SUM_B.at[pl.ds(0, n_gx - 1)], S_SUM_B, at(1, 0, 0))
-    along.wait_recv()
-    total = SUM_B[0]
-    for j in range(1, n_gx):
-        total = total + SUM_B[j]
-    sums = jnp.sum(total, axis=1, keepdims=True)
-    cells = float(CX * CY * CZ * n_gx * n_gy * n_gz)
-    column = lax.broadcasted_iota(jnp.int32, (1, 2), 1)
-    ham_sum = jnp.broadcast_to(sums[0:1], (1, 2))
-    mom_sum = jnp.broadcast_to(sums[1:2], (1, 2))
-    norm_out[...] = jnp.sqrt(jnp.where(column == 0, ham_sum / cells, mom_sum / (3.0 * cells)))
-
-    sent = geo_ys + geo_zs + rest_ys + rest_zs + edge_xy + edge_yz + edge_xz + ends_x + [others, along]
+    SUM_B[rank_b] = total
+    line = []
+    for dx in sorted(range(n_gx), key=lambda k: -min(k, n_gx - k)):
+        for z in [zs[0], twin[2]] if dx else [twin[2]]:
+            copy = pltpu.make_async_remote_copy(
+                src_ref=MINE.at[1], dst_ref=SUM_B.at[rank_b], send_sem=send_sem.at[S_LINE + len(line)],
+                recv_sem=recv_sem.at[S_SUM_B], device_id=(xs[dx], iy, z), device_id_type=MESH,
+            )
+            line.append((copy, jnp.logical_not(leads((xs[dx], iy, z)))))
+    for copy, wanted in line:
+        pl.when(wanted)(copy.start)
+
+    def norms(total):
+        cells = float(CX * CY * CZ * n_gx * n_gy * n_gz)
+        column = lax.broadcasted_iota(jnp.int32, (1, 2), 1)
+        ham_sum = jnp.sum(jnp.where(lower, total, 0.0), axis=1, keepdims=True)
+        mom_sum = jnp.sum(jnp.where(lower, 0.0, total), axis=1, keepdims=True)
+        ham_sum, mom_sum = jnp.broadcast_to(ham_sum, (1, 2)), jnp.broadcast_to(mom_sum, (1, 2))
+        norm_out[...] = jnp.sqrt(jnp.where(column == 0, ham_sum / cells, mom_sum / (3.0 * cells)))
+
+    @pl.when(jnp.logical_not(leading))
+    def _():
+        whole = SUM_B.at[pl.ds(0, n_line - 1)]
+        remote(whole, whole, S_SUM_B, twin).wait_recv()
+        total = SUM_B[0]
+        for j in range(1, n_line):
+            total = total + SUM_B[j]
+        norms(total)
+
+    @pl.when(leading)
+    def _():
+        whole = ALL.at[pl.ds(0, n_line * n_plane - 1)]
+        remote(whole, whole, S_DIRECT, twin).wait_recv()
+
+        def group(j):
+            rows = ALL[n_plane * j]
+            for k in range(1, n_plane):
+                rows = rows + ALL[n_plane * j + k]
+            return rows
+
+        norms(lax.fori_loop(1, n_line, lambda j, total: total + group(j), group(0)))
+
+    sent = geo_ys + geo_zs + rest_ys + rest_zs + edge_xy + edge_yz + edge_xz + [others]
     for copy in [c for row in geo_xs + terms for c in row] + sent:
         copy.wait_send()
+    for copy, wanted in line + direct:
+        pl.when(wanted)(copy.wait_send)
 
 
 def write_out(ham, mom, norm, ham_out, mom_out, norm_out, sems):
@@ -688,7 +773,6 @@
 
 def solution(mesh):
     sizes = (mesh.shape["gx"], mesh.shape["gy"], mesh.shape["gz"])
-    n_plane = sizes[1] * sizes[2]
     f32 = jnp.float32
 
     def step(chi, met, cur, trk, gam):
@@ -714,12 +798,13 @@
                 vm(2, 128, CZ), vm(2, 2, 8, CZ), vm(2, 2, 32, CZ),
                 pltpu.VMEM((3 * CZ, 2 * CZ), jnp.bfloat16),
                 vm(15, 8, CZ), vm(2, 15, 8, CZ), vm(15, 8, CZ), vm(GEO, 8, CZ),
-                vm(2, 2, 8, CZ), vm(2, 3, 2, 8, CZ), vm(2, 2, 8, CZ),
+                vm(2, 2, 8, CZ), vm(2, 2, 8, CZ), vm(2, 2, 8, CZ),
                 vm(2, 4, 2, CY, CZ), vm(2, 4, 2, CY, CZ), vm(18, CX, CY, CZ),
-                vm(2, 2, CZ), vm(n_plane, 2, CZ), vm(sizes[0], 2, CZ),
-                pltpu.SemaphoreType.DMA((6,)),
+                vm(2, 1, CZ), vm(sizes[1] * sizes[2] // 2, 1, CZ), vm(2 * sizes[0], 1, CZ), vm(sizes[0] * sizes[1] * sizes[2], 1, CZ),
+                pltpu.SemaphoreType.DMA((9,)),
                 pltpu.SemaphoreType.DMA((S_COUNT,)),
                 pltpu.SemaphoreType.DMA((S_COUNT,)),
+                pltpu.SemaphoreType.REGULAR,
                 pltpu.SemaphoreType.REGULAR,
                 pltpu.SemaphoreType.REGULAR,
                 pltpu.SemaphoreType.REGULAR,

time: 32.7 us -> 31 us (0.948)
  Pallas kernels: 32 us -> 30.1 us
    pallas_call x1, Pallas kernels: 31.1 us -> 29.3 us  [step(): pl.pallas_call(functools.partial(kernel, sizes), out_shape=(pltpu.VMEM((C...]
where the time goes in v5:
time: 31 us; the launch traced here: 30.7 us
  Pallas kernels  30.1 us (97%)
  between operations  0.64 us (2%)
    pallas_call x1, Pallas kernels, step(): pl.pallas_call(functools.partial(kernel, sizes), out_shape=(pltpu.VMEM((C...  29.3 us
    pallas_call x1, Pallas kernels, step(): pl.pallas_call(write_out, out_shape=(jax.ShapeDtypeStruct((CX, CY, CZ), f...  0.82 us

profile of v5, /device:TPU:1, one launch (start us, length us, event | category | flops | bytes accessed | tf_op | source)
XLA Modules:
  0.0 30.7 jit_solution(7306896614916301783)
XLA Ops:
  0.6 29.3 %shard_map.76 = (f32[8,32,128]{2,1,0:T(8,128)S(1)}, f32[3,8,32,128]{3,2,1,0:T(8,128)S(1)}, f32[1,2]{1,0:T(1,128)S(1)}) custom-call(f32[8,32,128]{2,1,0:T(8,128)} %chi_in.1, f32[6,8,32,128]{3,2,1,0:T(8,128)} %met_in.1, f32[6,8,32,128]{3,2,1,0:T(8,128)} %cur_in.1, f32[8,32,128]{2,1,0:T(8,128)} %trk_in.1, f32[3,8,32,128]{3,2,1,0:T(8,128)} %gam_in.1), custom_call_target="tpu_custom_call" | custom-call | tf_op jit(solution)/shard_map/pallas_call | solution.py:780
  29.9 0.8 %shard_map.77 = (f32[8,32,128]{2,1,0:T(8,128)}, f32[3,8,32,128]{3,2,1,0:T(8,128)}, f32[1,2]{1,0:T(1,128)}) custom-call(f32[8,32,128]{2,1,0:T(8,128)S(1)} %get-tuple-element.9.ham, f32[3,8,32,128]{3,2,1,0:T(8,128)S(1)} %get-tuple-element.10.mom, f32[1,2]{1,0:T(1,128)S(1)} %get-tuple-element.11.norm), custom_call_target="tpu_custom_call" | custom-call | tf_op jit(solution)/shard_map/pallas_call | solution.py:814

commit v6 on v5

--- a/solution.py
+++ b/solution.py
@@ -19,11 +19,9 @@
 Z_REST = (0, 1, 2, 3, 4, 5, 6, 9)
 X_REST = 8
 
-S_GEO_X, S_EDGE_XY, S_EDGE_YZ, S_EDGE_XZ = 0, 8, 12, 16
-S_GEO_Y, S_GEO_Z, S_REST_Y, S_REST_Z, S_TERM = 20, 22, 24, 26, 28
-S_SUM_A, S_SUM_B, S_DIRECT, S_LINE, S_LEAD = 36, 37, 38, 39, 54
-LEADS = ((0, 0, 1),)
-S_COUNT = S_LEAD + len(LEADS)
+S_GEO_Y, S_GEO_Z, S_REST_Y, S_REST_Z, S_EDGE_XY, S_EDGE_YZ, S_EDGE_XZ, S_TERM = range(8)
+S_SUM_A, S_SUM_B, S_DIRECT, S_GEO_X = 8, 9, 10, 11
+LEAD = (0, 0, 1)
 
 
 def lane_ids():
@@ -69,11 +67,19 @@
     def at(dx, dy, dz):
         return xs[dx], ys[dy], zs[dz]
 
-    def remote(src, dst, place, device):
+    def remote(src, dst, place, device, part=0):
         return pltpu.make_async_remote_copy(
-            src_ref=src, dst_ref=dst, send_sem=send_sem.at[place], recv_sem=recv_sem.at[place],
+            src_ref=src, dst_ref=dst, send_sem=send_sem.at[place], recv_sem=recv_sem.at[place + part],
             device_id=device, device_id_type=MESH,
         )
+
+    def group(whole, place, part=0):
+        return remote(whole, whole, place, at(1, 0, 0), part)
+
+    barrier = pltpu.get_barrier_semaphore()
+    faces = [(-1, 0, 0), (1, 0, 0), (0, -1, 0), (0, 1, 0), (0, 0, -1), (0, 0, 1)]
+    for step in faces:
+        pl.semaphore_signal(barrier, inc=1, device_id=at(*step), device_id_type=MESH)
 
     def block(src, dst, lo, hi):
         if len(src.shape) == 3:
@@ -85,14 +91,9 @@
     loads += [
         block(src, dst, 0, CX) for src, dst in ((cur_in, R.at[0:6]), (trk_in, R.at[6]), (gam_in, R.at[7:10]))
     ]
-    loads = [pltpu.make_async_copy(s, d, load_sem.at[i]) for i, (s, d) in enumerate(loads)]
+    loads = [pltpu.make_async_copy(s, d, load_sem.at[(i > 3) + (i > 5)]) for i, (s, d) in enumerate(loads)]
     for copy in loads:
         copy.start()
-
-    barrier = pltpu.get_barrier_semaphore()
-    faces = [(-1, 0, 0), (1, 0, 0), (0, -1, 0), (0, 1, 0), (0, 0, -1), (0, 0, 1)]
-    for step in faces:
-        pl.semaphore_signal(barrier, inc=1, device_id=at(*step), device_id_type=MESH)
 
     lane = lane_ids()
     lane4, place = lane // 4, lax.rem(lane, 4)
@@ -139,31 +140,31 @@
         rows = pl.ds(OWN + 8 * b, 8)
         src = F.at[0:GEO, pl.ds(CX if d else 2, 2), rows]
         dst = F.at[0:GEO, pl.ds(0 if d else CX + 2, 2), rows]
-        return remote(src, dst, S_GEO_X + 4 * d + b, at(2 * d - 1, 0, 0))
+        return remote(src, dst, S_GEO_X, at(2 * d - 1, 0, 0), b)
 
     geo_xs = [[geo_x(d, b) for b in range(BLOCKS)] for d in range(2)]
-    geo_ys = [remote(YSG.at[d], YRG.at[1 - d], S_GEO_Y + d, at(0, 2 * d - 1, 0)) for d in range(2)]
-    geo_zs = [remote(ZP.at[0:GEO], ZPR.at[1 - d, 0:GEO], S_GEO_Z + d, at(0, 0, 2 * d - 1)) for d in range(2)]
-    rest_ys = [remote(YSR.at[d], YRR.at[1 - d], S_REST_Y + d, at(0, 2 * d - 1, 0)) for d in range(2)]
+    geo_ys = [remote(YSG.at[d], YRG.at[1 - d], S_GEO_Y, at(0, 2 * d - 1, 0)) for d in range(2)]
+    geo_zs = [remote(ZP.at[0:GEO], ZPR.at[1 - d, 0:GEO], S_GEO_Z, at(0, 0, 2 * d - 1)) for d in range(2)]
+    rest_ys = [remote(YSR.at[d], YRR.at[1 - d], S_REST_Y, at(0, 2 * d - 1, 0)) for d in range(2)]
     rest_zs = [
-        remote(ZP.at[GEO : GEO + 8], ZPR.at[1 - d, GEO : GEO + 8], S_REST_Z + d, at(0, 0, 2 * d - 1)) for d in range(2)
+        remote(ZP.at[GEO : GEO + 8], ZPR.at[1 - d, GEO : GEO + 8], S_REST_Z, at(0, 0, 2 * d - 1)) for d in range(2)
     ]
     combos = [(a, b) for a in range(2) for b in range(2)]
     edge_xy = [
         remote(
-            YSG.at[dy, pl.ds(96 if dx else 0, 32)], XYR.at[1 - dx, 1 - dy], S_EDGE_XY + 2 * dx + dy,
+            YSG.at[dy, pl.ds(96 if dx else 0, 32)], XYR.at[1 - dx, 1 - dy], S_EDGE_XY,
             at(2 * dx - 1, 2 * dy - 1, 0),
         )
         for dx, dy in combos
     ]
     edge_yz = [
         remote(
-            YSG.at[dy, 128:136], YZR.at[1 - dz, 1 - dy], S_EDGE_YZ + 2 * dy + dz, at(0, 2 * dy - 1, 2 * dz - 1)
+            YSG.at[dy, 128:136], YZR.at[1 - dz, 1 - dy], S_EDGE_YZ, at(0, 2 * dy - 1, 2 * dz - 1)
         )
         for dy, dz in combos
     ]
     edge_xz = [
-        remote(XE.at[dx, dz], XER.at[1 - dx, 1 - dz], S_EDGE_XZ + 2 * dx + dz, at(2 * dx - 1, 0, 2 * dz - 1))
+        remote(XE.at[dx, dz], XER.at[1 - dx, 1 - dz], S_EDGE_XZ, at(2 * dx - 1, 0, 2 * dz - 1))
         for dx, dz in combos
     ]
 
@@ -195,16 +196,21 @@
         pieces = jnp.concatenate([high, middle, low], axis=1)
         return jnp.dot(pieces, TAPS[:, 0:width], preferred_element_type=jnp.float32)
 
-    for copy in loads[:4]:
-        copy.wait()
+    all_geo_x = group(F.at[:, 2 : 2 + CX // 2, OWN : OWN + CY], S_GEO_X)
+    all_geo_y, all_rest_y = group(YRG, S_GEO_Y), group(YRR, S_REST_Y)
+    all_geo_z, all_rest_z = group(ZPR.at[:, 0:GEO], S_GEO_Z), group(ZPR.at[:, GEO : GEO + 8], S_REST_Z)
+    all_xy, all_yz, all_xz = group(XYR, S_EDGE_XY), group(YZR, S_EDGE_YZ), group(XER, S_EDGE_XZ)
+    all_terms = group(CR, S_TERM)
+
+    half = F.at[:, 2 : 2 + CX // 2, OWN : OWN + CY]
+    pltpu.make_async_copy(half, half, load_sem.at[0]).wait()
     pl.semaphore_wait(barrier, len(faces))
     for step in faces:
         pl.semaphore_signal(two_sem, inc=1, device_id=at(*step), device_id_type=MESH)
     for b in range(BLOCKS - 1):
         for d in range(2):
             geo_xs[d][b].start()
-    for copy in loads[4:6]:
-        copy.wait()
+    pltpu.make_async_copy(half, half, load_sem.at[1]).wait()
     for c in range(GEO):
         ZP[c] = packed(own_tiles(F, c))
     for copy in geo_zs:
@@ -223,8 +229,8 @@
         XE[s, 1] = jnp.where(place < 2, parts[0], pltpu.roll(parts[1], 2, 1))
     for copy in geo_ys:
         copy.start()
-    for copy in loads[6:]:
-        copy.wait()
+    whole = R.at[:, 2 : 2 + CX, OWN : OWN + CY]
+    pltpu.make_async_copy(whole, whole, load_sem.at[2]).wait()
     for n, c in enumerate(Z_REST):
         ZP[GEO + n] = packed(own_tiles(R, c))
     for copy in rest_zs:
@@ -313,14 +319,13 @@
     lax.fori_loop(0, 2 * CX, point, 0)
     def term(d, b):
         rows = pl.ds(8 * b, 8)
-        return remote(CS.at[d, :, :, rows], CR.at[1 - d, :, :, rows], S_TERM + 4 * d + b, at(2 * d - 1, 0, 0))
+        return remote(CS.at[d, :, :, rows], CR.at[1 - d, :, :, rows], S_TERM, at(2 * d - 1, 0, 0))
 
     terms = [[term(d, b) for b in range(BLOCKS)] for d in range(2)]
 
     def send_terms(b):
         mid = pl.ds(OWN + 8 * b, 8)
-        for d in range(2):
-            geo_xs[d][b].wait_recv()
+        group(F.at[:, 2 : 2 + CX // 2, OWN : OWN + 8], S_GEO_X, b).wait_recv()
         for d in range(2):
             halo = CX + 2 if d else 0
             for k in range(2):
@@ -345,8 +350,7 @@
         for d in range(2):
             terms[d][b].start()
 
-    for copy in geo_zs:
-        copy.wait_recv()
+    all_geo_z.wait_recv()
 
     def change(own, left, right):
         e = jnp.where(place < 2, left, right) - own
@@ -375,8 +379,7 @@
         return 0
 
     lax.fori_loop(0, 2, z_ends, 0)
-    for copy in rest_zs:
-        copy.wait_recv()
+    all_rest_z.wait_recv()
     for n in range(8):
         C1[GEO + n] = change(ZP[GEO + n], ZPR[0, GEO + n], ZPR[1, GEO + n])[0]
 
@@ -575,17 +578,14 @@
     twin = (ix, iy, iz + 1 - 2 * lax.rem(iz, 2))
     for device in [at(0, k, 0) for k in range(1, n_gy)] + [twin]:
         pl.semaphore_signal(far_sem, inc=1, device_id=device, device_id_type=MESH)
-    for copy in geo_ys:
-        copy.wait_recv()
+    all_geo_y.wait_recv()
     lax.fori_loop(0, PAIRS, open_y_geo, 0)
     x_rows(lambda k: k + 2, (0, 5))
-    for copy in edge_yz:
-        copy.wait_recv()
+    all_yz.wait_recv()
     for s in range(2):
         y_ends(s)
     lax.fori_loop(0, PAIRS, open_y_dz, 0)
-    for copy in rest_ys:
-        copy.wait_recv()
+    all_rest_y.wait_recv()
     lax.fori_loop(0, CX, open_y_rest, 0)
     send_terms(1)
     inner(4, 8)
@@ -594,8 +594,7 @@
     for k in range(1, n_gx):
         pl.semaphore_signal(last_sem, inc=1, device_id=at(k, 0, 0), device_id_type=MESH)
 
-    for copy in edge_xz:
-        copy.wait_recv()
+    all_xz.wait_recv()
     def x_changes(half):
         for sx in range(2):
             left, right = XER[sx, 0], XER[sx, 1]
@@ -643,8 +642,7 @@
         x_ends(c, 1)
     x_edge_rows(4)
     outer(2)
-    for copy in edge_xy:
-        copy.wait_recv()
+    all_xy.wait_recv()
     for sx in range(2):
         for sy in range(2):
             for c in range(GEO):
@@ -655,9 +653,7 @@
     x_edge_rows(0, 5)
     outer(0)
     outer(3)
-    for d in range(2):
-        for b in range(BLOCKS):
-            terms[d][b].wait_recv()
+    all_terms.wait_recv()
 
     def finish(k, _):
         side, sub = k // 2, lax.rem(k, 2)
@@ -680,24 +676,14 @@
     rank_a, rank_b = iy * n_chips + iz // 2, 2 * ix + core
     SUM_A[rank_a] = MINE[0]
     pl.semaphore_wait(last_sem, n_gx - 1)
-    def is_at(device, other):
-        return (device[0] == other[0]) & (device[1] == other[1]) & (device[2] == other[2])
-
-    def leads(device):
-        return functools.reduce(jnp.logical_or, [is_at(device, lead) for lead in LEADS])
+    def is_lead(device):
+        return (device[0] == LEAD[0]) & (device[1] == LEAD[1]) & (device[2] == LEAD[2])
 
     own = rank_b * n_plane + rank_a
-    leading = leads((ix, iy, iz))
+    leading = is_lead((ix, iy, iz))
     ALL[own] = MINE[0]
-    direct = []
-    for lead in LEADS:
-        copy = pltpu.make_async_remote_copy(
-            src_ref=MINE.at[0], dst_ref=ALL.at[own], send_sem=send_sem.at[S_LEAD + len(direct)],
-            recv_sem=recv_sem.at[S_DIRECT], device_id=lead, device_id_type=MESH,
-        )
-        direct.append((copy, jnp.logical_not(is_at((ix, iy, iz), lead))))
-    for copy, wanted in direct:
-        pl.when(wanted)(copy.start)
+    direct = remote(MINE.at[0], ALL.at[own], S_DIRECT, LEAD)
+    pl.when(jnp.logical_not(leading))(direct.start)
 
     far_first = sorted(
         ((dy, k) for dy in range(n_gy) for k in range(n_chips) if dy or k),
@@ -712,16 +698,10 @@
         total = total + SUM_A[k]
     MINE[1] = total
     SUM_B[rank_b] = total
-    line = []
     for dx in sorted(range(n_gx), key=lambda k: -min(k, n_gx - k)):
         for z in [zs[0], twin[2]] if dx else [twin[2]]:
-            copy = pltpu.make_async_remote_copy(
-                src_ref=MINE.at[1], dst_ref=SUM_B.at[rank_b], send_sem=send_sem.at[S_LINE + len(line)],
-                recv_sem=recv_sem.at[S_SUM_B], device_id=(xs[dx], iy, z), device_id_type=MESH,
-            )
-            line.append((copy, jnp.logical_not(leads((xs[dx], iy, z)))))
-    for copy, wanted in line:
-        pl.when(wanted)(copy.start)
+            copy = remote(MINE.at[1], SUM_B.at[rank_b], S_SUM_B, (xs[dx], iy, z))
+            pl.when(jnp.logical_not(is_lead((xs[dx], iy, z))))(copy.start)
 
     def norms(total):
         cells = float(CX * CY * CZ * n_gx * n_gy * n_gz)
@@ -733,8 +713,7 @@
 
     @pl.when(jnp.logical_not(leading))
     def _():
-        whole = SUM_B.at[pl.ds(0, n_line - 1)]
-        remote(whole, whole, S_SUM_B, twin).wait_recv()
+        group(SUM_B.at[0 : n_line - 1], S_SUM_B).wait_recv()
         total = SUM_B[0]
         for j in range(1, n_line):
             total = total + SUM_B[j]
@@ -742,22 +721,22 @@
 
     @pl.when(leading)
     def _():
-        whole = ALL.at[pl.ds(0, n_line * n_plane - 1)]
-        remote(whole, whole, S_DIRECT, twin).wait_recv()
-
-        def group(j):
+        group(ALL.at[0 : n_line * n_plane - 1], S_DIRECT).wait_recv()
+
+        def rows_of(j):
             rows = ALL[n_plane * j]
             for k in range(1, n_plane):
                 rows = rows + ALL[n_plane * j + k]
             return rows
 
-        norms(lax.fori_loop(1, n_line, lambda j, total: total + group(j), group(0)))
-
-    sent = geo_ys + geo_zs + rest_ys + rest_zs + edge_xy + edge_yz + edge_xz + [others]
-    for copy in [c for row in geo_xs + terms for c in row] + sent:
-        copy.wait_send()
-    for copy, wanted in line + direct:
-        pl.when(wanted)(copy.wait_send)
+        norms(lax.fori_loop(1, n_line, lambda j, total: total + rows_of(j), rows_of(0)))
+
+    for sent in (all_geo_x, all_geo_y, all_geo_z, all_rest_y, all_rest_z, all_xy, all_yz, all_xz, all_terms, others):
+        sent.wait_send()
+    pl.when(jnp.logical_not(leading))(direct.wait_send)
+    fewer = jnp.logical_not(leading) & (iy == LEAD[1]) & (iz // 2 == LEAD[2] // 2)
+    pl.when(fewer)(group(SUM_B.at[0 : n_line - 2], S_SUM_B).wait_send)
+    pl.when(jnp.logical_not(fewer))(group(SUM_B.at[0 : n_line - 1], S_SUM_B).wait_send)
 
 
 def write_out(ham, mom, norm, ham_out, mom_out, norm_out, sems):
@@ -801,9 +780,9 @@
                 vm(2, 2, 8, CZ), vm(2, 2, 8, CZ), vm(2, 2, 8, CZ),
                 vm(2, 4, 2, CY, CZ), vm(2, 4, 2, CY, CZ), vm(18, CX, CY, CZ),
                 vm(2, 1, CZ), vm(sizes[1] * sizes[2] // 2, 1, CZ), vm(2 * sizes[0], 1, CZ), vm(sizes[0] * sizes[1] * sizes[2], 1, CZ),
-                pltpu.SemaphoreType.DMA((9,)),
-                pltpu.SemaphoreType.DMA((S_COUNT,)),
-                pltpu.SemaphoreType.DMA((S_COUNT,)),
+                pltpu.SemaphoreType.DMA((3,)),
+                pltpu.SemaphoreType.DMA((S_GEO_X + 1,)),
+                pltpu.SemaphoreType.DMA((S_GEO_X + BLOCKS,)),
                 pltpu.SemaphoreType.REGULAR,
                 pltpu.SemaphoreType.REGULAR,
                 pltpu.SemaphoreType.REGULAR,

time: 31 us -> 30.1 us (0.971)
  Pallas kernels: 30.1 us -> 29.2 us
    pallas_call x1, Pallas kernels: 29.3 us -> 28.4 us  [step(): pl.pallas_call(functools.partial(kernel, sizes), out_shape=(pltpu.VMEM((C...]
where the time goes in v6:
time: 30.1 us; the launch traced here: 29.8 us
  Pallas kernels  29.2 us (97%)
  between operations  0.64 us (2%)
    pallas_call x1, Pallas kernels, step(): pl.pallas_call(functools.partial(kernel, sizes), out_shape=(pltpu.VMEM((C...  28.4 us
    pallas_call x1, Pallas kernels, step(): pl.pallas_call(write_out, out_shape=(jax.ShapeDtypeStruct((CX, CY, CZ), f...  0.82 us

profile of v6, /device:TPU:1, one launch (start us, length us, event | category | flops | bytes accessed | tf_op | source)
XLA Modules:
  0.0 29.8 jit_solution(6271422785983309414)
XLA Ops:
  0.6 28.4 %shard_map.76 = (f32[8,32,128]{2,1,0:T(8,128)S(1)}, f32[3,8,32,128]{3,2,1,0:T(8,128)S(1)}, f32[1,2]{1,0:T(1,128)S(1)}) custom-call(f32[8,32,128]{2,1,0:T(8,128)} %chi_in.1, f32[6,8,32,128]{3,2,1,0:T(8,128)} %met_in.1, f32[6,8,32,128]{3,2,1,0:T(8,128)} %cur_in.1, f32[8,32,128]{2,1,0:T(8,128)} %trk_in.1, f32[3,8,32,128]{3,2,1,0:T(8,128)} %gam_in.1), custom_call_target="tpu_custom_call" | custom-call | tf_op jit(solution)/shard_map/pallas_call | solution.py:759
  29.0 0.8 %shard_map.77 = (f32[8,32,128]{2,1,0:T(8,128)}, f32[3,8,32,128]{3,2,1,0:T(8,128)}, f32[1,2]{1,0:T(1,128)}) custom-call(f32[8,32,128]{2,1,0:T(8,128)S(1)} %get-tuple-element.9.ham, f32[3,8,32,128]{3,2,1,0:T(8,128)S(1)} %get-tuple-element.10.mom, f32[1,2]{1,0:T(1,128)S(1)} %get-tuple-element.11.norm), custom_call_target="tpu_custom_call" | custom-call | tf_op jit(solution)/shard_map/pallas_call | solution.py:793

commit v7 on v6

--- a/solution.py
+++ b/solution.py
@@ -21,6 +21,10 @@
 
 S_GEO_Y, S_GEO_Z, S_REST_Y, S_REST_Z, S_EDGE_XY, S_EDGE_YZ, S_EDGE_XZ, S_TERM = range(8)
 S_SUM_A, S_SUM_B, S_DIRECT, S_GEO_X = 8, 9, 10, 11
+SENT = {
+    S_GEO_X: 0, S_REST_Y: 0, S_REST_Z: 0, S_EDGE_XY: 0, S_TERM: 0,
+    S_GEO_Y: 1, S_GEO_Z: 1, S_EDGE_YZ: 1, S_EDGE_XZ: 1, S_SUM_A: 2, S_SUM_B: 3, S_DIRECT: 4,
+}
 LEAD = (0, 0, 1)
 
 
@@ -69,17 +73,12 @@
 
     def remote(src, dst, place, device, part=0):
         return pltpu.make_async_remote_copy(
-            src_ref=src, dst_ref=dst, send_sem=send_sem.at[place], recv_sem=recv_sem.at[place + part],
+            src_ref=src, dst_ref=dst, send_sem=send_sem.at[SENT[place]], recv_sem=recv_sem.at[place + part],
             device_id=device, device_id_type=MESH,
         )
 
     def group(whole, place, part=0):
         return remote(whole, whole, place, at(1, 0, 0), part)
-
-    barrier = pltpu.get_barrier_semaphore()
-    faces = [(-1, 0, 0), (1, 0, 0), (0, -1, 0), (0, 1, 0), (0, 0, -1), (0, 0, 1)]
-    for step in faces:
-        pl.semaphore_signal(barrier, inc=1, device_id=at(*step), device_id_type=MESH)
 
     def block(src, dst, lo, hi):
         if len(src.shape) == 3:
@@ -94,6 +93,11 @@
     loads = [pltpu.make_async_copy(s, d, load_sem.at[(i > 3) + (i > 5)]) for i, (s, d) in enumerate(loads)]
     for copy in loads:
         copy.start()
+
+    barrier = pltpu.get_barrier_semaphore()
+    faces = [(-1, 0, 0), (1, 0, 0), (0, -1, 0), (0, 1, 0), (0, 0, -1), (0, 0, 1)]
+    for step in faces:
+        pl.semaphore_signal(barrier, inc=1, device_id=at(*step), device_id_type=MESH)
 
     lane = lane_ids()
     lane4, place = lane // 4, lax.rem(lane, 4)
@@ -196,7 +200,6 @@
         pieces = jnp.concatenate([high, middle, low], axis=1)
         return jnp.dot(pieces, TAPS[:, 0:width], preferred_element_type=jnp.float32)
 
-    all_geo_x = group(F.at[:, 2 : 2 + CX // 2, OWN : OWN + CY], S_GEO_X)
     all_geo_y, all_rest_y = group(YRG, S_GEO_Y), group(YRR, S_REST_Y)
     all_geo_z, all_rest_z = group(ZPR.at[:, 0:GEO], S_GEO_Z), group(ZPR.at[:, GEO : GEO + 8], S_REST_Z)
     all_xy, all_yz, all_xz = group(XYR, S_EDGE_XY), group(YZR, S_EDGE_YZ), group(XER, S_EDGE_XZ)
@@ -268,7 +271,7 @@
     for n in range(8):
         z_rest(n)
     pl.semaphore_wait(two_sem, len(faces))
-    for copy in edge_yz + edge_xz + [geo_xs[0][BLOCKS - 1], geo_xs[1][BLOCKS - 1]] + edge_xy:
+    for copy in edge_yz + [geo_xs[0][BLOCKS - 1], geo_xs[1][BLOCKS - 1]] + edge_xz + edge_xy:
         copy.start()
     for step in [(-2, 0, 0), (2, 0, 0), (0, 0, -2), (0, 0, 2)]:
         pl.semaphore_signal(near_sem, inc=1, device_id=at(*step), device_id_type=MESH)
@@ -588,12 +591,14 @@
     all_rest_y.wait_recv()
     lax.fori_loop(0, CX, open_y_rest, 0)
     send_terms(1)
-    inner(4, 8)
+    inner(4, 6)
     send_terms(2)
+    inner(6, 8)
     pl.semaphore_wait(far_sem, n_gy)
     for k in range(1, n_gx):
         pl.semaphore_signal(last_sem, inc=1, device_id=at(k, 0, 0), device_id_type=MESH)
 
+    send_terms(3)
     all_xz.wait_recv()
     def x_changes(half):
         for sx in range(2):
@@ -635,7 +640,6 @@
     for c in range(GEO):
         x_ends(c, 0)
     x_edge_rows(1, 2, 3)
-    send_terms(3)
     outer(1)
     x_changes(1)
     for c in range(GEO):
@@ -731,8 +735,9 @@
 
         norms(lax.fori_loop(1, n_line, lambda j, total: total + rows_of(j), rows_of(0)))
 
-    for sent in (all_geo_x, all_geo_y, all_geo_z, all_rest_y, all_rest_z, all_xy, all_yz, all_xz, all_terms, others):
-        sent.wait_send()
+    group(PT.at[0:15, 0:4], S_GEO_X).wait_send()
+    group(PT.at[0:7, 0:2], S_GEO_Y).wait_send()
+    others.wait_send()
     pl.when(jnp.logical_not(leading))(direct.wait_send)
     fewer = jnp.logical_not(leading) & (iy == LEAD[1]) & (iz // 2 == LEAD[2] // 2)
     pl.when(fewer)(group(SUM_B.at[0 : n_line - 2], S_SUM_B).wait_send)
@@ -781,7 +786,7 @@
                 vm(2, 4, 2, CY, CZ), vm(2, 4, 2, CY, CZ), vm(18, CX, CY, CZ),
                 vm(2, 1, CZ), vm(sizes[1] * sizes[2] // 2, 1, CZ), vm(2 * sizes[0], 1, CZ), vm(sizes[0] * sizes[1] * sizes[2], 1, CZ),
                 pltpu.SemaphoreType.DMA((3,)),
-                pltpu.SemaphoreType.DMA((S_GEO_X + 1,)),
+                pltpu.SemaphoreType.DMA((5,)),
                 pltpu.SemaphoreType.DMA((S_GEO_X + BLOCKS,)),
                 pltpu.SemaphoreType.REGULAR,
                 pltpu.SemaphoreType.REGULAR,

time: 30.1 us -> 29.8 us (0.990)
  no operation moved by 1% of the time
where the time goes in v7:
time: 29.8 us; the launch traced here: 29.6 us
  Pallas kernels  29 us (97%)
  between operations  0.64 us (2%)
    pallas_call x1, Pallas kernels, step(): pl.pallas_call(functools.partial(kernel, sizes), out_shape=(pltpu.VMEM((C...  28.2 us
    pallas_call x1, Pallas kernels, step(): pl.pallas_call(write_out, out_shape=(jax.ShapeDtypeStruct((CX, CY, CZ), f...  0.82 us

profile of v7, /device:TPU:1, one launch (start us, length us, event | category | flops | bytes accessed | tf_op | source)
XLA Modules:
  0.0 29.6 jit_solution(3672546453138955026)
XLA Ops:
  0.6 28.2 %shard_map.76 = (f32[8,32,128]{2,1,0:T(8,128)S(1)}, f32[3,8,32,128]{3,2,1,0:T(8,128)S(1)}, f32[1,2]{1,0:T(1,128)S(1)}) custom-call(f32[8,32,128]{2,1,0:T(8,128)} %chi_in.1, f32[6,8,32,128]{3,2,1,0:T(8,128)} %met_in.1, f32[6,8,32,128]{3,2,1,0:T(8,128)} %cur_in.1, f32[8,32,128]{2,1,0:T(8,128)} %trk_in.1, f32[3,8,32,128]{3,2,1,0:T(8,128)} %gam_in.1), custom_call_target="tpu_custom_call" | custom-call | tf_op jit(solution)/shard_map/pallas_call | solution.py:764
  28.8 0.8 %shard_map.77 = (f32[8,32,128]{2,1,0:T(8,128)}, f32[3,8,32,128]{3,2,1,0:T(8,128)}, f32[1,2]{1,0:T(1,128)}) custom-call(f32[8,32,128]{2,1,0:T(8,128)S(1)} %get-tuple-element.9.ham, f32[3,8,32,128]{3,2,1,0:T(8,128)S(1)} %get-tuple-element.10.mom, f32[1,2]{1,0:T(1,128)S(1)} %get-tuple-element.11.norm), custom_call_target="tpu_custom_call" | custom-call | tf_op jit(solution)/shard_map/pallas_call | solution.py:798

commit v8 on v7

--- a/solution.py
+++ b/solution.py
@@ -733,7 +733,11 @@
                 rows = rows + ALL[n_plane * j + k]
             return rows
 
-        norms(lax.fori_loop(1, n_line, lambda j, total: total + rows_of(j), rows_of(0)))
+        parts = [rows_of(j) for j in range(n_line)]
+        total = parts[0]
+        for part in parts[1:]:
+            total = total + part
+        norms(total)
 
     group(PT.at[0:15, 0:4], S_GEO_X).wait_send()
     group(PT.at[0:7, 0:2], S_GEO_Y).wait_send()

time: 29.8 us -> 29.8 us (level)
  no operation moved by 1% of the time
where the time goes in v8:
time: 29.8 us; the launch traced here: 29.4 us
  Pallas kernels  28.8 us (97%)
  between operations  0.64 us (2%)
    pallas_call x1, Pallas kernels, step(): pl.pallas_call(functools.partial(kernel, sizes), out_shape=(pltpu.VMEM((C...  28 us
    pallas_call x1, Pallas kernels, step(): pl.pallas_call(write_out, out_shape=(jax.ShapeDtypeStruct((CX, CY, CZ), f...  0.82 us

profile of v8, /device:TPU:1, one launch (start us, length us, event | category | flops | bytes accessed | tf_op | source)
XLA Modules:
  0.0 29.4 jit_solution(17221129328384155743)
XLA Ops:
  0.6 28.0 %shard_map.76 = (f32[8,32,128]{2,1,0:T(8,128)S(1)}, f32[3,8,32,128]{3,2,1,0:T(8,128)S(1)}, f32[1,2]{1,0:T(1,128)S(1)}) custom-call(f32[8,32,128]{2,1,0:T(8,128)} %chi_in.1, f32[6,8,32,128]{3,2,1,0:T(8,128)} %met_in.1, f32[6,8,32,128]{3,2,1,0:T(8,128)} %cur_in.1, f32[8,32,128]{2,1,0:T(8,128)} %trk_in.1, f32[3,8,32,128]{3,2,1,0:T(8,128)} %gam_in.1), custom_call_target="tpu_custom_call" | custom-call | tf_op jit(solution)/shard_map/pallas_call | solution.py:768
  28.6 0.8 %shard_map.77 = (f32[8,32,128]{2,1,0:T(8,128)}, f32[3,8,32,128]{3,2,1,0:T(8,128)}, f32[1,2]{1,0:T(1,128)}) custom-call(f32[8,32,128]{2,1,0:T(8,128)S(1)} %get-tuple-element.9.ham, f32[3,8,32,128]{3,2,1,0:T(8,128)S(1)} %get-tuple-element.10.mom, f32[1,2]{1,0:T(1,128)S(1)} %get-tuple-element.11.norm), custom_call_target="tpu_custom_call" | custom-call | tf_op jit(solution)/shard_map/pallas_call | solution.py:802
